TPU v7x, 256 devices: a whole 4x4x8 slice. The times are simulated.
256 devices in a mesh: gx: 16 (over z, core), gy: 4 (over x), gz: 4 (over y).
Axes of the slice: x: 4, y: 4, z: 8, core: 2. Of those that a mesh axis runs over, the one named last changes fastest.
Arguments:
- quant_codes: int32 [512, 128, 512], P('gx', 'gy', 'gz'), may hold values from -1073741824 to 1073741824, as said below
- error_step: float32 [1], replicated, may hold values from 4e-09 to 1.5e-08
Outputs:
- decoded: float32 [512, 128, 512], P('gx', 'gy', 'gz')
Inputs may be any that keep to these rules, and one draw needn't show every extreme that they name: quant_codes are the third differences (along the three dimensions, with zeros before the grid's first cells) of a field of integers between -134217728 and 134217728.
All inputs are finite; a program needn't handle non-finite values.
Results may differ from a plain program's by a relative error of at most 0.00002.
Values sent between devices are 32-bit elements; how exact they have to be, the bound alone decides.
No kernel may reach another device: no remote copies, remote signals or barrier semaphores. Data moves between devices by JAX's collectives and lax.ppermute only.
A program may use at most 64 MiB of HBM per device.

v0:
```python
import jax
import jax.numpy as jnp
from jax import lax
from jax.sharding import PartitionSpec as P


def prefix_2(value, axis, combine, identity):
    size, position = (lax.axis_size(axis), lax.axis_index(axis))
    everything = lax.all_gather(value, axis)
    start = jnp.broadcast_to(jnp.asarray(identity, value.dtype), value.shape)

    def turn(k, before):
        reached = k < position
        new = combine(before, everything[k])
        return jnp.where(reached, new, before)

    return lax.fori_loop(0, size, turn, start)


def from_everyone(value, axis):
    copies = jnp.broadcast_to(value, (lax.axis_size(axis), *value.shape))
    return lax.all_to_all(copies, axis, split_axis=0, concat_axis=0, tiled=True)


def collected_together(value, axis):
    leaves = jax.tree.leaves(value)
    order = sorted(range(len(leaves)), key=lambda k: -leaves[k].size)
    width = (1, *leaves[order[0]].shape)[-1]
    lines = [
        jnp.pad(leaves[k].reshape(-1), (0, -leaves[k].size % width)).reshape(-1, width)
        for k in order
    ]
    both, at, found = (from_everyone(jnp.concatenate(lines), axis), 0, {})
    for k, line in zip(order, lines):
        share = both[:, at : at + len(line)].reshape(len(both), -1)
        found[k] = share[:, : leaves[k].size].reshape(-1, *leaves[k].shape)
        at += len(line)
    numbers = iter(range(len(leaves)))
    return jax.tree.map(lambda _: found[next(numbers)], value)


def once_a_type(value, axis):
    leaves, found = (jax.tree.leaves(value), {})
    for first, a in enumerate(leaves):
        if first not in found:
            alike = [k for k, b in enumerate(leaves) if b.dtype == a.dtype]
            got = (
                collected_together([leaves[k] for k in alike], axis)
                if len(alike) > 1
                else [from_everyone(a, axis)]
            )
            for k, b in zip(alike, got):
                found[k] = b
    numbers = iter(range(len(leaves)))
    return jax.tree.map(lambda _: found[next(numbers)], value)


def folded_in_pairs(pieces, combine):
    while len(jax.tree.leaves(pieces)[0]) > 1:
        pieces = jax.vmap(combine)(
            *(jax.tree.map(lambda part: part[side::2], pieces) for side in (0, 1))
        )
    return jax.tree.map(lambda part: part[0], pieces)


def prefix_3(value, axis, combine, identity):
    size, position = (lax.axis_size(axis), lax.axis_index(axis))
    passed = jnp.arange(size) < position

    def kept(part, zero, own):
        part = jnp.where(
            passed.reshape(-1, *(1 for _ in own.shape)), part, jnp.asarray(zero, own.dtype)
        )
        return part

    pieces = once_a_type(value, axis)
    return folded_in_pairs(jax.tree.map(kept, pieces, identity, value), combine)


def passed_along(block, axis, distance):
    devices = range(lax.axis_size(axis))
    route = [(i - distance, i) for i in devices if i - distance in devices]
    return lax.ppermute(block, axis, route)


def add_terms(earlier, later):
    return jax.tree.map(jnp.add, earlier, later)


def cumulate(values, axis_dim):
    length = values.shape[axis_dim]
    position = lax.broadcasted_iota(jnp.int32, values.shape, axis_dim)
    offset = 1
    while offset < length:
        rolled = jnp.roll(values, offset, axis_dim)
        values = values + jnp.where(position >= offset, rolled, jnp.zeros_like(rolled))
        offset = offset * 2
    return values


def beside(values, low_plane, high_plane, axis_dim):
    length = values.shape[axis_dim]
    position = lax.broadcasted_iota(jnp.int32, values.shape, axis_dim)
    below = jnp.where(
        position == 0, jnp.expand_dims(low_plane, axis_dim), jnp.roll(values, 1, axis_dim)
    )
    above = jnp.where(
        position == length - 1,
        jnp.expand_dims(high_plane, axis_dim),
        jnp.roll(values, -1, axis_dim),
    )
    return below + above


def on_device(quant_codes, error_step):
    step_size = error_step[0]
    sectioned = cumulate(quant_codes, 0)
    x_face = sectioned[-1]
    carry_x = prefix_2(x_face, "gx", add_terms, jnp.zeros_like(x_face))
    sectioned = cumulate(sectioned + carry_x[None], 1)
    y_face = sectioned[:, -1, :]
    plane_x = cumulate(carry_x, 0)
    edge_in = plane_x[-1]
    carry_y, edge_x = prefix_3(
        (y_face, edge_in), "gy", add_terms, (jnp.zeros_like(y_face), jnp.zeros_like(edge_in))
    )
    plane_x = plane_x + edge_x[None]
    sectioned = cumulate(sectioned + carry_y[:, None, :], 2)
    z_face = sectioned[:, :, -1]
    plane_x = cumulate(plane_x, 1)
    plane_y = cumulate(carry_y, 1)
    row_in_x = plane_x[:, -1]
    row_in_y = plane_y[:, -1]
    carry_z, row_x, row_y = prefix_3(
        (z_face, row_in_x, row_in_y),
        "gz",
        add_terms,
        (jnp.zeros_like(z_face), jnp.zeros_like(row_in_x), jnp.zeros_like(row_in_y)),
    )
    plane_x = plane_x + row_x[:, None]
    plane_y = plane_y + row_y[:, None]
    prefix = sectioned + carry_z[:, :, None]
    recon = prefix.astype(jnp.float32) * step_size
    below_x = plane_x.astype(jnp.float32) * step_size
    below_y = plane_y.astype(jnp.float32) * step_size
    below_z = carry_z.astype(jnp.float32) * step_size
    above_x = passed_along(recon[0], "gx", -1)
    above_y = passed_along(recon[:, 0, :], "gy", -1)
    above_z = passed_along(recon[:, :, 0], "gz", -1)
    neighbours = beside(recon, below_x, above_x, 0)
    neighbours = neighbours + beside(recon, below_y, above_y, 1)
    neighbours = neighbours + beside(recon, below_z, above_z, 2)
    return recon + 0.5 * (neighbours / 6.0 - recon)


def solution(mesh):
    in_specs = (P("gx", "gy", "gz"), P())
    out_specs = P("gx", "gy", "gz")
    return jax.shard_map(
        on_device, mesh=mesh, in_specs=in_specs, out_specs=out_specs, check_vma=False
    )
```

profile of v0, /device:TPU:8, one launch (start us, length us, event | category | flops | bytes accessed | tf_op | source)
XLA Modules:
  0.0 72.9 jit_solution(9118280489910276714)
XLA Ops:
  0.0 1.0 %slice-done.1 = s32[31,32,128]{2,1,0:T(8,128)S(1)} async-done(((s32[32,32,128]{2,1,0:T(8,128)}), s32[31,32,128]{2,1,0:T(8,128)S(1)}, s32[]{:S(2)}) %slice-start.1) | async-done | bytes 507928 | tf_op jit(solution)/shard_map/jit(_roll_static)/slice | solution.py:95
  1.0 0.3 copy.41
  1.4 0.4 slice-done.2
  1.8 0.4 fusion
  3.0 20.7 %all_gather.3 = s32[16,32,128]{2,1,0:T(8,128)S(1)} all-gather(s32[1,32,128]{2,1,0:T(8,128)S(1)} %bitcast.88), channel_id=1, replica_groups=mesh['gx'=16,'gy'=4,'gz'=4] {'gx'}, dimensions={0}, use_global_device_ids=true | all-gather | bytes 278528 | tf_op jit(solution)/shard_map/all_gather | solution.py:9
  23.7 0.6 while.14
  24.5 0.6 copy-done.2
  25.8 0.7 %copy-done = s32[32,32,128]{2,0,1:T(8,128)} copy-done((s32[32,32,128]{2,0,1:T(8,128)}, s32[32,32,128]{2,0,1:T(8,128)S(1)}, u32[]{:S(2)}) %copy-start) | copy-done | bytes 524312
  26.5 0.7 copy-done.3
  27.5 0.7 %slice-done = s32[32,8,128]{2,0,1:T(8,128)S(1)} async-done(((s32[32,32,128]{2,0,1:T(8,128)}), s32[32,8,128]{2,0,1:T(8,128)S(1)}, s32[]{:S(2)}) %slice-start) | async-done | bytes 131096 | tf_op jit(solution)/shard_map/jit(_roll_static)/slice | solution.py:95
  28.2 1.2 %fusion.8 = s32[32,32,128]{2,0,1:T(8,128)S(1)} fusion(s32[32,32,128]{2,0,1:T(8,128)} %copy-done, s32[32,24,128]{2,0,1:T(8,128)S(1)} %slice.560, s32[32,8,128]{2,0,1:T(8,128)S(1)} %slice-done, pred[32]{0:T(512)(128)(4,1)S(1)} %iota_compare_fusion.14), kind=kLoop, calls=%fused_computation.18 | loop fusion | flops 393216 | bytes 1572896 | tf_op jit(solution)/shard_map/add | solution.py:96
  29.6 0.6 broadcast_in_dim.107
  30.2 4.3 %all-to-all-start = ((s32[4,33,128]{2,1,0:T(8,128)}), s32[4,33,128]{2,1,0:T(8,128)S(1)}, u32[]{:S(2)}, u32[]{:S(2)}) async-start(s32[4,33,128]{2,1,0:T(8,128)} %broadcast_in_dim.107), calls=%async_computation | async-start | bytes 163840 | tf_op jit(solution)/shard_map/all_to_all | solution.py:22
  34.6 5.6 %all-to-all-done = s32[4,33,128]{2,1,0:T(8,128)S(1)} async-done(((s32[4,33,128]{2,1,0:T(8,128)}), s32[4,33,128]{2,1,0:T(8,128)S(1)}, u32[]{:S(2)}, u32[]{:S(2)}) %all-to-all-start) | async-done | bytes 67616 | tf_op jit(solution)/shard_map/all_to_all | solution.py:22
  40.6 0.2 slice.576
  40.8 0.2 fusion.10
  41.0 0.2 slice.578
  41.2 0.2 fusion.11
  41.4 0.2 slice.580
  41.6 0.2 fusion.12
  41.8 0.2 slice.582
  42.0 0.2 fusion.13
  42.2 0.2 slice.584
  42.4 0.2 fusion.14
  42.6 0.2 slice.586
  42.8 0.2 fusion.15
  43.1 0.2 fusion.53
  43.3 0.2 fusion.16
  43.5 0.2 slice.590
  43.7 0.4 copy.35
  46.1 0.7 %reshape.268 = s32[4,1,1088]{2,1,0:T(1,128)} reshape(s32[4,32,34]{2,1,0:T(8,128)S(1)} %broadcast_bitcast_fusion) | data formatting | bytes 34816
  46.8 4.9 %all-to-all-start.1 = ((s32[4,1,1088]{2,1,0:T(1,128)}), s32[4,1,1088]{2,1,0:T(1,128)S(1)}, u32[]{:S(2)}, u32[]{:S(2)}) async-start(s32[4,1,1088]{2,1,0:T(1,128)} %reshape.268), calls=%async_computation.1 | async-start | bytes 36864 | tf_op jit(solution)/shard_map/all_to_all | solution.py:22
  52.4 3.3 %all-to-all-done.1 = s32[4,1,1088]{2,1,0:T(1,128)S(1)} async-done(((s32[4,1,1088]{2,1,0:T(1,128)}), s32[4,1,1088]{2,1,0:T(1,128)S(1)}, u32[]{:S(2)}, u32[]{:S(2)}) %all-to-all-start.1) | async-done | bytes 17440 | tf_op jit(solution)/shard_map/all_to_all | solution.py:22
  55.7 0.5 broadcast.307
  56.2 0.7 reduce.8
  57.0 0.3 slice_reduce_fusion.1
  57.6 0.2 convert_multiply_fusion
  57.8 0.2 fusion.49
  58.0 0.2 fusion.48
  58.2 0.9 %fusion.51 = (f32[31,32,128]{2,0,1:T(8,128)S(1)}, f32[31,32,128]{2,0,1:T(8,128)}) fusion(f32[32,32,128]{2,0,1:T(8,128)S(1)} %convert_multiply_fusion), kind=kLoop, calls=%fused_computation.138 | loop fusion | bytes 2031616 | tf_op jit(solution)/shard_map/jit(_roll_static)/slice | solution.py:110
  59.1 1.1 %fusion.50 = (f32[32,31,128]{2,0,1:T(8,128)}, f32[32,31,128]{2,0,1:T(8,128)}) fusion(f32[32,32,128]{2,0,1:T(8,128)S(1)} %convert_multiply_fusion), kind=kLoop, calls=%fused_computation.137 | loop fusion | bytes 2031616 | tf_op jit(solution)/shard_map/jit(_roll_static)/slice | solution.py:110
  60.3 0.4 copy.37
  60.6 3.4 %collective-permute-start.2 = (f32[32,32]{1,0:T(8,128)S(1)}, f32[32,32]{1,0:T(8,128)S(1)}, u32[]{:S(2)}, u32[]{:S(2)}) collective-permute-start(f32[32,32]{1,0:T(8,128)S(1)} %bitcast.89), channel_id=1, source_target_pairs={{1,0},{2,1},{3,2},{5,4},{6,5},{7,6},{9,8},{10,9},{11,10},{13,12},{... | collective-permute-start | bytes 12296 | tf_op jit(solution)/shard_map/ppermute | solution.py:83
  64.0 1.3 %collective-permute-start.1 = (f32[32,128]{1,0:T(8,128)S(1)}, f32[32,128]{1,0:T(8,128)S(1)}, u32[]{:S(2)}, u32[]{:S(2)}) collective-permute-start(f32[32,128]{1,0:T(8,128)S(1)} %get-tuple-element.120), channel_id=1, source_target_pairs={{4,0},{8,4},{12,8},{5,1},{9,5},{13,9},{6,2},{10,6},{14,10},{7,3},{... | collective-permute-start | bytes 49160 | tf_op jit(solution)/shard_map/ppermute | solution.py:83
  65.3 1.3 %collective-permute-start = (f32[32,128]{1,0:T(8,128)S(1)}, f32[32,128]{1,0:T(8,128)S(1)}, u32[]{:S(2)}, u32[]{:S(2)}) collective-permute-start(f32[32,128]{1,0:T(8,128)S(1)} %bitcast.86), channel_id=1, source_target_pairs={{16,0},{32,16},{48,32},{64,48},{80,64},{96,80},{112,96},{128,112},... | collective-permute-start | bytes 49160 | tf_op jit(solution)/shard_map/ppermute | solution.py:83
  66.8 2.9 %collective-permute-done.1 = f32[32,128]{1,0:T(8,128)S(1)} collective-permute-done((f32[32,128]{1,0:T(8,128)S(1)}, f32[32,128]{1,0:T(8,128)S(1)}, u32[]{:S(2)}, u32[]{:S(2)}) %collective-permute-start.1) | collective-permute-done | bytes 16416 | tf_op jit(solution)/shard_map/ppermute | solution.py:83
  69.6 2.2 %fusion.23 = f32[32,32,128]{2,0,1:T(8,128)S(1)} fusion(f32[31,32,128]{2,0,1:T(8,128)} %get-tuple-element.130, f32[1,32,128]{2,0,1:T(1,128)S(1)} %get-tuple-element.132, f32[1,32,128]{2,0,1:T(1,128)S(1)} %get-tuple-element.131, f32[31,32,128]{2,0,1:T(8,128)S(1)} %get-tuple-element.129, f32[32,31,128]{2,0,1:T(8,128)} %get-tuple-element.128, ...), kind=kLoop, calls=%fused_computation.42 | loop fusion | flops 3145728 | bytes 4272452 | tf_op jit(solution)/shard_map/add | solution.py:153
  71.8 1.1 %copy.39 = f32[32,32,128]{2,1,0:T(8,128)} copy(f32[32,32,128]{2,0,1:T(8,128)S(1)} %fusion.23) | data formatting | bytes 1048576 | tf_op jit(solution)/shard_map/add | solution.py:153
  (136 shorter events, 5.1 us)
Async XLA Ops:
  0.0 1.0 %slice-start.1 = ((s32[32,32,128]{2,1,0:T(8,128)}), s32[31,32,128]{2,1,0:T(8,128)S(1)}, s32[]{:S(2)}) async-start(s32[32,32,128]{2,1,0:T(8,128)} %param.4), calls=%async_computation.3 | async-start | bytes 1015808 | tf_op jit(solution)/shard_map/jit(_roll_static)/slice | solution.py:95
  0.0 1.3 %copy-start.1 = (s32[32,32,128]{2,1,0:T(8,128)S(1)}, s32[32,32,128]{2,1,0:T(8,128)}, u32[]{:S(2)}) copy-start(s32[32,32,128]{2,1,0:T(8,128)} %param.4) | copy-start | bytes 1572868
  1.0 0.8 %slice-start.2 = ((s32[32,32,128]{2,1,0:T(8,128)}), s32[1,32,128]{2,1,0:T(8,128)S(1)}, s32[]{:S(2)}) async-start(s32[32,32,128]{2,1,0:T(8,128)} %param.4), calls=%async_computation.4 | async-start | bytes 32768 | tf_op jit(solution)/shard_map/jit(_roll_static)/slice | solution.py:95
  24.5 0.6 copy-start.2
  25.7 0.8 %copy-start = (s32[32,32,128]{2,0,1:T(8,128)}, s32[32,32,128]{2,0,1:T(8,128)S(1)}, u32[]{:S(2)}) copy-start(s32[32,32,128]{2,0,1:T(8,128)S(1)} %fusion.7) | copy-start | bytes 1572868
  26.5 0.7 copy-start.3
  26.5 0.8 %slice-start.3 = ((s32[32,128]{1,0:T(8,128)}), s32[24,128]{1,0:T(8,128)S(1)}, s32[]{:S(2)}) async-start(s32[32,128]{1,0:T(8,128)} %copy-done.2), calls=%async_computation.5 | async-start | bytes 24576 | tf_op jit(solution)/shard_map/jit(_roll_static)/slice | solution.py:95
  26.5 0.8 %slice-start.4 = ((s32[32,128]{1,0:T(8,128)}), s32[8,128]{1,0:T(8,128)S(1)}, s32[]{:S(2)}) async-start(s32[32,128]{1,0:T(8,128)} %copy-done.2), calls=%async_computation.6 | async-start | bytes 8192 | tf_op jit(solution)/shard_map/jit(_roll_static)/slice | solution.py:95
  27.3 0.9 %slice-start = ((s32[32,32,128]{2,0,1:T(8,128)}), s32[32,8,128]{2,0,1:T(8,128)S(1)}, s32[]{:S(2)}) async-start(s32[32,32,128]{2,0,1:T(8,128)} %copy-done), calls=%async_computation.2 | async-start | bytes 262144 | tf_op jit(solution)/shard_map/jit(_roll_static)/slice | solution.py:95
  30.2 10.0 %all-to-all-start = ((s32[4,33,128]{2,1,0:T(8,128)}), s32[4,33,128]{2,1,0:T(8,128)S(1)}, u32[]{:S(2)}, u32[]{:S(2)}) async-start(s32[4,33,128]{2,1,0:T(8,128)} %broadcast_in_dim.107), calls=%async_computation | async-start | bytes 163840 | tf_op jit(solution)/shard_map/all_to_all | solution.py:22
  46.8 8.8 %all-to-all-start.1 = ((s32[4,1,1088]{2,1,0:T(1,128)}), s32[4,1,1088]{2,1,0:T(1,128)S(1)}, u32[]{:S(2)}, u32[]{:S(2)}) async-start(s32[4,1,1088]{2,1,0:T(1,128)} %reshape.268), calls=%async_computation.1 | async-start | bytes 36864 | tf_op jit(solution)/shard_map/all_to_all | solution.py:22
  60.6 6.0 %collective-permute-start.2 = (f32[32,32]{1,0:T(8,128)S(1)}, f32[32,32]{1,0:T(8,128)S(1)}, u32[]{:S(2)}, u32[]{:S(2)}) collective-permute-start(f32[32,32]{1,0:T(8,128)S(1)} %bitcast.89), channel_id=1, source_target_pairs={{1,0},{2,1},{3,2},{5,4},{6,5},{7,6},{9,8},{10,9},{11,10},{13,12},{... | collective-permute-start | bytes 12296 | tf_op jit(solution)/shard_map/ppermute | solution.py:83
  64.0 5.6 %collective-permute-start.1 = (f32[32,128]{1,0:T(8,128)S(1)}, f32[32,128]{1,0:T(8,128)S(1)}, u32[]{:S(2)}, u32[]{:S(2)}) collective-permute-start(f32[32,128]{1,0:T(8,128)S(1)} %get-tuple-element.120), channel_id=1, source_target_pairs={{4,0},{8,4},{12,8},{5,1},{9,5},{13,9},{6,2},{10,6},{14,10},{7,3},{... | collective-permute-start | bytes 49160 | tf_op jit(solution)/shard_map/ppermute | solution.py:83
  65.3 4.3 %collective-permute-start = (f32[32,128]{1,0:T(8,128)S(1)}, f32[32,128]{1,0:T(8,128)S(1)}, u32[]{:S(2)}, u32[]{:S(2)}) collective-permute-start(f32[32,128]{1,0:T(8,128)S(1)} %bitcast.86), channel_id=1, source_target_pairs={{16,0},{32,16},{48,32},{64,48},{80,64},{96,80},{112,96},{128,112},... | collective-permute-start | bytes 49160 | tf_op jit(solution)/shard_map/ppermute | solution.py:83
where the time goes:
time: 73.7 us; the launch traced here: 72.9 us
  blocking collectives  20.7 us (28%)
  starting transfers between devices  15.1 us (20%)
  local copies, waits for them, and re-layouts  14.9 us (20%)
  waiting for transfers between devices  11.7 us (16%)
  other arithmetic  8.86 us (12%)
  between operations  1.23 us (2%)
    all_gather x1, blocking collectives, prefix_2(): everything = lax.all_gather(value, axis)  20.7 us
    all_to_all x2, starting transfers between devices, from_everyone(): return lax.all_to_all(copies, axis, split_axis=0, concat_axis=0, tiled=True)  9.2 us
    all_to_all x2, waiting for transfers between devices, from_everyone(): return lax.all_to_all(copies, axis, split_axis=0, concat_axis=0, tiled=True)  8.86 us
    ppermute x3, starting transfers between devices, passed_along(): return lax.ppermute(block, axis, route)  5.94 us
    slice x48, local copies, waits for them, and re-layouts, cumulate(): rolled = jnp.roll(values, offset, axis_dim)  5.04 us
    add x29, other arithmetic, cumulate(): values + jnp.where(position >= offset, rolled, jnp.zeros_like(rolled))  4.99 us
    unnamed x12, local copies, waits for them, and re-layouts  3.22 us
    ppermute x3, waiting for transfers between devices, passed_along(): return lax.ppermute(block, axis, route)  2.88 us
  transfers between devices with their start and end apart: 5, of which 3 were waited for; matrix products, arithmetic and copies ran while one was open for 0% of the time, Pallas kernels for 0%

commit v1 on v0

v1 whole, which is shorter than its diff:
```python
import functools

import jax
import jax.numpy as jnp
from jax import lax
from jax.experimental import pallas as pl
from jax.experimental.pallas import tpu as pltpu
from jax.sharding import PartitionSpec as P

I32 = jnp.int32
LIMIT = 16 * 1024 * 1024


def params():
    return pltpu.CompilerParams(vmem_limit_bytes=LIMIT)


def at_lane(tile, lane):
    return jnp.broadcast_to(tile[:, lane : lane + 1], tile.shape)


def scan_lanes(v, lane):
    s = 1
    while s < v.shape[1]:
        v = v + jnp.where(lane >= s, pltpu.roll(v, s, 1), 0)
        s *= 2
    return v


def scan_rows(v, row):
    for s in (1, 2, 4):
        v = v + jnp.where(row >= s, pltpu.roll(v, s, 0), 0)
    return v


def prefix_kernel(q, full, y_last, y_first, z_last, z_first, send, *, me, n):
    nx, ny, _ = q.shape
    tiles = ny // 8
    lane = lax.broadcasted_iota(I32, (8, 128), 1)
    row = lax.broadcasted_iota(I32, (8, 128), 0)
    zero = jnp.zeros((8, 128), I32)
    sums, zl, zf = [zero] * tiles, [zero] * tiles, [zero] * tiles
    for i in range(nx):
        carry = None
        for t in range(tiles):
            rows = slice(8 * t, 8 * t + 8)
            v = scan_rows(scan_lanes(q[i, rows, :], lane), row)
            if carry is not None:
                v = v + carry
            if t + 1 < tiles:
                carry = jnp.broadcast_to(v[7:8, :], v.shape)
            v = v + sums[t] if i else v
            if t + 1 < tiles:
                pass
            sums[t] = v
            full[i, rows, :] = v
            zl[t] = jnp.where(lane == i, at_lane(v, 127), zl[t])
            zf[t] = jnp.where(lane == i, at_lane(v, 0), zf[t])
        y_first[i : i + 1, :] = sums[0][0:1, :]
        y_last[i : i + 1, :] = sums[-1][7:8, :]
    for t in range(tiles):
        z_last[8 * t : 8 * t + 8, :] = zl[t]
        z_first[8 * t : 8 * t + 8, :] = zf[t]
    x = lax.axis_index(me)
    for d in range(n):
        for t in range(tiles):
            rows = slice(8 * t, 8 * t + 8)
            send[d, rows, :] = jnp.where(d == x - 1, full[0, rows, :], sums[t])


def faces_kernel(got, y_last, y_first, z_last, z_first, low, high, send, *, n, ny, nz):
    x, y, z = lax.axis_index("gx"), lax.axis_index("gy"), lax.axis_index("gz")
    lane = lax.broadcasted_iota(I32, (32, 128), 1)
    c = jnp.zeros((32, 128), I32)
    for s in range(n):
        c = c + jnp.where(s < x, got[s], 0)
    h = got[jnp.minimum(x + 1, n - 1)]
    low[...] = c
    high[...] = h
    yl, yf, zl, zf = y_last[...], y_first[...], z_last[...], z_first[...]
    yl_main = yl + c[31:32, :]
    yf_main = yf + c[0:1, :]
    below = c[31:32, :]
    above = yl[31:32, :] + c[31:32, :] + h[31:32, :]
    row = lax.broadcasted_iota(I32, (8, 128), 0)
    yl_tail = jnp.where(row == 0, below, jnp.where(row == 1, above, 0))
    zl_main = zl + at_lane(c, 127)
    zl_main = zl_main + jnp.where(lane == 33, at_lane(zl, 31) + at_lane(h, 127), 0)
    zf_main = zf + at_lane(c, 0)
    for a in range(ny):
        for b in range(nz):
            main = jnp.where(
                b == z,
                jnp.where(a > y, yl_main, yf_main),
                jnp.where(b > z, zl_main, zf_main),
            )
            send[a * nz + b, 0:32, :] = main
            send[a * nz + b, 32:40, :] = yl_tail


def stencil_kernel(step, got, full, low, high, out, *, n, ny, nz):
    x, y, z = lax.axis_index("gx"), lax.axis_index("gy"), lax.axis_index("gz")
    nx = full.shape[0]
    lane = lax.broadcasted_iota(I32, (32, 128), 1)
    row = lax.broadcasted_iota(I32, (32, 128), 0)
    ay = jnp.zeros((40, 128), I32)
    az = jnp.zeros((32, 128), I32)
    ayz = jnp.zeros((1, 128), I32)
    hyz = jnp.zeros((1, 128), I32)
    yp, zp = jnp.minimum(y + 1, ny - 1), jnp.minimum(z + 1, nz - 1)
    hz = got[y * nz + zp, 0:32, :]
    for a in range(ny - 1):
        ay = ay + jnp.where(a < y, got[a * nz + z], 0)
        hz = hz + jnp.where(a < y, got[a * nz + zp, 31:32, :], 0)
        for b in range(nz - 1):
            ayz = ayz + jnp.where((a < y) & (b < z), got[a * nz + b, 31:32, :], 0)
    for b in range(nz - 1):
        az = az + jnp.where(b < z, got[y * nz + b, 0:32, :], 0)
        hyz = hyz + jnp.where(b < z, got[yp * nz + b, 0:1, :], 0)
    az = az + ayz
    hy = got[yp * nz + z, 0:32, :]
    has_x = (x < n - 1).astype(jnp.float32)
    has_y = (y < ny - 1).astype(jnp.float32)
    has_z = (z < nz - 1).astype(jnp.float32)
    half = step[0] * 0.5
    twelfth = step[0] * (1.0 / 12.0)
    f32 = jnp.float32
    c = low[...]

    def plane(i):
        k = nx if i < 0 else nx + 1 if i == nx else i
        left = at_lane(az, k)
        here = c + left + ay[k : k + 1, :]
        if i >= 0:
            here = here + full[min(i, nx - 1)]
        if i == nx:
            here = here + high[...]
        return here, left

    before = plane(-1)[0].astype(f32)
    now, left = plane(0)
    now_f = now.astype(f32)
    for i in range(nx):
        after, after_left = plane(i + 1)
        after_f = after.astype(f32)
        if i == nx - 1:
            after_f = after_f * has_x
        total = before + after_f
        up = (ay[i : i + 1, :] + jnp.broadcast_to(ayz[:, i : i + 1], (1, 128))).astype(f32)
        down = now[31:32, :] + hy[i : i + 1, :] + jnp.broadcast_to(hyz[:, i : i + 1], (1, 128))
        down = down.astype(f32) * has_y
        total = total + jnp.where(row == 0, up, pltpu.roll(now_f, 1, 0))
        total = total + jnp.where(row == 31, down, pltpu.roll(now_f, 31, 0))
        right = (now + at_lane(hz, i)).astype(f32) * has_z
        total = total + jnp.where(lane == 0, left.astype(f32), pltpu.roll(now_f, 1, 1))
        total = total + jnp.where(lane == 127, right, pltpu.roll(now_f, 127, 1))
        out[i] = now_f * half + total * twelfth
        before, now, now_f, left = now_f, after, after_f, after_left


def on_device(quant_codes, error_step):
    n, ny, nz = (lax.axis_size(a) for a in ("gx", "gy", "gz"))
    face = jax.ShapeDtypeStruct((32, 128), I32)
    full, y_last, y_first, z_last, z_first, send = pl.pallas_call(
        functools.partial(prefix_kernel, me="gx", n=n),
        out_shape=(
            jax.ShapeDtypeStruct(quant_codes.shape, I32),
            face,
            face,
            face,
            face,
            jax.ShapeDtypeStruct((n, 32, 128), I32),
        ),
        compiler_params=params(),
        name="prefix",
    )(quant_codes)
    got = lax.all_to_all(send, "gx", split_axis=0, concat_axis=0, tiled=True)
    low, high, send = pl.pallas_call(
        functools.partial(faces_kernel, n=n, ny=ny, nz=nz),
        out_shape=(face, face, jax.ShapeDtypeStruct((ny * nz, 40, 128), I32)),
        compiler_params=params(),
        name="faces",
    )(got, y_last, y_first, z_last, z_first)
    got = lax.all_to_all(send, ("gy", "gz"), split_axis=0, concat_axis=0, tiled=True)
    vmem = pl.BlockSpec(memory_space=pltpu.VMEM)
    return pl.pallas_call(
        functools.partial(stencil_kernel, n=n, ny=ny, nz=nz),
        in_specs=[pl.BlockSpec(memory_space=pltpu.SMEM)] + [vmem] * 4,
        out_shape=jax.ShapeDtypeStruct(quant_codes.shape, jnp.float32),
        compiler_params=params(),
        name="stencil",
    )(error_step, got, full, low, high)


def solution(mesh):
    spec = P("gx", "gy", "gz")
    return jax.shard_map(
        on_device, mesh=mesh, in_specs=(spec, P()), out_specs=spec, check_vma=False
    )
```

time: 73.7 us -> 71.2 us (0.966)
  Pallas kernels: 0 us -> 33.2 us
  local copies, waits for them, and re-layouts: 14.9 us -> 1.04 us
  other arithmetic: 8.86 us -> 0 us
  starting transfers between devices: 15.1 us -> 7.39 us
  waiting for transfers between devices: 11.7 us -> 8.13 us
  blocking collectives: 20.7 us -> 19.5 us
    pallas_call x0 -> x3, Pallas kernels: none -> 33.2 us  [the longest x1 30.2 us: on_device(): pl.pallas_call(functools.partial(prefix_kernel, me='gx', n=n), out_shape=...]
    all_gather x1 -> x0, blocking collectives: 20.7 us -> none  [prefix_2(): everything = lax.all_gather(value, axis)]
    all_to_all x0 -> x1, blocking collectives: none -> 19.5 us  [on_device(): got = lax.all_to_all(send, 'gx', split_axis=0, concat_axis=0, tiled=True)]
    slice x68 -> x0, local copies, waits for them, and re-layouts: 9.22 us -> none  [the longest x48 5.04 us: cumulate(): rolled = jnp.roll(values, offset, axis_dim)]
    add x42 -> x0, other arithmetic: 7.32 us -> none  [the longest x29 4.99 us: cumulate(): values + jnp.where(position >= offset, rolled, jnp.zeros_like(rolled))]
    ppermute x3 -> x0, starting transfers between devices: 5.94 us -> none  [passed_along(): return lax.ppermute(block, axis, route)]
    ppermute x3 -> x0, waiting for transfers between devices: 2.88 us -> none  [passed_along(): return lax.ppermute(block, axis, route)]
    unnamed x12 -> x2, local copies, waits for them, and re-layouts: 3.22 us -> 1.04 us
  transfers between devices with their start and end apart: 5 -> 1, of which waited for: 3 -> 1; matrix products, arithmetic and copies ran while one was open for 0% -> 0% of each run, Pallas kernels for 0% -> 0%
where the time goes in v1:
time: 71.2 us; the launch traced here: 70 us
  Pallas kernels  33.2 us (47%)
  blocking collectives  19.5 us (27%)
  waiting for transfers between devices  8.13 us (11%)
  starting transfers between devices  7.39 us (10%)
  local copies, waits for them, and re-layouts  1.04 us (1%)
    pallas_call x1, Pallas kernels, on_device(): pl.pallas_call(functools.partial(prefix_kernel, me='gx', n=n), out_shape=...  30.2 us
    all_to_all x1, blocking collectives, on_device(): got = lax.all_to_all(send, 'gx', split_axis=0, concat_axis=0, tiled=True)  19.5 us
    all_to_all x1, waiting for transfers between devices, on_device(): lax.all_to_all(send, ('gy', 'gz'), split_axis=0, concat_axis=0, tiled=True)  8.13 us
    all_to_all x1, starting transfers between devices, on_device(): lax.all_to_all(send, ('gy', 'gz'), split_axis=0, concat_axis=0, tiled=True)  7.39 us
    pallas_call x1, Pallas kernels, on_device(): pl.pallas_call(functools.partial(stencil_kernel, n=n, ny=ny, nz=nz), in_s...  2.19 us
  transfers between devices with their start and end apart: 1, of which 1 were waited for; matrix products, arithmetic and copies ran while one was open for 0% of the time, Pallas kernels for 0%

profile of v1, /device:TPU:8, one launch (start us, length us, event | category | flops | bytes accessed | tf_op | source)
XLA Modules:
  0.0 70.0 jit_solution(5967758336920763002)
XLA Ops:
  0.0 0.0 copy-start
  0.0 1.0 %copy-done = s32[32,32,128]{2,1,0:T(8,128)S(1)} copy-done((s32[32,32,128]{2,1,0:T(8,128)S(1)}, s32[32,32,128]{2,1,0:T(8,128)}, u32[]{:S(2)}) %copy-start) | copy-done | bytes 524312
  1.0 30.2 %prefix.1 = (s32[32,32,128]{2,1,0:T(8,128)S(1)}, s32[32,128]{1,0:T(8,128)S(1)}, s32[32,128]{1,0:T(8,128)S(1)}, s32[32,128]{1,0:T(8,128)S(1)}, s32[32,128]{1,0:T(8,128)S(1)}, /*index=5*/s32[16,32,128]{2,1,0:T(8,128)S(1)}) custom-call(s32[32,32,128]{2,1,0:T(8,128)S(1)} %copy-done), custom_call_target="tpu_custom_call" | custom-call | tf_op jit(solution)/shard_map/prefix/pallas_call | solution.py:164
  31.2 19.5 %all_to_all.10.got = s32[16,32,128]{2,1,0:T(8,128)S(1)} all-to-all(s32[16,32,128]{2,1,0:T(8,128)S(1)} %get-tuple-element.14), channel_id=1, replica_groups=mesh['gx'=16,'gy'=4,'gz'=4] {'gx'}, dimensions={0} | all-to-all | bytes 524288 | tf_op jit(solution)/shard_map/all_to_all | solution.py:177
  50.7 0.8 %faces.1 = (s32[32,128]{1,0:T(8,128)S(1)}, s32[32,128]{1,0:T(8,128)S(1)}, s32[16,40,128]{2,1,0:T(8,128)}) custom-call(s32[16,32,128]{2,1,0:T(8,128)S(1)} %all_to_all.10.got, s32[32,128]{1,0:T(8,128)S(1)} %get-tuple-element.15.y_last, s32[32,128]{1,0:T(8,128)S(1)} %get-tuple-element.16.y_first, s32[32,128]{1,0:T(8,128)S(1)} %get-tuple-element.17.z_last, ...), custom_call_target="tpu_custom_call" | custom-call | tf_op jit(solution)/shard_map/faces/pallas_call | solution.py:178
  51.6 7.4 %all-to-all-start.1 = ((s32[16,40,128]{2,1,0:T(8,128)}), s32[16,40,128]{2,1,0:T(8,128)S(1)}, u32[]{:S(2)}, u32[]{:S(2)}) async-start(s32[16,40,128]{2,1,0:T(8,128)} %get-tuple-element.19), calls=%async_computation.1 | async-start | bytes 655360 | tf_op jit(solution)/shard_map/all_to_all | solution.py:184
  59.6 8.1 %all-to-all-done.1.got = s32[16,40,128]{2,1,0:T(8,128)S(1)} async-done(((s32[16,40,128]{2,1,0:T(8,128)}), s32[16,40,128]{2,1,0:T(8,128)S(1)}, u32[]{:S(2)}, u32[]{:S(2)}) %all-to-all-start.1) | async-done | bytes 327712 | tf_op jit(solution)/shard_map/all_to_all | solution.py:184
  67.8 2.2 %stencil.1 = f32[32,32,128]{2,1,0:T(8,128)} custom-call(f32[1]{0:T(128)S(6)} %copy.3.step, s32[16,40,128]{2,1,0:T(8,128)S(1)} %all-to-all-done.1.got, s32[32,32,128]{2,1,0:T(8,128)S(1)} %get-tuple-element.20.full, s32[32,128]{1,0:T(8,128)S(1)} %get-tuple-element.21.low, s32[32,128]{1,0:T(8,128)S(1)} %get-tuple-element.22.high), custom_call_target="tpu_custom_call" | custom-call | tf_op jit(solution)/shard_map/stencil/pallas_call | solution.py:186
Async XLA Ops:
  0.0 1.0 %copy-start = (s32[32,32,128]{2,1,0:T(8,128)S(1)}, s32[32,32,128]{2,1,0:T(8,128)}, u32[]{:S(2)}) copy-start(s32[32,32,128]{2,1,0:T(8,128)} %q.1) | copy-start | bytes 1572868
  51.6 16.2 %all-to-all-start.1 = ((s32[16,40,128]{2,1,0:T(8,128)}), s32[16,40,128]{2,1,0:T(8,128)S(1)}, u32[]{:S(2)}, u32[]{:S(2)}) async-start(s32[16,40,128]{2,1,0:T(8,128)} %get-tuple-element.19), calls=%async_computation.1 | async-start | bytes 655360 | tf_op jit(solution)/shard_map/all_to_all | solution.py:184

commit v2 on v1

--- a/solution.py
+++ b/solution.py
@@ -19,62 +19,72 @@
     return jnp.broadcast_to(tile[:, lane : lane + 1], tile.shape)
 
 
-def scan_lanes(v, lane):
-    s = 1
-    while s < v.shape[1]:
+def prefix_planes(v):
+    lane = lax.broadcasted_iota(I32, v.shape, 1)
+    for s in (1, 2, 4, 8, 16, 32, 64):
         v = v + jnp.where(lane >= s, pltpu.roll(v, s, 1), 0)
-        s *= 2
-    return v
-
-
-def scan_rows(v, row):
+    v = v.reshape(-1, 8, 128)
+    row = lax.broadcasted_iota(I32, v.shape, 1)
     for s in (1, 2, 4):
-        v = v + jnp.where(row >= s, pltpu.roll(v, s, 0), 0)
-    return v
-
-
-def prefix_kernel(q, full, y_last, y_first, z_last, z_first, send, *, me, n):
-    nx, ny, _ = q.shape
-    tiles = ny // 8
+        v = v + jnp.where(row >= s, pltpu.roll(v, s, 1), 0)
+    v = v.reshape(-1, 4, 8, 128)
+    tiles = [v[:, 0]]
+    for t in range(1, 4):
+        tiles.append(v[:, t] + tiles[-1][:, 7:8, :])
+    return tiles
+
+
+def planes_kernel(q, pair):
+    total = q[0]
+    for i in range(1, q.shape[0]):
+        total = total + q[i]
+    tiles = prefix_planes(jnp.concatenate([total, q[0]], 0))
+    for t in range(4):
+        for p in range(2):
+            pair[32 * p + 8 * t : 32 * p + 8 * t + 8, :] = tiles[t][p]
+
+
+def block_kernel(step, q, full, y_last, y_first, z_last, z_first, scale):
+    nx = q.shape[0]
     lane = lax.broadcasted_iota(I32, (8, 128), 1)
-    row = lax.broadcasted_iota(I32, (8, 128), 0)
     zero = jnp.zeros((8, 128), I32)
-    sums, zl, zf = [zero] * tiles, [zero] * tiles, [zero] * tiles
-    for i in range(nx):
-        carry = None
-        for t in range(tiles):
-            rows = slice(8 * t, 8 * t + 8)
-            v = scan_rows(scan_lanes(q[i, rows, :], lane), row)
-            if carry is not None:
-                v = v + carry
-            if t + 1 < tiles:
-                carry = jnp.broadcast_to(v[7:8, :], v.shape)
-            v = v + sums[t] if i else v
-            if t + 1 < tiles:
-                pass
-            sums[t] = v
-            full[i, rows, :] = v
-            zl[t] = jnp.where(lane == i, at_lane(v, 127), zl[t])
-            zf[t] = jnp.where(lane == i, at_lane(v, 0), zf[t])
-        y_first[i : i + 1, :] = sums[0][0:1, :]
-        y_last[i : i + 1, :] = sums[-1][7:8, :]
-    for t in range(tiles):
+    sums, zl, zf = [zero] * 4, [zero] * 4, [zero] * 4
+    for g in range(0, nx, 8):
+        tiles = prefix_planes(q[g : g + 8].reshape(256, 128))
+        for i in range(8):
+            for t in range(4):
+                sums[t] = sums[t] + tiles[t][i]
+                full[g + i, 8 * t : 8 * t + 8, :] = sums[t]
+                zl[t] = jnp.where(lane == g + i, at_lane(sums[t], 127), zl[t])
+                zf[t] = jnp.where(lane == g + i, at_lane(sums[t], 0), zf[t])
+            y_first[g + i : g + i + 1, :] = sums[0][0:1, :]
+            y_last[g + i : g + i + 1, :] = sums[3][7:8, :]
+    for t in range(4):
         z_last[8 * t : 8 * t + 8, :] = zl[t]
         z_first[8 * t : 8 * t + 8, :] = zf[t]
-    x = lax.axis_index(me)
-    for d in range(n):
-        for t in range(tiles):
-            rows = slice(8 * t, 8 * t + 8)
-            send[d, rows, :] = jnp.where(d == x - 1, full[0, rows, :], sums[t])
-
-
-def faces_kernel(got, y_last, y_first, z_last, z_first, low, high, send, *, n, ny, nz):
+    scale[...] = jnp.full((8, 128), step[0], jnp.float32)
+
+
+def pack_kernel(mine, other, send):
+    x = lax.axis_index("gx")
+    chip, south = x // 2, x % 2 == 0
+    both = mine[0:32, :] + other[0:32, :]
+    first = jnp.where(south, mine[32:64, :], other[32:64, :])
+    for d in range(send.shape[0]):
+        send[d] = jnp.where(d == chip - 1, first, both)
+
+
+def faces_kernel(
+    got, other, y_last, y_first, z_last, z_first, low, high, send, *, ny, nz
+):
     x, y, z = lax.axis_index("gx"), lax.axis_index("gy"), lax.axis_index("gz")
+    chips = got.shape[0]
+    chip, south = x // 2, x % 2 == 0
     lane = lax.broadcasted_iota(I32, (32, 128), 1)
-    c = jnp.zeros((32, 128), I32)
-    for s in range(n):
-        c = c + jnp.where(s < x, got[s], 0)
-    h = got[jnp.minimum(x + 1, n - 1)]
+    c = jnp.where(south, 0, other[0:32, :])
+    for s in range(chips - 1):
+        c = c + jnp.where(s < chip, got[s], 0)
+    h = jnp.where(south, other[32:64, :], got[jnp.minimum(chip + 1, chips - 1)])
     low[...] = c
     high[...] = h
     yl, yf, zl, zf = y_last[...], y_first[...], z_last[...], z_first[...]
@@ -122,8 +132,8 @@
     has_x = (x < n - 1).astype(jnp.float32)
     has_y = (y < ny - 1).astype(jnp.float32)
     has_z = (z < nz - 1).astype(jnp.float32)
-    half = step[0] * 0.5
-    twelfth = step[0] * (1.0 / 12.0)
+    half = jnp.broadcast_to(step[0:1, :], (32, 128)) * 0.5
+    twelfth = jnp.broadcast_to(step[0:1, :], (32, 128)) * (1.0 / 12.0)
     f32 = jnp.float32
     c = low[...]
 
@@ -160,36 +170,48 @@
 
 def on_device(quant_codes, error_step):
     n, ny, nz = (lax.axis_size(a) for a in ("gx", "gy", "gz"))
-    face = jax.ShapeDtypeStruct((32, 128), I32)
-    full, y_last, y_first, z_last, z_first, send = pl.pallas_call(
-        functools.partial(prefix_kernel, me="gx", n=n),
-        out_shape=(
-            jax.ShapeDtypeStruct(quant_codes.shape, I32),
-            face,
-            face,
-            face,
-            face,
-            jax.ShapeDtypeStruct((n, 32, 128), I32),
-        ),
-        compiler_params=params(),
-        name="prefix",
+    shape = jax.ShapeDtypeStruct
+    face = shape((32, 128), I32)
+    vmem = pl.BlockSpec(memory_space=pltpu.VMEM)
+    smem = pl.BlockSpec(memory_space=pltpu.SMEM)
+    mine = pl.pallas_call(
+        planes_kernel,
+        out_shape=shape((64, 128), I32),
+        compiler_params=params(),
+        name="planes",
     )(quant_codes)
-    got = lax.all_to_all(send, "gx", split_axis=0, concat_axis=0, tiled=True)
+    other = lax.ppermute(mine, "gx", [(i, i ^ 1) for i in range(n)])
+    full, y_last, y_first, z_last, z_first, scale = pl.pallas_call(
+        block_kernel,
+        in_specs=[smem, vmem],
+        out_shape=(shape(quant_codes.shape, I32), face, face, face, face, shape((8, 128), jnp.float32)),
+        compiler_params=params(),
+        cost_estimate=pl.CostEstimate(flops=4_000_000, bytes_accessed=1_100_000, transcendentals=0),
+        name="block",
+    )(error_step, quant_codes)
+    send = pl.pallas_call(
+        pack_kernel,
+        out_shape=shape((n // 2, 32, 128), I32),
+        compiler_params=params(),
+        name="pack",
+    )(mine, other)
+    same_core = [list(range(k, n, 2)) for k in range(2)]
+    got = lax.all_to_all(
+        send, "gx", split_axis=0, concat_axis=0, tiled=True, axis_index_groups=same_core
+    )
     low, high, send = pl.pallas_call(
-        functools.partial(faces_kernel, n=n, ny=ny, nz=nz),
-        out_shape=(face, face, jax.ShapeDtypeStruct((ny * nz, 40, 128), I32)),
+        functools.partial(faces_kernel, ny=ny, nz=nz),
+        out_shape=(face, face, shape((ny * nz, 40, 128), I32)),
         compiler_params=params(),
         name="faces",
-    )(got, y_last, y_first, z_last, z_first)
+    )(got, other, y_last, y_first, z_last, z_first)
     got = lax.all_to_all(send, ("gy", "gz"), split_axis=0, concat_axis=0, tiled=True)
-    vmem = pl.BlockSpec(memory_space=pltpu.VMEM)
     return pl.pallas_call(
         functools.partial(stencil_kernel, n=n, ny=ny, nz=nz),
-        in_specs=[pl.BlockSpec(memory_space=pltpu.SMEM)] + [vmem] * 4,
-        out_shape=jax.ShapeDtypeStruct(quant_codes.shape, jnp.float32),
+        out_shape=shape(quant_codes.shape, jnp.float32),
         compiler_params=params(),
         name="stencil",
-    )(error_step, got, full, low, high)
+    )(scale, got, full, low, high)
 
 
 def solution(mesh):

time: 71.2 us -> 38.5 us (0.54); the launches traced: 70 us -> 38.2 us
  Pallas kernels: 33.2 us -> 5.77 us
  blocking collectives: 19.5 us -> 14.5 us
  starting transfers between devices: 7.39 us -> 8.56 us
    pallas_call x3 -> x5, Pallas kernels: 33.2 us -> 5.77 us  [the longest x1 2.27 us: on_device(): pl.pallas_call(block_kernel, in_specs=[smem, vmem], out_shape=(shape(quan...]
    all_to_all x1, blocking collectives: 19.5 us -> 14.5 us  [on_device(): lax.all_to_all(send, ('gy', 'gz'), split_axis=0, concat_axis=0, tiled=True)]
    all_to_all x1, waiting for transfers between devices: 8.13 us -> 6.46 us  [on_device(): lax.all_to_all(send, 'gx', split_axis=0, concat_axis=0, tiled=True, axis_...]
    ppermute x0 -> x1, waiting for transfers between devices: none -> 1.19 us  [on_device(): other = lax.ppermute(mine, 'gx', [(i, i ^ 1) for i in range(n)])]
    all_to_all x1, starting transfers between devices: 7.39 us -> 8.47 us  [on_device(): lax.all_to_all(send, 'gx', split_axis=0, concat_axis=0, tiled=True, axis_...]
  transfers between devices with their start and end apart: 1 -> 2, of which waited for: 1 -> 2; matrix products, arithmetic and copies ran while one was open for 0% -> 0% of each run, Pallas kernels for 0% -> 6%
where the time goes in v2:
time: 38.5 us; the launch traced here: 38.2 us
  blocking collectives  14.5 us (38%)
  starting transfers between devices  8.56 us (22%)
  waiting for transfers between devices  7.65 us (20%)
  Pallas kernels  5.77 us (15%)
  local copies, waits for them, and re-layouts  1.04 us (3%)
  between operations  0.69 us (2%)
    all_to_all x1, blocking collectives, on_device(): lax.all_to_all(send, ('gy', 'gz'), split_axis=0, concat_axis=0, tiled=True)  14.5 us
    all_to_all x1, starting transfers between devices, on_device(): lax.all_to_all(send, 'gx', split_axis=0, concat_axis=0, tiled=True, axis_...  8.47 us
    all_to_all x1, waiting for transfers between devices, on_device(): lax.all_to_all(send, 'gx', split_axis=0, concat_axis=0, tiled=True, axis_...  6.46 us
    pallas_call x1, Pallas kernels, on_device(): pl.pallas_call(block_kernel, in_specs=[smem, vmem], out_shape=(shape(quan...  2.27 us
    pallas_call x1, Pallas kernels, on_device(): pl.pallas_call(functools.partial(stencil_kernel, n=n, ny=ny, nz=nz), out_...  2.19 us
    ppermute x1, waiting for transfers between devices, on_device(): other = lax.ppermute(mine, 'gx', [(i, i ^ 1) for i in range(n)])  1.19 us
    unnamed x4, local copies, waits for them, and re-layouts  1.04 us
  transfers between devices with their start and end apart: 2, of which 2 were waited for; matrix products, arithmetic and copies ran while one was open for 0% of the time, Pallas kernels for 6%

profile of v2, /device:TPU:8, one launch (start us, length us, event | category | flops | bytes accessed | tf_op | source)
XLA Modules:
  0.0 38.2 jit_solution(481147202497761194)
XLA Ops:
  0.0 0.0 copy-start
  0.0 1.0 %copy-done = s32[32,32,128]{2,1,0:T(8,128)S(1)} copy-done((s32[32,32,128]{2,1,0:T(8,128)S(1)}, s32[32,32,128]{2,1,0:T(8,128)}, u32[]{:S(2)}) %copy-start) | copy-done | bytes 524312
  1.0 0.0 copy-start.1
  1.0 0.5 %planes.1.mine = s32[64,128]{1,0:T(8,128)S(1)} custom-call(s32[32,32,128]{2,1,0:T(8,128)S(1)} %copy-done), custom_call_target="tpu_custom_call" | custom-call | tf_op jit(solution)/shard_map/planes/pallas_call | solution.py:177
  1.6 0.1 collective-permute-start
  1.7 1.2 %collective-permute-done.other = s32[64,128]{1,0:T(8,128)S(1)} collective-permute-done((s32[64,128]{1,0:T(8,128)S(1)}, s32[64,128]{1,0:T(8,128)S(1)}, u32[]{:S(2)}, u32[]{:S(2)}) %collective-permute-start) | collective-permute-done | bytes 32800 | tf_op jit(solution)/shard_map/ppermute | solution.py:183
  2.9 0.7 %pack.1 = s32[8,32,128]{2,1,0:T(8,128)} custom-call(s32[64,128]{1,0:T(8,128)S(1)} %planes.1.mine, s32[64,128]{1,0:T(8,128)S(1)} %collective-permute-done.other), custom_call_target="tpu_custom_call" | custom-call | tf_op jit(solution)/shard_map/pack/pallas_call | solution.py:192
  3.6 8.5 %all-to-all-start = ((s32[8,32,128]{2,1,0:T(8,128)}), s32[8,32,128]{2,1,0:T(8,128)S(1)}, u32[]{:S(2)}, u32[]{:S(2)}) async-start(s32[8,32,128]{2,1,0:T(8,128)} %pack.1), calls=%async_computation | async-start | bytes 262144 | tf_op jit(solution)/shard_map/all_to_all | solution.py:199
  12.7 0.0 copy-done.1
  12.7 2.3 %block.1 = (s32[32,32,128]{2,1,0:T(8,128)S(1)}, s32[32,128]{1,0:T(8,128)S(1)}, s32[32,128]{1,0:T(8,128)S(1)}, s32[32,128]{1,0:T(8,128)S(1)}, s32[32,128]{1,0:T(8,128)S(1)}, /*index=5*/f32[8,128]{1,0:T(8,128)S(1)}) custom-call(f32[1]{0:T(128)S(6)} %copy.3.step, s32[32,32,128]{2,1,0:T(8,128)S(1)} %copy-done.1), custom_call_target="tpu_custom_call" | custom-call | flops 4000000 | bytes 1100000 | tf_op jit(solution)/shard_map/block/pallas_call | solution.py:184
  15.0 6.5 %all-to-all-done.got = s32[8,32,128]{2,1,0:T(8,128)S(1)} async-done(((s32[8,32,128]{2,1,0:T(8,128)}), s32[8,32,128]{2,1,0:T(8,128)S(1)}, u32[]{:S(2)}, u32[]{:S(2)}) %all-to-all-start) | async-done | bytes 131104 | tf_op jit(solution)/shard_map/all_to_all | solution.py:199
  21.4 0.1 faces.1
  21.5 14.5 %all_to_all.10.got = s32[16,40,128]{2,1,0:T(8,128)S(1)} all-to-all(s32[16,40,128]{2,1,0:T(8,128)S(1)} %get-tuple-element.19), channel_id=1, replica_groups=mesh['gx'=16,'gy'=4,'gz'=4] {'gy','gz'}, dimensions={0} | all-to-all | bytes 655360 | tf_op jit(solution)/shard_map/all_to_all | solution.py:208
  36.0 2.2 %stencil.1 = f32[32,32,128]{2,1,0:T(8,128)} custom-call(f32[8,128]{1,0:T(8,128)S(1)} %get-tuple-element.14.step, s32[16,40,128]{2,1,0:T(8,128)S(1)} %all_to_all.10.got, s32[32,32,128]{2,1,0:T(8,128)S(1)} %get-tuple-element.20.full, s32[32,128]{1,0:T(8,128)S(1)} %get-tuple-element.21.low, s32[32,128]{1,0:T(8,128)S(1)} %get-tuple-element.22.high), custom_call_target="tpu_custom_call" | custom-call | tf_op jit(solution)/shard_map/stencil/pallas_call | solution.py:209
Async XLA Ops:
  0.0 1.0 %copy-start = (s32[32,32,128]{2,1,0:T(8,128)S(1)}, s32[32,32,128]{2,1,0:T(8,128)}, u32[]{:S(2)}) copy-start(s32[32,32,128]{2,1,0:T(8,128)} %q.3) | copy-start | bytes 1572868
  1.0 11.6 %copy-start.1 = (s32[32,32,128]{2,1,0:T(8,128)S(1)}, s32[32,32,128]{2,1,0:T(8,128)}, u32[]{:S(2)}) copy-start(s32[32,32,128]{2,1,0:T(8,128)} %q.3) | copy-start | bytes 1572868
  1.6 1.3 %collective-permute-start = (s32[64,128]{1,0:T(8,128)S(1)}, s32[64,128]{1,0:T(8,128)S(1)}, u32[]{:S(2)}, u32[]{:S(2)}) collective-permute-start(s32[64,128]{1,0:T(8,128)S(1)} %planes.1.mine), channel_id=1, source_target_pairs={{0,16},{16,0},{32,48},{48,32},{64,80},{80,64},{96,112},{112,96},{1... | collective-permute-start | bytes 98312 | tf_op jit(solution)/shard_map/ppermute | solution.py:183
  3.6 17.9 %all-to-all-start = ((s32[8,32,128]{2,1,0:T(8,128)}), s32[8,32,128]{2,1,0:T(8,128)S(1)}, u32[]{:S(2)}, u32[]{:S(2)}) async-start(s32[8,32,128]{2,1,0:T(8,128)} %pack.1), calls=%async_computation | async-start | bytes 262144 | tf_op jit(solution)/shard_map/all_to_all | solution.py:199

commit v3 on v2

--- a/solution.py
+++ b/solution.py
@@ -19,11 +19,22 @@
     return jnp.broadcast_to(tile[:, lane : lane + 1], tile.shape)
 
 
+def prefix_lanes(v):
+    k = lax.broadcasted_iota(I32, (256, 128), 0)
+    upto = (k & 127) <= lax.broadcasted_iota(I32, (256, 128), 1)
+    ones = jnp.where(upto, jnp.where(k < 128, 1.0, 256.0), 0.0).astype(jnp.bfloat16)
+
+    def halves(low, high):
+        both = jnp.concatenate([low, high], 1).astype(jnp.float32).astype(jnp.bfloat16)
+        return jnp.dot(both, ones, preferred_element_type=jnp.float32).astype(I32)
+
+    small = halves(v & 255, (v >> 8) & 255)
+    large = halves((v >> 16) & 255, v >> 24)
+    return small + (large << 16)
+
+
 def prefix_planes(v):
-    lane = lax.broadcasted_iota(I32, v.shape, 1)
-    for s in (1, 2, 4, 8, 16, 32, 64):
-        v = v + jnp.where(lane >= s, pltpu.roll(v, s, 1), 0)
-    v = v.reshape(-1, 8, 128)
+    v = prefix_lanes(v).reshape(-1, 8, 128)
     row = lax.broadcasted_iota(I32, v.shape, 1)
     for s in (1, 2, 4):
         v = v + jnp.where(row >= s, pltpu.roll(v, s, 1), 0)
@@ -35,9 +46,10 @@
 
 
 def planes_kernel(q, pair):
-    total = q[0]
-    for i in range(1, q.shape[0]):
-        total = total + q[i]
+    sums = [q[i] for i in range(4)]
+    for i in range(4, q.shape[0]):
+        sums[i % 4] = sums[i % 4] + q[i]
+    total = (sums[0] + sums[1]) + (sums[2] + sums[3])
     tiles = prefix_planes(jnp.concatenate([total, q[0]], 0))
     for t in range(4):
         for p in range(2):
@@ -65,7 +77,7 @@
     scale[...] = jnp.full((8, 128), step[0], jnp.float32)
 
 
-def pack_kernel(mine, other, send):
+def pack_kernel(mine, other, _, send):
     x = lax.axis_index("gx")
     chip, south = x // 2, x % 2 == 0
     both = mine[0:32, :] + other[0:32, :]
@@ -108,11 +120,12 @@
             send[a * nz + b, 32:40, :] = yl_tail
 
 
-def stencil_kernel(step, got, full, low, high, out, *, n, ny, nz):
+def stencil_kernel(
+    step, got, full, low, high, result, field, left, right, out, sems, *, n, ny, nz
+):
     x, y, z = lax.axis_index("gx"), lax.axis_index("gy"), lax.axis_index("gz")
+    f32 = jnp.float32
     nx = full.shape[0]
-    lane = lax.broadcasted_iota(I32, (32, 128), 1)
-    row = lax.broadcasted_iota(I32, (32, 128), 0)
     ay = jnp.zeros((40, 128), I32)
     az = jnp.zeros((32, 128), I32)
     ayz = jnp.zeros((1, 128), I32)
@@ -129,43 +142,45 @@
         hyz = hyz + jnp.where(b < z, got[yp * nz + b, 0:1, :], 0)
     az = az + ayz
     hy = got[yp * nz + z, 0:32, :]
-    has_x = (x < n - 1).astype(jnp.float32)
-    has_y = (y < ny - 1).astype(jnp.float32)
-    has_z = (z < nz - 1).astype(jnp.float32)
+    has_x = (x < n - 1).astype(f32)
+    has_y = (y < ny - 1).astype(f32)
+    has_z = (z < nz - 1).astype(f32)
     half = jnp.broadcast_to(step[0:1, :], (32, 128)) * 0.5
     twelfth = jnp.broadcast_to(step[0:1, :], (32, 128)) * (1.0 / 12.0)
-    f32 = jnp.float32
     c = low[...]
-
-    def plane(i):
+    for i in range(-1, nx + 1):
         k = nx if i < 0 else nx + 1 if i == nx else i
-        left = at_lane(az, k)
-        here = c + left + ay[k : k + 1, :]
+        edge = at_lane(az, k)
+        here = c + edge + ay[k : k + 1, :]
         if i >= 0:
             here = here + full[min(i, nx - 1)]
         if i == nx:
-            here = here + high[...]
-        return here, left
-
-    before = plane(-1)[0].astype(f32)
-    now, left = plane(0)
-    now_f = now.astype(f32)
+            field[i + 1, 8:40, :] = (here + high[...]).astype(f32) * has_x
+            continue
+        field[i + 1, 8:40, :] = here.astype(f32)
+        if i < 0:
+            continue
+        left[i] = edge.astype(f32)
+        right[i] = (here + at_lane(hz, i)).astype(f32) * has_z
+        up = ay[i : i + 1, :] + jnp.broadcast_to(ayz[:, i : i + 1], (1, 128))
+        field[i + 1, 7:8, :] = up.astype(f32)
+        down = here[31:32, :] + hy[i : i + 1, :] + jnp.broadcast_to(hyz[:, i : i + 1], (1, 128))
+        field[i + 1, 40:41, :] = down.astype(f32) * has_y
+    lane = lax.broadcasted_iota(I32, (32, 128), 1)
+    copies = []
     for i in range(nx):
-        after, after_left = plane(i + 1)
-        after_f = after.astype(f32)
-        if i == nx - 1:
-            after_f = after_f * has_x
-        total = before + after_f
-        up = (ay[i : i + 1, :] + jnp.broadcast_to(ayz[:, i : i + 1], (1, 128))).astype(f32)
-        down = now[31:32, :] + hy[i : i + 1, :] + jnp.broadcast_to(hyz[:, i : i + 1], (1, 128))
-        down = down.astype(f32) * has_y
-        total = total + jnp.where(row == 0, up, pltpu.roll(now_f, 1, 0))
-        total = total + jnp.where(row == 31, down, pltpu.roll(now_f, 31, 0))
-        right = (now + at_lane(hz, i)).astype(f32) * has_z
-        total = total + jnp.where(lane == 0, left.astype(f32), pltpu.roll(now_f, 1, 1))
-        total = total + jnp.where(lane == 127, right, pltpu.roll(now_f, 127, 1))
-        out[i] = now_f * half + total * twelfth
-        before, now, now_f, left = now_f, after, after_f, after_left
+        now = field[i + 1, 8:40, :]
+        total = field[i, 8:40, :] + field[i + 2, 8:40, :]
+        total = total + (field[i + 1, 7:39, :] + field[i + 1, 9:41, :])
+        total = total + jnp.where(lane == 0, left[i], pltpu.roll(now, 1, 1))
+        total = total + jnp.where(lane == 127, right[i], pltpu.roll(now, 127, 1))
+        out[i] = now * half + total * twelfth
+        if i % 8 == 7:
+            rows = slice(i - 7, i + 1)
+            copies.append(pltpu.make_async_copy(out.at[rows], result.at[rows], sems.at[i // 8]))
+            copies[-1].start()
+    for c in copies:
+        c.wait()
 
 
 def on_device(quant_codes, error_step):
@@ -174,6 +189,7 @@
     face = shape((32, 128), I32)
     vmem = pl.BlockSpec(memory_space=pltpu.VMEM)
     smem = pl.BlockSpec(memory_space=pltpu.SMEM)
+    hbm = pl.BlockSpec(memory_space=pltpu.HBM)
     mine = pl.pallas_call(
         planes_kernel,
         out_shape=shape((64, 128), I32),
@@ -191,10 +207,11 @@
     )(error_step, quant_codes)
     send = pl.pallas_call(
         pack_kernel,
+        in_specs=[vmem, vmem, pl.BlockSpec(memory_space=pl.ANY)],
         out_shape=shape((n // 2, 32, 128), I32),
         compiler_params=params(),
         name="pack",
-    )(mine, other)
+    )(mine, other, scale)
     same_core = [list(range(k, n, 2)) for k in range(2)]
     got = lax.all_to_all(
         send, "gx", split_axis=0, concat_axis=0, tiled=True, axis_index_groups=same_core
@@ -208,7 +225,15 @@
     got = lax.all_to_all(send, ("gy", "gz"), split_axis=0, concat_axis=0, tiled=True)
     return pl.pallas_call(
         functools.partial(stencil_kernel, n=n, ny=ny, nz=nz),
+        out_specs=hbm,
         out_shape=shape(quant_codes.shape, jnp.float32),
+        scratch_shapes=[
+            pltpu.VMEM((34, 48, 128), jnp.float32),
+            pltpu.VMEM(quant_codes.shape, jnp.float32),
+            pltpu.VMEM(quant_codes.shape, jnp.float32),
+            pltpu.VMEM(quant_codes.shape, jnp.float32),
+            pltpu.SemaphoreType.DMA((4,)),
+        ],
         compiler_params=params(),
         name="stencil",
     )(scale, got, full, low, high)

time: 38.5 us -> 36.9 us (0.958)
  blocking collectives: 14.5 us -> 32.4 us
  starting transfers between devices: 8.56 us -> 0.09 us
  waiting for transfers between devices: 7.65 us -> 0.01 us
  Pallas kernels: 5.77 us -> 2.49 us
    all_to_all x0 -> x1, blocking collectives: none -> 18 us  [on_device(): lax.all_to_all(send, 'gx', split_axis=0, concat_axis=0, tiled=True, axis_...]
    all_to_all x1 -> x0, starting transfers between devices: 8.47 us -> none  [on_device(): lax.all_to_all(send, 'gx', split_axis=0, concat_axis=0, tiled=True, axis_...]
    all_to_all x1 -> x0, waiting for transfers between devices: 6.46 us -> none  [on_device(): lax.all_to_all(send, 'gx', split_axis=0, concat_axis=0, tiled=True, axis_...]
    pallas_call x1, Pallas kernels: 2.27 us -> 0.69 us  [on_device(): pl.pallas_call(block_kernel, in_specs=[smem, vmem], out_shape=(shape(quan...]
    ppermute x1, waiting for transfers between devices: 1.19 us -> 0.01 us  [on_device(): other = lax.ppermute(mine, 'gx', [(i, i ^ 1) for i in range(n)])]
    pallas_call x1, Pallas kernels: 2.19 us -> 1.48 us  [on_device(): pl.pallas_call(functools.partial(stencil_kernel, n=n, ny=ny, nz=nz), out_...]
    pallas_call x1, Pallas kernels: 0.67 us -> 0.03 us  [on_device(): pl.pallas_call(pack_kernel, in_specs=[vmem, vmem, pl.BlockSpec(memory_spa...]
    unnamed x4 -> x2, local copies, waits for them, and re-layouts: 1.04 us -> 1.04 us
  transfers between devices with their start and end apart: 2 -> 1, of which waited for: 2 -> 0; matrix products, arithmetic and copies ran while one was open for 0% -> 0% of each run, Pallas kernels for 6% -> 2%
where the time goes in v3:
time: 36.9 us; the launch traced here: 36.7 us
  blocking collectives  32.4 us (88%)
  Pallas kernels  2.49 us (7%)
  local copies, waits for them, and re-layouts  1.04 us (3%)
  between operations  0.69 us (2%)
    all_to_all x1, blocking collectives, on_device(): lax.all_to_all(send, 'gx', split_axis=0, concat_axis=0, tiled=True, axis_...  18 us
    all_to_all x1, blocking collectives, on_device(): lax.all_to_all(send, ('gy', 'gz'), split_axis=0, concat_axis=0, tiled=True)  14.4 us
    pallas_call x1, Pallas kernels, on_device(): pl.pallas_call(functools.partial(stencil_kernel, n=n, ny=ny, nz=nz), out_...  1.48 us
    unnamed x2, local copies, waits for them, and re-layouts  1.04 us
  transfers between devices with their start and end apart: 1, of which 0 were waited for; matrix products, arithmetic and copies ran while one was open for 0% of the time, Pallas kernels for 2%

profile of v3, /device:TPU:8, one launch (start us, length us, event | category | flops | bytes accessed | tf_op | source)
XLA Modules:
  0.0 36.7 jit_solution(9572411556100477840)
XLA Ops:
  0.0 0.0 copy-start
  0.0 1.0 %copy-done = s32[32,32,128]{2,1,0:T(8,128)S(1)} copy-done((s32[32,32,128]{2,1,0:T(8,128)S(1)}, s32[32,32,128]{2,1,0:T(8,128)}, u32[]{:S(2)}) %copy-start) | copy-done | bytes 524312
  1.0 0.2 planes.1.mine
  1.2 0.1 collective-permute-start
  2.0 0.7 %block.1 = (s32[32,32,128]{2,1,0:T(8,128)S(1)}, s32[32,128]{1,0:T(8,128)S(1)}, s32[32,128]{1,0:T(8,128)S(1)}, s32[32,128]{1,0:T(8,128)S(1)}, s32[32,128]{1,0:T(8,128)S(1)}, /*index=5*/f32[8,128]{1,0:T(8,128)S(1)}) custom-call(f32[1]{0:T(128)S(6)} %copy.3.step, s32[32,32,128]{2,1,0:T(8,128)S(1)} %copy-done), custom_call_target="tpu_custom_call" | custom-call | flops 4000000 | bytes 1100000 | tf_op jit(solution)/shard_map/block/pallas_call | solution.py:200
  2.7 0.0 collective-permute-done.other
  2.7 18.0 %all_to_all.10.got = s32[8,32,128]{2,1,0:T(8,128)S(1)} all-to-all(s32[8,32,128]{2,1,0:T(8,128)S(1)} %pack.1), channel_id=1, replica_groups={{0,32,64,96,128,160,192,224},{16,48,80,112,144,176,208,240},{1,33,65,97..., dimensions={0} | all-to-all | bytes 262144 | tf_op jit(solution)/shard_map/all_to_all | solution.py:216
  20.7 0.1 faces.1
  20.8 14.4 %all_to_all.11.got = s32[16,40,128]{2,1,0:T(8,128)S(1)} all-to-all(s32[16,40,128]{2,1,0:T(8,128)S(1)} %get-tuple-element.19), channel_id=1, replica_groups=mesh['gx'=16,'gy'=4,'gz'=4] {'gy','gz'}, dimensions={0} | all-to-all | bytes 655360 | tf_op jit(solution)/shard_map/all_to_all | solution.py:225
  35.3 1.5 %stencil.1 = f32[32,32,128]{2,1,0:T(8,128)} custom-call(f32[8,128]{1,0:T(8,128)S(1)} %get-tuple-element.14._.step, s32[16,40,128]{2,1,0:T(8,128)S(1)} %all_to_all.11.got, s32[32,32,128]{2,1,0:T(8,128)S(1)} %get-tuple-element.20.full, s32[32,128]{1,0:T(8,128)S(1)} %get-tuple-element.21.low, s32[32,128]{1,0:T(8,128)S(1)} %get-tuple-element.22.high), custom_call_target="tpu_custom_call" | custom-call | tf_op jit(solution)/shard_map/stencil/pallas_call | solution.py:226
  (1 shorter events, 0.0 us)
Async XLA Ops:
  0.0 1.0 %copy-start = (s32[32,32,128]{2,1,0:T(8,128)S(1)}, s32[32,32,128]{2,1,0:T(8,128)}, u32[]{:S(2)}) copy-start(s32[32,32,128]{2,1,0:T(8,128)} %q.3) | copy-start | bytes 1572868
  1.2 1.4 %collective-permute-start = (s32[64,128]{1,0:T(8,128)S(1)}, s32[64,128]{1,0:T(8,128)S(1)}, u32[]{:S(2)}, u32[]{:S(2)}) collective-permute-start(s32[64,128]{1,0:T(8,128)S(1)} %planes.1.mine), channel_id=1, source_target_pairs={{0,16},{16,0},{32,48},{48,32},{64,80},{80,64},{96,112},{112,96},{1... | collective-permute-start | bytes 98312 | tf_op jit(solution)/shard_map/ppermute | solution.py:199

commit v4 on v3

v4 whole, which is shorter than its diff:
```python
import functools

import jax
import jax.numpy as jnp
from jax import lax
from jax.experimental import pallas as pl
from jax.experimental.pallas import tpu as pltpu
from jax.sharding import PartitionSpec as P

I32 = jnp.int32
LIMIT = 16 * 1024 * 1024


def params():
    return pltpu.CompilerParams(vmem_limit_bytes=LIMIT)


def at_lane(tile, lane):
    return jnp.broadcast_to(tile[:, lane : lane + 1], tile.shape)


def prefix_lanes(v):
    k = lax.broadcasted_iota(I32, (256, 128), 0)
    upto = (k & 127) <= lax.broadcasted_iota(I32, (256, 128), 1)
    ones = jnp.where(upto, jnp.where(k < 128, 1.0, 256.0), 0.0).astype(jnp.bfloat16)

    def halves(low, high):
        both = jnp.concatenate([low, high], 1).astype(jnp.float32).astype(jnp.bfloat16)
        return jnp.dot(both, ones, preferred_element_type=jnp.float32).astype(I32)

    small = halves(v & 255, (v >> 8) & 255)
    large = halves((v >> 16) & 255, v >> 24)
    return small + (large << 16)


def prefix_planes(v):
    v = prefix_lanes(v).reshape(-1, 8, 128)
    row = lax.broadcasted_iota(I32, v.shape, 1)
    for s in (1, 2, 4):
        v = v + jnp.where(row >= s, pltpu.roll(v, s, 1), 0)
    v = v.reshape(-1, 4, 8, 128)
    tiles = [v[:, 0]]
    for t in range(1, 4):
        tiles.append(v[:, t] + tiles[-1][:, 7:8, :])
    return tiles


def planes_kernel(q, pair):
    sums = [q[i] for i in range(4)]
    for i in range(4, q.shape[0]):
        sums[i % 4] = sums[i % 4] + q[i]
    total = (sums[0] + sums[1]) + (sums[2] + sums[3])
    tiles = prefix_planes(jnp.concatenate([total, q[0]], 0))
    for t in range(4):
        for p in range(2):
            pair[32 * p + 8 * t : 32 * p + 8 * t + 8, :] = tiles[t][p]


def block_kernel(step, q, full, faces, scale):
    nx = q.shape[0]
    lane = lax.broadcasted_iota(I32, (8, 128), 1)
    zero = jnp.zeros((8, 128), I32)
    sums, zl, zf = [zero] * 4, [zero] * 4, [zero] * 4
    for g in range(0, nx, 8):
        tiles = prefix_planes(q[g : g + 8].reshape(256, 128))
        for i in range(8):
            for t in range(4):
                sums[t] = sums[t] + tiles[t][i]
                full[g + i, 8 * t : 8 * t + 8, :] = sums[t]
                zl[t] = jnp.where(lane == g + i, at_lane(sums[t], 127), zl[t])
                zf[t] = jnp.where(lane == g + i, at_lane(sums[t], 0), zf[t])
            faces[g + i : g + i + 1, :] = sums[3][7:8, :]
            faces[32 + g + i : 33 + g + i, :] = sums[0][0:1, :]
    for t in range(4):
        faces[64 + 8 * t : 72 + 8 * t, :] = zl[t]
        faces[96 + 8 * t : 104 + 8 * t, :] = zf[t]
    scale[...] = jnp.full((8, 128), step[0], jnp.float32)


def chip_kernel(mine, other, send):
    send[0:32, :] = mine[0:32, :] + other[0:32, :]
    send[32:64, :] = other[32:64, :]


def pair_kernel(sent, got, send, state):
    chip = lax.axis_index("gx") // 2
    odd = chip % 2 == 1
    send[0:32, :] = sent[0:32, :] + got[0:32, :]
    send[32:64, :] = got[32:64, :]
    state[0:32, :] = jnp.where(odd, got[0:32, :], 0)
    state[32:64, :] = got[32:64, :]


def quad_kernel(sent, got, before, send, state):
    chip = lax.axis_index("gx") // 2
    send[0:32, :] = sent[0:32, :] + got[0:32, :]
    send[32:64, :] = got[32:64, :]
    state[0:32, :] = before[0:32, :] + jnp.where(chip % 4 >= 2, got[0:32, :], 0)
    state[32:64, :] = jnp.where(chip % 4 == 1, got[32:64, :], before[32:64, :])


def faces_kernel(got, before, other, mine, theirs, y_up, y_back, z_base, planes):
    chip, y = lax.axis_index("gx") // 2, lax.axis_index("gy")
    lane = lax.broadcasted_iota(I32, (32, 128), 1)
    row = lax.broadcasted_iota(I32, (8, 128), 0)
    c = before[0:32, :] + jnp.where(chip >= 4, got[0:32, :], 0)
    nxt = jnp.where(chip == 3, got[32:64, :], before[32:64, :])
    d = c + other[0:32, :]
    planes[0:32, :] = c
    planes[32:64, :] = d
    planes[64:96, :] = nxt
    last = d[31:32, :] + mine[31:32, :] + nxt[31:32, :]
    tail = jnp.where(row == 0, c[31:32, :], jnp.where(row == 1, last, 0))
    south, north = theirs[0:32, :] + c[31:32, :], mine[0:32, :] + d[31:32, :]
    y_up[0:32, :] = south
    y_up[32:64, :] = north
    y_up[64:72, :] = tail
    y_back[0:32, :] = jnp.where(y == 0, south, theirs[32:64, :] + c[0:1, :])
    y_back[32:64, :] = jnp.where(y == 0, north, mine[32:64, :] + d[0:1, :])
    y_back[64:72, :] = tail
    for k, at in ((64, 127), (96, 0)):
        low, high = at_lane(c, at), at_lane(d, at)
        above = high + at_lane(mine[k : k + 32, :], 31) + at_lane(nxt, at)
        base = jnp.where(lane < 32, theirs[k : k + 32, :] + low, 0)
        base = jnp.where((lane >= 32) & (lane < 64), pltpu.roll(mine[k : k + 32, :], 32, 1) + high, base)
        base = jnp.where(lane == 64, low, jnp.where(lane == 65, above, base))
        z_base[k - 64 : k - 32, :] = base


def lower(index, got1, got2, got3):
    one = jnp.where(index >= 1, got1[...], 0)
    two = jnp.where(index >= 2, got2[...], 0)
    return one + two + jnp.where(index >= 3, got3[...], 0)


def columns_kernel(got1, got2, got3, z_base, rows, z_up, z_back):
    y, z = lax.axis_index("gy"), lax.axis_index("gz")
    ay = lower(y, got1, got2, got3)
    hy = jnp.where(y < 3, got3[...], 0)
    rows[0:72, :] = ay
    rows[72:144, :] = hy
    pad = jnp.zeros((56, 128), I32)
    ay_t = jnp.concatenate([ay, pad], 0).T
    hy_t = jnp.concatenate([hy, pad], 0).T
    row = lax.broadcasted_iota(I32, (8, 128), 0)
    end = ay_t[127:128, :]
    tail = jnp.where(row == 0, end, jnp.where(row == 1, hy_t[127:128, :], 0))
    up = z_base[0:32, :] + end
    z_up[0:32, :] = up
    z_up[32:40, :] = tail
    z_back[0:32, :] = jnp.where(z == 0, up, z_base[32:64, :] + ay_t[0:1, :])
    z_back[32:40, :] = tail


def split_kernel(got1, got2, got3, rows, planes, south, north):
    z = lax.axis_index("gz")
    az = lower(z, got1, got2, got3)
    hz = got3[0:32, :]
    lane = lax.broadcasted_iota(I32, (40, 128), 1)
    row = lax.broadcasted_iota(I32, (8, 128), 0)

    def tail(a, b):
        return jnp.where(row == 0, rows[a : a + 1, :], jnp.where(row == 1, rows[b : b + 1, :], 0))

    south[0:32, :] = rows[0:32, :]
    south[32:40, :] = tail(64, 32)
    edges = jnp.where(lane == 32, at_lane(az, 64), jnp.where(lane == 33, at_lane(az, 32), az))
    south[40:80, :] = edges
    south[80:112, :] = hz
    south[112:144, :] = rows[72:104, :]
    south[144:176, :] = planes[0:32, :]
    north[0:32, :] = rows[32:64, :]
    north[32:40, :] = tail(31, 65)
    north[40:80, :] = jnp.where(lane == 32, at_lane(az, 31), pltpu.roll(az, 96, 1))
    north[80:112, :] = pltpu.roll(hz, 96, 1)
    north[112:144, :] = rows[104:136, :]
    north[144:176, :] = planes[32:64, :]


def stencil(step, pack, full, high, result, field, left, right, out, sems, *, n, ny, nz):
    x, y, z = lax.axis_index("gx"), lax.axis_index("gy"), lax.axis_index("gz")
    f32 = jnp.float32
    nx = full.shape[0]
    ay, az, hz, hy = pack[0:40, :], pack[40:72, :], pack[80:112, :], pack[112:144, :]
    ayz, hyz, c = pack[72:73, :], pack[73:74, :], pack[144:176, :]
    has_x = (x < n - 1).astype(f32)
    has_y = (y < ny - 1).astype(f32)
    has_z = (z < nz - 1).astype(f32)
    half = jnp.broadcast_to(step[0:1, :], (32, 128)) * 0.5
    twelfth = jnp.broadcast_to(step[0:1, :], (32, 128)) * (1.0 / 12.0)
    for i in range(-1, nx + 1):
        k = nx if i < 0 else nx + 1 if i == nx else i
        edge = at_lane(az, k)
        here = c + edge + ay[k : k + 1, :]
        if i >= 0:
            here = here + full[min(i, nx - 1)]
        if i == nx:
            field[i + 1, 8:40, :] = (here + high).astype(f32) * has_x
            continue
        field[i + 1, 8:40, :] = here.astype(f32)
        if i < 0:
            continue
        left[i] = edge.astype(f32)
        right[i] = (here + at_lane(hz, i)).astype(f32) * has_z
        up = ay[i : i + 1, :] + jnp.broadcast_to(ayz[:, i : i + 1], (1, 128))
        field[i + 1, 7:8, :] = up.astype(f32)
        down = here[31:32, :] + hy[i : i + 1, :] + jnp.broadcast_to(hyz[:, i : i + 1], (1, 128))
        field[i + 1, 40:41, :] = down.astype(f32) * has_y
    lane = lax.broadcasted_iota(I32, (32, 128), 1)
    copies = []
    for i in range(nx):
        now = field[i + 1, 8:40, :]
        total = field[i, 8:40, :] + field[i + 2, 8:40, :]
        total = total + (field[i + 1, 7:39, :] + field[i + 1, 9:41, :])
        total = total + jnp.where(lane == 0, left[i], pltpu.roll(now, 1, 1))
        total = total + jnp.where(lane == 127, right[i], pltpu.roll(now, 127, 1))
        out[i] = now * half + total * twelfth
        if i % 8 == 7:
            rows = slice(i - 7, i + 1)
            copies.append(pltpu.make_async_copy(out.at[rows], result.at[rows], sems.at[i // 8]))
            copies[-1].start()
    for c in copies:
        c.wait()


def north_kernel(step, pack, full, planes, *rest, **sizes):
    @pl.when(lax.axis_index("gx") % 2 == 1)
    def _():
        stencil(step, pack, full, planes[64:96, :], *rest, **sizes)


def south_kernel(step, pack, full, other, _, *rest, **sizes):
    @pl.when(lax.axis_index("gx") % 2 == 0)
    def _():
        stencil(step, pack, full, other[32:64, :], *rest, **sizes)


def routes(n, ny, nz):
    def route(move):
        pairs = []
        for x in range(n):
            for y in range(ny):
                for z in range(nz):
                    to = move(x, y, z) if x % 2 else (x, y ^ 1, z)
                    pairs.append(((x * ny + y) * nz + z, (to[0] * ny + to[1]) * nz + to[2]))
        return pairs

    across = [route(lambda x, y, z, d=d: (x ^ 2 * d, y, z)) for d in (1, 2, 4)]
    along_y = [route(lambda x, y, z, d=d: (x, (y + d) % ny, z)) for d in (1, 2, 3)]
    along_z = [route(lambda x, y, z, d=d: (x, y, (z + d) % nz)) for d in (1, 2, 3)]
    return across, along_y, along_z


def on_device(quant_codes, error_step):
    n, ny, nz = (lax.axis_size(a) for a in ("gx", "gy", "gz"))
    shape = jax.ShapeDtypeStruct
    vmem = pl.BlockSpec(memory_space=pltpu.VMEM)
    smem = pl.BlockSpec(memory_space=pltpu.SMEM)
    hbm = pl.BlockSpec(memory_space=pltpu.HBM)
    across, along_y, along_z = routes(n, ny, nz)

    def call(kernel, rows, *operands, **options):
        outs = tuple(shape((r, 128), I32) for r in rows)
        return pl.pallas_call(
            kernel, out_shape=outs, compiler_params=params(), name=kernel.__name__, **options
        )(*operands)

    def send(block, route):
        return lax.ppermute(block, ("gx", "gy", "gz"), route)

    def swap(block):
        return lax.ppermute(block, "gx", [(i, i ^ 1) for i in range(n)])

    (mine,) = call(planes_kernel, (64,), quant_codes)
    other = swap(mine)
    full, faces, scale = pl.pallas_call(
        block_kernel,
        in_specs=[smem, vmem],
        out_shape=(
            shape(quant_codes.shape, I32),
            shape((128, 128), I32),
            shape((8, 128), jnp.float32),
        ),
        compiler_params=params(),
        cost_estimate=pl.CostEstimate(flops=4_000_000, bytes_accessed=1_100_000, transcendentals=0),
        name="block",
    )(error_step, quant_codes)
    their_faces = swap(faces)
    (sent,) = call(chip_kernel, (64,), mine, other)
    got = send(sent, across[0])
    sent, state = call(pair_kernel, (64, 64), sent, got)
    got = send(sent, across[1])
    sent, state = call(quad_kernel, (64, 64), sent, got, state)
    got = send(sent, across[2])
    y_up, y_back, z_base, planes = call(
        faces_kernel, (72, 72, 64, 96), got, state, other, faces, their_faces
    )
    got = [send(b, r) for b, r in zip((y_up, y_up, y_back), along_y)]
    rows, z_up, z_back = call(columns_kernel, (144, 40, 40), *got, z_base)
    got = [send(b, r) for b, r in zip((z_up, z_up, z_back), along_z)]
    south, north = call(split_kernel, (176, 176), *got, rows, planes)
    pack = swap(south)
    sizes = dict(n=n, ny=ny, nz=nz)
    options = dict(
        out_specs=hbm,
        out_shape=shape(quant_codes.shape, jnp.float32),
        scratch_shapes=[
            pltpu.VMEM((34, 48, 128), jnp.float32),
            pltpu.VMEM(quant_codes.shape, jnp.float32),
            pltpu.VMEM(quant_codes.shape, jnp.float32),
            pltpu.VMEM(quant_codes.shape, jnp.float32),
            pltpu.SemaphoreType.DMA((4,)),
        ],
        compiler_params=params(),
        cost_estimate=pl.CostEstimate(flops=4_000_000, bytes_accessed=1_100_000, transcendentals=0),
    )
    result = pl.pallas_call(
        functools.partial(north_kernel, **sizes), in_specs=[vmem] * 4, name="north", **options
    )(scale, north, full, planes)
    return pl.pallas_call(
        functools.partial(south_kernel, **sizes),
        in_specs=[vmem] * 4 + [hbm],
        input_output_aliases={4: 0},
        name="south",
        **options,
    )(scale, pack, full, other, result)


def solution(mesh):
    spec = P("gx", "gy", "gz")
    return jax.shard_map(
        on_device, mesh=mesh, in_specs=(spec, P()), out_specs=spec, check_vma=False
    )
```

time: 36.9 us -> 35.1 us (0.951)
  the two profiles are of different devices: /device:TPU:8 before, /device:TPU:1 now
where the time goes in v4:
time: 35.1 us; the launch traced here: 35 us
  starting transfers between devices  17.8 us (51%)
  waiting for transfers between devices  12.6 us (36%)
  Pallas kernels  2.75 us (8%)
  local copies, waits for them, and re-layouts  1.04 us (3%)
  between operations  0.73 us (2%)
    ppermute x9, starting transfers between devices, send(): return lax.ppermute(block, ('gx', 'gy', 'gz'), route)  14.3 us
    ppermute x9, waiting for transfers between devices, send(): return lax.ppermute(block, ('gx', 'gy', 'gz'), route)  11.8 us
    ppermute x3, starting transfers between devices, swap(): return lax.ppermute(block, 'gx', [(i, i ^ 1) for i in range(n)])  3.53 us
    pallas_call x1, Pallas kernels, on_device(): pl.pallas_call(functools.partial(north_kernel, **sizes), in_specs=[vmem]...  1.48 us
    unnamed x4, local copies, waits for them, and re-layouts  1.04 us
    ppermute x3, waiting for transfers between devices, swap(): return lax.ppermute(block, 'gx', [(i, i ^ 1) for i in range(n)])  0.87 us
  transfers between devices with their start and end apart: 12, of which 8 were waited for; matrix products, arithmetic and copies ran while one was open for 0% of the time, Pallas kernels for 6%

profile of v4, /device:TPU:1, one launch (start us, length us, event | category | flops | bytes accessed | tf_op | source)
XLA Modules:
  0.0 35.0 jit_solution(9983687037298150291)
XLA Ops:
  0.0 0.0 copy-start
  0.0 1.0 %copy-done = s32[32,32,128]{2,1,0:T(8,128)S(1)} copy-done((s32[32,32,128]{2,1,0:T(8,128)S(1)}, s32[32,32,128]{2,1,0:T(8,128)}, u32[]{:S(2)}) %copy-start) | copy-done | bytes 524312
  1.0 0.0 copy-start.1
  1.0 0.2 planes_kernel.1.mine
  1.2 3.3 %collective-permute-start = (s32[64,128]{1,0:T(8,128)S(1)}, s32[64,128]{1,0:T(8,128)S(1)}, u32[]{:S(2)}, u32[]{:S(2)}) collective-permute-start(s32[64,128]{1,0:T(8,128)S(1)} %planes_kernel.1.mine), channel_id=1, source_target_pairs={{0,16},{16,0},{32,48},{48,32},{64,80},{80,64},{96,112},{112,96},{1... | collective-permute-start | bytes 98312 | tf_op jit(solution)/shard_map/ppermute | solution.py:272
  4.5 0.9 %collective-permute-done.other = s32[64,128]{1,0:T(8,128)S(1)} collective-permute-done((s32[64,128]{1,0:T(8,128)S(1)}, s32[64,128]{1,0:T(8,128)S(1)}, u32[]{:S(2)}, u32[]{:S(2)}) %collective-permute-start) | collective-permute-done | bytes 32800 | tf_op jit(solution)/shard_map/ppermute | solution.py:272
  5.4 0.0 collective-permute-start.1
  6.0 2.1 %collective-permute-done.1.got = s32[64,128]{1,0:T(8,128)S(1)} collective-permute-done((s32[64,128]{1,0:T(8,128)S(1)}, s32[64,128]{1,0:T(8,128)S(1)}, u32[]{:S(2)}, u32[]{:S(2)}) %collective-permute-start.1) | collective-permute-done | bytes 32800 | tf_op jit(solution)/shard_map/ppermute | solution.py:269
  8.2 1.5 %collective-permute-start.2 = (s32[64,128]{1,0:T(8,128)S(1)}, s32[64,128]{1,0:T(8,128)S(1)}, u32[]{:S(2)}, u32[]{:S(2)}) collective-permute-start(s32[64,128]{1,0:T(8,128)S(1)} %get-tuple-element.22.sent), channel_id=1, source_target_pairs={{0,4},{1,5},{2,6},{3,7},{4,0},{5,1},{6,2},{7,3},{8,12},{9,13},{10,... | collective-permute-start | bytes 98312 | tf_op jit(solution)/shard_map/ppermute | solution.py:269
  9.7 0.0 copy-done.1
  9.7 0.7 %block.1 = (s32[32,32,128]{2,1,0:T(8,128)S(1)}, s32[128,128]{1,0:T(8,128)S(1)}, f32[8,128]{1,0:T(8,128)S(1)}) custom-call(f32[1]{0:T(128)S(6)} %copy.5.step, s32[32,32,128]{2,1,0:T(8,128)S(1)} %copy-done.1), custom_call_target="tpu_custom_call" | custom-call | flops 4000000 | bytes 1100000 | tf_op jit(solution)/shard_map/block/pallas_call | solution.py:276
  10.4 0.1 collective-permute-start.4
  10.5 1.4 %collective-permute-done.2.got = s32[64,128]{1,0:T(8,128)S(1)} collective-permute-done((s32[64,128]{1,0:T(8,128)S(1)}, s32[64,128]{1,0:T(8,128)S(1)}, u32[]{:S(2)}, u32[]{:S(2)}) %collective-permute-start.2) | collective-permute-done | bytes 32800 | tf_op jit(solution)/shard_map/ppermute | solution.py:269
  11.9 5.4 %collective-permute-start.3 = (s32[64,128]{1,0:T(8,128)S(1)}, s32[64,128]{1,0:T(8,128)S(1)}, u32[]{:S(2)}, u32[]{:S(2)}) collective-permute-start(s32[64,128]{1,0:T(8,128)S(1)} %get-tuple-element.24), channel_id=1, source_target_pairs={{0,4},{1,5},{2,6},{3,7},{4,0},{5,1},{6,2},{7,3},{8,12},{9,13},{10,... | collective-permute-start | bytes 98312 | tf_op jit(solution)/shard_map/ppermute | solution.py:269
  17.3 0.0 collective-permute-done.4.theirs
  17.3 1.4 %collective-permute-done.3.got = s32[64,128]{1,0:T(8,128)S(1)} collective-permute-done((s32[64,128]{1,0:T(8,128)S(1)}, s32[64,128]{1,0:T(8,128)S(1)}, u32[]{:S(2)}, u32[]{:S(2)}) %collective-permute-start.3) | collective-permute-done | bytes 32800 | tf_op jit(solution)/shard_map/ppermute | solution.py:269
  18.7 0.1 faces_kernel.1
  18.8 2.4 %collective-permute-start.7 = (s32[72,128]{1,0:T(8,128)S(1)}, s32[72,128]{1,0:T(8,128)S(1)}, u32[]{:S(2)}, u32[]{:S(2)}) collective-permute-start(s32[72,128]{1,0:T(8,128)S(1)} %get-tuple-element.28), channel_id=1, source_target_pairs={{0,4},{1,5},{2,6},{3,7},{4,0},{5,1},{6,2},{7,3},{8,12},{9,13},{10,... | collective-permute-start | bytes 110600 | tf_op jit(solution)/shard_map/ppermute | solution.py:269
  21.2 0.5 %collective-permute-start.6 = (s32[72,128]{1,0:T(8,128)S(1)}, s32[72,128]{1,0:T(8,128)S(1)}, u32[]{:S(2)}, u32[]{:S(2)}) collective-permute-start(s32[72,128]{1,0:T(8,128)S(1)} %get-tuple-element.27), channel_id=1, source_target_pairs={{0,4},{1,5},{2,6},{3,7},{4,0},{5,1},{6,2},{7,3},{8,12},{9,13},{10,... | collective-permute-start | bytes 110600 | tf_op jit(solution)/shard_map/ppermute | solution.py:269
  21.7 0.6 %collective-permute-start.5 = (s32[72,128]{1,0:T(8,128)S(1)}, s32[72,128]{1,0:T(8,128)S(1)}, u32[]{:S(2)}, u32[]{:S(2)}) collective-permute-start(s32[72,128]{1,0:T(8,128)S(1)} %get-tuple-element.27), channel_id=1, source_target_pairs={{0,4},{1,5},{2,6},{3,7},{4,0},{5,1},{6,2},{7,3},{8,12},{9,13},{10,... | collective-permute-start | bytes 110600 | tf_op jit(solution)/shard_map/ppermute | solution.py:269
  22.3 0.0 collective-permute-done.7.got3
  22.3 3.2 %collective-permute-done.6.got2 = s32[72,128]{1,0:T(8,128)S(1)} collective-permute-done((s32[72,128]{1,0:T(8,128)S(1)}, s32[72,128]{1,0:T(8,128)S(1)}, u32[]{:S(2)}, u32[]{:S(2)}) %collective-permute-start.6) | collective-permute-done | bytes 36896 | tf_op jit(solution)/shard_map/ppermute | solution.py:269
  25.5 0.4 %collective-permute-done.5.got1 = s32[72,128]{1,0:T(8,128)S(1)} collective-permute-done((s32[72,128]{1,0:T(8,128)S(1)}, s32[72,128]{1,0:T(8,128)S(1)}, u32[]{:S(2)}, u32[]{:S(2)}) %collective-permute-start.5) | collective-permute-done | bytes 36896 | tf_op jit(solution)/shard_map/ppermute | solution.py:269
  25.9 0.1 columns_kernel.1
  26.0 2.8 %collective-permute-start.10 = (s32[40,128]{1,0:T(8,128)S(1)}, s32[40,128]{1,0:T(8,128)S(1)}, u32[]{:S(2)}, u32[]{:S(2)}) collective-permute-start(s32[40,128]{1,0:T(8,128)S(1)} %get-tuple-element.31), channel_id=1, source_target_pairs={{0,4},{1,5},{2,6},{3,7},{4,0},{5,1},{6,2},{7,3},{8,12},{9,13},{10,... | collective-permute-start | bytes 61448 | tf_op jit(solution)/shard_map/ppermute | solution.py:269
  28.8 0.3 collective-permute-start.9
  29.2 0.7 %collective-permute-start.8 = (s32[40,128]{1,0:T(8,128)S(1)}, s32[40,128]{1,0:T(8,128)S(1)}, u32[]{:S(2)}, u32[]{:S(2)}) collective-permute-start(s32[40,128]{1,0:T(8,128)S(1)} %get-tuple-element.30), channel_id=1, source_target_pairs={{0,4},{1,5},{2,6},{3,7},{4,0},{5,1},{6,2},{7,3},{8,12},{9,13},{10,... | collective-permute-start | bytes 61448 | tf_op jit(solution)/shard_map/ppermute | solution.py:269
  29.9 0.0 collective-permute-done.10.got3
  29.9 3.1 %collective-permute-done.9.got2 = s32[40,128]{1,0:T(8,128)S(1)} collective-permute-done((s32[40,128]{1,0:T(8,128)S(1)}, s32[40,128]{1,0:T(8,128)S(1)}, u32[]{:S(2)}, u32[]{:S(2)}) %collective-permute-start.9) | collective-permute-done | bytes 20512 | tf_op jit(solution)/shard_map/ppermute | solution.py:269
  33.0 0.2 collective-permute-done.8.got1
  33.2 0.1 split_kernel.1
  33.3 0.1 collective-permute-start.11
  33.4 1.5 %north.1._ = f32[32,32,128]{2,1,0:T(8,128)} custom-call(f32[8,128]{1,0:T(8,128)S(1)} %get-tuple-element.21.step, s32[176,128]{1,0:T(8,128)S(1)} %get-tuple-element.36.pack, s32[32,32,128]{2,1,0:T(8,128)S(1)} %get-tuple-element.35.full, s32[96,128]{1,0:T(8,128)S(1)} %get-tuple-element.33.planes), custom_call_target="tpu_custom_call" | custom-call | flops 4000000 | bytes 1100000 | tf_op jit(solution)/shard_map/north/pallas_call | solution.py:317
  34.9 0.0 collective-permute-done.11.pack
  34.9 0.1 south.1
  (3 shorter events, 0.0 us)
Async XLA Ops:
  0.0 1.0 %copy-start = (s32[32,32,128]{2,1,0:T(8,128)S(1)}, s32[32,32,128]{2,1,0:T(8,128)}, u32[]{:S(2)}) copy-start(s32[32,32,128]{2,1,0:T(8,128)} %q.3) | copy-start | bytes 1572868
  1.0 8.7 %copy-start.1 = (s32[32,32,128]{2,1,0:T(8,128)S(1)}, s32[32,32,128]{2,1,0:T(8,128)}, u32[]{:S(2)}) copy-start(s32[32,32,128]{2,1,0:T(8,128)} %q.3) | copy-start | bytes 1572868
  1.2 4.1 %collective-permute-start = (s32[64,128]{1,0:T(8,128)S(1)}, s32[64,128]{1,0:T(8,128)S(1)}, u32[]{:S(2)}, u32[]{:S(2)}) collective-permute-start(s32[64,128]{1,0:T(8,128)S(1)} %planes_kernel.1.mine), channel_id=1, source_target_pairs={{0,16},{16,0},{32,48},{48,32},{64,80},{80,64},{96,112},{112,96},{1... | collective-permute-start | bytes 98312 | tf_op jit(solution)/shard_map/ppermute | solution.py:272
  5.4 2.8 %collective-permute-start.1 = (s32[64,128]{1,0:T(8,128)S(1)}, s32[64,128]{1,0:T(8,128)S(1)}, u32[]{:S(2)}, u32[]{:S(2)}) collective-permute-start(s32[64,128]{1,0:T(8,128)S(1)} %chip_kernel.1.sent), channel_id=1, source_target_pairs={{0,4},{1,5},{2,6},{3,7},{4,0},{5,1},{6,2},{7,3},{8,12},{9,13},{10,... | collective-permute-start | bytes 98312 | tf_op jit(solution)/shard_map/ppermute | solution.py:269
  8.2 3.8 %collective-permute-start.2 = (s32[64,128]{1,0:T(8,128)S(1)}, s32[64,128]{1,0:T(8,128)S(1)}, u32[]{:S(2)}, u32[]{:S(2)}) collective-permute-start(s32[64,128]{1,0:T(8,128)S(1)} %get-tuple-element.22.sent), channel_id=1, source_target_pairs={{0,4},{1,5},{2,6},{3,7},{4,0},{5,1},{6,2},{7,3},{8,12},{9,13},{10,... | collective-permute-start | bytes 98312 | tf_op jit(solution)/shard_map/ppermute | solution.py:269
  10.4 6.9 %collective-permute-start.4 = (s32[128,128]{1,0:T(8,128)S(1)}, s32[128,128]{1,0:T(8,128)S(1)}, u32[]{:S(2)}, u32[]{:S(2)}) collective-permute-start(s32[128,128]{1,0:T(8,128)S(1)} %get-tuple-element.26.mine), channel_id=1, source_target_pairs={{0,16},{16,0},{32,48},{48,32},{64,80},{80,64},{96,112},{112,96},{1... | collective-permute-start | bytes 196616 | tf_op jit(solution)/shard_map/ppermute | solution.py:272
  11.9 6.8 %collective-permute-start.3 = (s32[64,128]{1,0:T(8,128)S(1)}, s32[64,128]{1,0:T(8,128)S(1)}, u32[]{:S(2)}, u32[]{:S(2)}) collective-permute-start(s32[64,128]{1,0:T(8,128)S(1)} %get-tuple-element.24), channel_id=1, source_target_pairs={{0,4},{1,5},{2,6},{3,7},{4,0},{5,1},{6,2},{7,3},{8,12},{9,13},{10,... | collective-permute-start | bytes 98312 | tf_op jit(solution)/shard_map/ppermute | solution.py:269
  18.8 3.5 %collective-permute-start.7 = (s32[72,128]{1,0:T(8,128)S(1)}, s32[72,128]{1,0:T(8,128)S(1)}, u32[]{:S(2)}, u32[]{:S(2)}) collective-permute-start(s32[72,128]{1,0:T(8,128)S(1)} %get-tuple-element.28), channel_id=1, source_target_pairs={{0,4},{1,5},{2,6},{3,7},{4,0},{5,1},{6,2},{7,3},{8,12},{9,13},{10,... | collective-permute-start | bytes 110600 | tf_op jit(solution)/shard_map/ppermute | solution.py:269
  21.2 4.3 %collective-permute-start.6 = (s32[72,128]{1,0:T(8,128)S(1)}, s32[72,128]{1,0:T(8,128)S(1)}, u32[]{:S(2)}, u32[]{:S(2)}) collective-permute-start(s32[72,128]{1,0:T(8,128)S(1)} %get-tuple-element.27), channel_id=1, source_target_pairs={{0,4},{1,5},{2,6},{3,7},{4,0},{5,1},{6,2},{7,3},{8,12},{9,13},{10,... | collective-permute-start | bytes 110600 | tf_op jit(solution)/shard_map/ppermute | solution.py:269
  21.7 4.2 %collective-permute-start.5 = (s32[72,128]{1,0:T(8,128)S(1)}, s32[72,128]{1,0:T(8,128)S(1)}, u32[]{:S(2)}, u32[]{:S(2)}) collective-permute-start(s32[72,128]{1,0:T(8,128)S(1)} %get-tuple-element.27), channel_id=1, source_target_pairs={{0,4},{1,5},{2,6},{3,7},{4,0},{5,1},{6,2},{7,3},{8,12},{9,13},{10,... | collective-permute-start | bytes 110600 | tf_op jit(solution)/shard_map/ppermute | solution.py:269
  26.0 3.9 %collective-permute-start.10 = (s32[40,128]{1,0:T(8,128)S(1)}, s32[40,128]{1,0:T(8,128)S(1)}, u32[]{:S(2)}, u32[]{:S(2)}) collective-permute-start(s32[40,128]{1,0:T(8,128)S(1)} %get-tuple-element.31), channel_id=1, source_target_pairs={{0,4},{1,5},{2,6},{3,7},{4,0},{5,1},{6,2},{7,3},{8,12},{9,13},{10,... | collective-permute-start | bytes 61448 | tf_op jit(solution)/shard_map/ppermute | solution.py:269
  28.8 4.2 %collective-permute-start.9 = (s32[40,128]{1,0:T(8,128)S(1)}, s32[40,128]{1,0:T(8,128)S(1)}, u32[]{:S(2)}, u32[]{:S(2)}) collective-permute-start(s32[40,128]{1,0:T(8,128)S(1)} %get-tuple-element.30), channel_id=1, source_target_pairs={{0,4},{1,5},{2,6},{3,7},{4,0},{5,1},{6,2},{7,3},{8,12},{9,13},{10,... | collective-permute-start | bytes 61448 | tf_op jit(solution)/shard_map/ppermute | solution.py:269
  29.2 4.0 %collective-permute-start.8 = (s32[40,128]{1,0:T(8,128)S(1)}, s32[40,128]{1,0:T(8,128)S(1)}, u32[]{:S(2)}, u32[]{:S(2)}) collective-permute-start(s32[40,128]{1,0:T(8,128)S(1)} %get-tuple-element.30), channel_id=1, source_target_pairs={{0,4},{1,5},{2,6},{3,7},{4,0},{5,1},{6,2},{7,3},{8,12},{9,13},{10,... | collective-permute-start | bytes 61448 | tf_op jit(solution)/shard_map/ppermute | solution.py:269
  33.3 1.6 %collective-permute-start.11 = (s32[176,128]{1,0:T(8,128)S(1)}, s32[176,128]{1,0:T(8,128)S(1)}, u32[]{:S(2)}, u32[]{:S(2)}) collective-permute-start(s32[176,128]{1,0:T(8,128)S(1)} %get-tuple-element.34), channel_id=1, source_target_pairs={{0,16},{16,0},{32,48},{48,32},{64,80},{80,64},{96,112},{112,96},{1... | collective-permute-start | bytes 270344 | tf_op jit(solution)/shard_map/ppermute | solution.py:272

commit v5 on v4

--- a/solution.py
+++ b/solution.py
@@ -6,6 +6,7 @@
 from jax.experimental import pallas as pl
 from jax.experimental.pallas import tpu as pltpu
 from jax.sharding import PartitionSpec as P
+
 
 I32 = jnp.int32
 LIMIT = 16 * 1024 * 1024
@@ -82,7 +83,7 @@
     send[32:64, :] = other[32:64, :]
 
 
-def pair_kernel(sent, got, send, state):
+def pair_kernel(sent, got, _, send, state):
     chip = lax.axis_index("gx") // 2
     odd = chip % 2 == 1
     send[0:32, :] = sent[0:32, :] + got[0:32, :]
@@ -91,15 +92,15 @@
     state[32:64, :] = got[32:64, :]
 
 
-def quad_kernel(sent, got, before, send, state):
+def quad_kernel(sent, got, before, other, send, state):
     chip = lax.axis_index("gx") // 2
     send[0:32, :] = sent[0:32, :] + got[0:32, :]
-    send[32:64, :] = got[32:64, :]
+    send[32:64, :] = other[32:64, :]
     state[0:32, :] = before[0:32, :] + jnp.where(chip % 4 >= 2, got[0:32, :], 0)
     state[32:64, :] = jnp.where(chip % 4 == 1, got[32:64, :], before[32:64, :])
 
 
-def faces_kernel(got, before, other, mine, theirs, y_up, y_back, z_base, planes):
+def faces_kernel(got, before, other, mine, theirs, up, near, mid, z_base, planes):
     chip, y = lax.axis_index("gx") // 2, lax.axis_index("gy")
     lane = lax.broadcasted_iota(I32, (32, 128), 1)
     row = lax.broadcasted_iota(I32, (8, 128), 0)
@@ -111,13 +112,16 @@
     planes[64:96, :] = nxt
     last = d[31:32, :] + mine[31:32, :] + nxt[31:32, :]
     tail = jnp.where(row == 0, c[31:32, :], jnp.where(row == 1, last, 0))
-    south, north = theirs[0:32, :] + c[31:32, :], mine[0:32, :] + d[31:32, :]
-    y_up[0:32, :] = south
-    y_up[32:64, :] = north
-    y_up[64:72, :] = tail
-    y_back[0:32, :] = jnp.where(y == 0, south, theirs[32:64, :] + c[0:1, :])
-    y_back[32:64, :] = jnp.where(y == 0, north, mine[32:64, :] + d[0:1, :])
-    y_back[64:72, :] = tail
+    halves = (theirs, c), (mine, d)
+    for k, (face, plane) in enumerate(halves):
+        rows = slice(32 * k, 32 * k + 32)
+        last_row = face[0:32, :] + plane[31:32, :]
+        first_row = face[32:64, :] + plane[0:1, :]
+        up[rows, :] = last_row
+        near[rows, :] = jnp.where(y % 2 == 1, first_row, last_row)
+        mid[rows, :] = jnp.where(y == 2, first_row, last_row)
+    for ref in (up, near, mid):
+        ref[64:72, :] = tail
     for k, at in ((64, 127), (96, 0)):
         low, high = at_lane(c, at), at_lane(d, at)
         above = high + at_lane(mine[k : k + 32, :], 31) + at_lane(nxt, at)
@@ -128,15 +132,19 @@
 
 
 def lower(index, got1, got2, got3):
-    one = jnp.where(index >= 1, got1[...], 0)
+    one = jnp.where(index % 2 == 1, got1[...], 0)
     two = jnp.where(index >= 2, got2[...], 0)
-    return one + two + jnp.where(index >= 3, got3[...], 0)
-
-
-def columns_kernel(got1, got2, got3, z_base, rows, z_up, z_back):
+    return one + two + jnp.where(index >= 2, got3[...], 0)
+
+
+def beyond(index, got1, got3):
+    return jnp.where(index % 2 == 0, got1[...], got3[...])
+
+
+def columns_kernel(got1, got2, got3, z_base, rows, up, near, mid):
     y, z = lax.axis_index("gy"), lax.axis_index("gz")
     ay = lower(y, got1, got2, got3)
-    hy = jnp.where(y < 3, got3[...], 0)
+    hy = jnp.where(y < 3, beyond(y, got1, got3), 0)
     rows[0:72, :] = ay
     rows[72:144, :] = hy
     pad = jnp.zeros((56, 128), I32)
@@ -145,17 +153,19 @@
     row = lax.broadcasted_iota(I32, (8, 128), 0)
     end = ay_t[127:128, :]
     tail = jnp.where(row == 0, end, jnp.where(row == 1, hy_t[127:128, :], 0))
-    up = z_base[0:32, :] + end
-    z_up[0:32, :] = up
-    z_up[32:40, :] = tail
-    z_back[0:32, :] = jnp.where(z == 0, up, z_base[32:64, :] + ay_t[0:1, :])
-    z_back[32:40, :] = tail
+    last = z_base[0:32, :] + end
+    first = z_base[32:64, :] + ay_t[0:1, :]
+    up[0:32, :] = last
+    near[0:32, :] = jnp.where(z % 2 == 1, first, last)
+    mid[0:32, :] = jnp.where(z == 2, first, last)
+    for ref in (up, near, mid):
+        ref[32:40, :] = tail
 
 
 def split_kernel(got1, got2, got3, rows, planes, south, north):
     z = lax.axis_index("gz")
     az = lower(z, got1, got2, got3)
-    hz = got3[0:32, :]
+    hz = beyond(z, got1, got3)[0:32, :]
     lane = lax.broadcasted_iota(I32, (40, 128), 1)
     row = lax.broadcasted_iota(I32, (8, 128), 0)
 
@@ -245,9 +255,10 @@
                     pairs.append(((x * ny + y) * nz + z, (to[0] * ny + to[1]) * nz + to[2]))
         return pairs
 
-    across = [route(lambda x, y, z, d=d: (x ^ 2 * d, y, z)) for d in (1, 2, 4)]
-    along_y = [route(lambda x, y, z, d=d: (x, (y + d) % ny, z)) for d in (1, 2, 3)]
-    along_z = [route(lambda x, y, z, d=d: (x, y, (z + d) % nz)) for d in (1, 2, 3)]
+    across = [route(lambda x, y, z, d=d: (x ^ d, y, z)) for d in (2, 4)]
+    across.append(route(lambda x, y, z: (n - x, y, z)))
+    along_y = [route(lambda x, y, z, d=d: (x, y ^ d, z)) for d in (1, 2, 3)]
+    along_z = [route(lambda x, y, z, d=d: (x, y, z ^ d)) for d in (1, 2, 3)]
     return across, along_y, along_z
 
 
@@ -262,11 +273,18 @@
     def call(kernel, rows, *operands, **options):
         outs = tuple(shape((r, 128), I32) for r in rows)
         return pl.pallas_call(
-            kernel, out_shape=outs, compiler_params=params(), name=kernel.__name__, **options
+            kernel, out_shape=outs, compiler_params=params(), **options
         )(*operands)
 
     def send(block, route):
         return lax.ppermute(block, ("gx", "gy", "gz"), route)
+
+    def exchange(blocks, routes):
+        up, near, mid = blocks
+        got = []
+        for block, route in zip((near, up, mid), routes):
+            got.append(send(block, route))
+        return got
 
     def swap(block):
         return lax.ppermute(block, "gx", [(i, i ^ 1) for i in range(n)])
@@ -285,19 +303,19 @@
         cost_estimate=pl.CostEstimate(flops=4_000_000, bytes_accessed=1_100_000, transcendentals=0),
         name="block",
     )(error_step, quant_codes)
-    their_faces = swap(faces)
     (sent,) = call(chip_kernel, (64,), mine, other)
     got = send(sent, across[0])
-    sent, state = call(pair_kernel, (64, 64), sent, got)
+    sent, state = call(pair_kernel, (64, 64), sent, got, scale)
     got = send(sent, across[1])
-    sent, state = call(quad_kernel, (64, 64), sent, got, state)
+    sent, state = call(quad_kernel, (64, 64), sent, got, state, other)
+    their_faces = swap(faces)
     got = send(sent, across[2])
-    y_up, y_back, z_base, planes = call(
-        faces_kernel, (72, 72, 64, 96), got, state, other, faces, their_faces
+    *sent, z_base, planes = call(
+        faces_kernel, (72, 72, 72, 64, 96), got, state, other, faces, their_faces
     )
-    got = [send(b, r) for b, r in zip((y_up, y_up, y_back), along_y)]
-    rows, z_up, z_back = call(columns_kernel, (144, 40, 40), *got, z_base)
-    got = [send(b, r) for b, r in zip((z_up, z_up, z_back), along_z)]
+    got = exchange(sent, along_y)
+    rows, *sent = call(columns_kernel, (144, 40, 40, 40), *got, z_base)
+    got = exchange(sent, along_z)
     south, north = call(split_kernel, (176, 176), *got, rows, planes)
     pack = swap(south)
     sizes = dict(n=n, ny=ny, nz=nz)

time: 35.1 us -> 34.9 us (level)
  starting transfers between devices: 17.8 us -> 17 us
  waiting for transfers between devices: 12.6 us -> 13.3 us
    ppermute x9, starting transfers between devices: 14.3 us -> 13.5 us  [send(): return lax.ppermute(block, ('gx', 'gy', 'gz'), route)]
    ppermute x9, waiting for transfers between devices: 11.8 us -> 12.4 us  [send(): return lax.ppermute(block, ('gx', 'gy', 'gz'), route)]
where the time goes in v5:
time: 34.9 us; the launch traced here: 34.8 us
  starting transfers between devices  17 us (49%)
  waiting for transfers between devices  13.3 us (38%)
  Pallas kernels  2.75 us (8%)
  local copies, waits for them, and re-layouts  1.04 us (3%)
  between operations  0.74 us (2%)
    ppermute x9, starting transfers between devices, send(): return lax.ppermute(block, ('gx', 'gy', 'gz'), route)  13.5 us
    ppermute x9, waiting for transfers between devices, send(): return lax.ppermute(block, ('gx', 'gy', 'gz'), route)  12.4 us
    ppermute x3, starting transfers between devices, swap(): return lax.ppermute(block, 'gx', [(i, i ^ 1) for i in range(n)])  3.44 us
    pallas_call x1, Pallas kernels, on_device(): pl.pallas_call(functools.partial(north_kernel, **sizes), in_specs=[vmem]...  1.48 us
    unnamed x4, local copies, waits for them, and re-layouts  1.04 us
    ppermute x3, waiting for transfers between devices, swap(): return lax.ppermute(block, 'gx', [(i, i ^ 1) for i in range(n)])  0.87 us
  transfers between devices with their start and end apart: 12, of which 8 were waited for; matrix products, arithmetic and copies ran while one was open for 0% of the time, Pallas kernels for 6%

profile of v5, /device:TPU:1, one launch (start us, length us, event | category | flops | bytes accessed | tf_op | source)
XLA Modules:
  0.0 34.8 jit_solution(12294651748607786994)
XLA Ops:
  0.0 0.0 copy-start
  0.0 1.0 %copy-done = s32[32,32,128]{2,1,0:T(8,128)S(1)} copy-done((s32[32,32,128]{2,1,0:T(8,128)S(1)}, s32[32,32,128]{2,1,0:T(8,128)}, u32[]{:S(2)}) %copy-start) | copy-done | bytes 524312
  1.0 0.0 copy-start.1
  1.0 0.2 shard_map.28.mine
  1.2 3.3 %collective-permute-start = (s32[64,128]{1,0:T(8,128)S(1)}, s32[64,128]{1,0:T(8,128)S(1)}, u32[]{:S(2)}, u32[]{:S(2)}) collective-permute-start(s32[64,128]{1,0:T(8,128)S(1)} %shard_map.28.mine), channel_id=1, source_target_pairs={{0,16},{16,0},{32,48},{48,32},{64,80},{80,64},{96,112},{112,96},{1... | collective-permute-start | bytes 98312 | tf_op jit(solution)/shard_map/ppermute | solution.py:290
  4.5 0.9 %collective-permute-done.other = s32[64,128]{1,0:T(8,128)S(1)} collective-permute-done((s32[64,128]{1,0:T(8,128)S(1)}, s32[64,128]{1,0:T(8,128)S(1)}, u32[]{:S(2)}, u32[]{:S(2)}) %collective-permute-start) | collective-permute-done | bytes 32800 | tf_op jit(solution)/shard_map/ppermute | solution.py:290
  5.4 0.0 collective-permute-start.1
  6.0 0.0 copy-done.1
  6.0 0.7 %block.1 = (s32[32,32,128]{2,1,0:T(8,128)S(1)}, s32[128,128]{1,0:T(8,128)S(1)}, f32[8,128]{1,0:T(8,128)S(1)}) custom-call(f32[1]{0:T(128)S(6)} %copy.5.step, s32[32,32,128]{2,1,0:T(8,128)S(1)} %copy-done.1), custom_call_target="tpu_custom_call" | custom-call | flops 4000000 | bytes 1100000 | tf_op jit(solution)/shard_map/block/pallas_call | solution.py:294
  6.7 1.4 %collective-permute-done.1.got = s32[64,128]{1,0:T(8,128)S(1)} collective-permute-done((s32[64,128]{1,0:T(8,128)S(1)}, s32[64,128]{1,0:T(8,128)S(1)}, u32[]{:S(2)}, u32[]{:S(2)}) %collective-permute-start.1) | collective-permute-done | bytes 32800 | tf_op jit(solution)/shard_map/ppermute | solution.py:280
  8.2 1.6 %collective-permute-start.2 = (s32[64,128]{1,0:T(8,128)S(1)}, s32[64,128]{1,0:T(8,128)S(1)}, u32[]{:S(2)}, u32[]{:S(2)}) collective-permute-start(s32[64,128]{1,0:T(8,128)S(1)} %get-tuple-element.24.sent), channel_id=1, source_target_pairs={{0,4},{1,5},{2,6},{3,7},{4,0},{5,1},{6,2},{7,3},{8,12},{9,13},{10,... | collective-permute-start | bytes 98312 | tf_op jit(solution)/shard_map/ppermute | solution.py:280
  9.8 0.1 collective-permute-start.4
  9.8 2.1 %collective-permute-done.2.got = s32[64,128]{1,0:T(8,128)S(1)} collective-permute-done((s32[64,128]{1,0:T(8,128)S(1)}, s32[64,128]{1,0:T(8,128)S(1)}, u32[]{:S(2)}, u32[]{:S(2)}) %collective-permute-start.2) | collective-permute-done | bytes 32800 | tf_op jit(solution)/shard_map/ppermute | solution.py:280
  11.9 3.9 %collective-permute-start.3 = (s32[64,128]{1,0:T(8,128)S(1)}, s32[64,128]{1,0:T(8,128)S(1)}, u32[]{:S(2)}, u32[]{:S(2)}) collective-permute-start(s32[64,128]{1,0:T(8,128)S(1)} %get-tuple-element.26), channel_id=1, source_target_pairs={{0,4},{1,5},{2,6},{3,7},{4,0},{5,1},{6,2},{7,3},{8,12},{9,13},{10,... | collective-permute-start | bytes 98312 | tf_op jit(solution)/shard_map/ppermute | solution.py:280
  15.9 0.0 collective-permute-done.4.theirs
  15.9 1.3 %collective-permute-done.3.got = s32[64,128]{1,0:T(8,128)S(1)} collective-permute-done((s32[64,128]{1,0:T(8,128)S(1)}, s32[64,128]{1,0:T(8,128)S(1)}, u32[]{:S(2)}, u32[]{:S(2)}) %collective-permute-start.3) | collective-permute-done | bytes 32800 | tf_op jit(solution)/shard_map/ppermute | solution.py:280
  17.2 0.1 shard_map.32
  17.3 1.3 %collective-permute-start.5 = (s32[72,128]{1,0:T(8,128)S(1)}, s32[72,128]{1,0:T(8,128)S(1)}, u32[]{:S(2)}, u32[]{:S(2)}) collective-permute-start(s32[72,128]{1,0:T(8,128)S(1)} %get-tuple-element.29), channel_id=1, source_target_pairs={{0,4},{1,5},{2,6},{3,7},{4,0},{5,1},{6,2},{7,3},{8,12},{9,13},{10,... | collective-permute-start | bytes 110600 | tf_op jit(solution)/shard_map/ppermute | solution.py:280
  18.6 2.4 %collective-permute-start.6 = (s32[72,128]{1,0:T(8,128)S(1)}, s32[72,128]{1,0:T(8,128)S(1)}, u32[]{:S(2)}, u32[]{:S(2)}) collective-permute-start(s32[72,128]{1,0:T(8,128)S(1)} %get-tuple-element.30), channel_id=1, source_target_pairs={{0,4},{1,5},{2,6},{3,7},{4,0},{5,1},{6,2},{7,3},{8,12},{9,13},{10,... | collective-permute-start | bytes 110600 | tf_op jit(solution)/shard_map/ppermute | solution.py:280
  21.1 0.2 collective-permute-start.7
  21.3 0.0 collective-permute-done.5.got1
  21.3 1.9 %collective-permute-done.6.got2 = s32[72,128]{1,0:T(8,128)S(1)} collective-permute-done((s32[72,128]{1,0:T(8,128)S(1)}, s32[72,128]{1,0:T(8,128)S(1)}, u32[]{:S(2)}, u32[]{:S(2)}) %collective-permute-start.6) | collective-permute-done | bytes 36896 | tf_op jit(solution)/shard_map/ppermute | solution.py:280
  23.2 1.9 %collective-permute-done.7.got3 = s32[72,128]{1,0:T(8,128)S(1)} collective-permute-done((s32[72,128]{1,0:T(8,128)S(1)}, s32[72,128]{1,0:T(8,128)S(1)}, u32[]{:S(2)}, u32[]{:S(2)}) %collective-permute-start.7) | collective-permute-done | bytes 36896 | tf_op jit(solution)/shard_map/ppermute | solution.py:280
  25.1 0.1 shard_map.33
  25.2 1.4 %collective-permute-start.8 = (s32[40,128]{1,0:T(8,128)S(1)}, s32[40,128]{1,0:T(8,128)S(1)}, u32[]{:S(2)}, u32[]{:S(2)}) collective-permute-start(s32[40,128]{1,0:T(8,128)S(1)} %get-tuple-element.33), channel_id=1, source_target_pairs={{0,4},{1,5},{2,6},{3,7},{4,0},{5,1},{6,2},{7,3},{8,12},{9,13},{10,... | collective-permute-start | bytes 61448 | tf_op jit(solution)/shard_map/ppermute | solution.py:280
  26.6 2.6 %collective-permute-start.9 = (s32[40,128]{1,0:T(8,128)S(1)}, s32[40,128]{1,0:T(8,128)S(1)}, u32[]{:S(2)}, u32[]{:S(2)}) collective-permute-start(s32[40,128]{1,0:T(8,128)S(1)} %get-tuple-element.34), channel_id=1, source_target_pairs={{0,4},{1,5},{2,6},{3,7},{4,0},{5,1},{6,2},{7,3},{8,12},{9,13},{10,... | collective-permute-start | bytes 61448 | tf_op jit(solution)/shard_map/ppermute | solution.py:280
  29.2 0.0 collective-permute-start.10
  29.2 0.0 collective-permute-done.8.got1
  29.2 1.5 %collective-permute-done.9.got2 = s32[40,128]{1,0:T(8,128)S(1)} collective-permute-done((s32[40,128]{1,0:T(8,128)S(1)}, s32[40,128]{1,0:T(8,128)S(1)}, u32[]{:S(2)}, u32[]{:S(2)}) %collective-permute-start.9) | collective-permute-done | bytes 20512 | tf_op jit(solution)/shard_map/ppermute | solution.py:280
  30.7 2.3 %collective-permute-done.10.got3 = s32[40,128]{1,0:T(8,128)S(1)} collective-permute-done((s32[40,128]{1,0:T(8,128)S(1)}, s32[40,128]{1,0:T(8,128)S(1)}, u32[]{:S(2)}, u32[]{:S(2)}) %collective-permute-start.10) | collective-permute-done | bytes 20512 | tf_op jit(solution)/shard_map/ppermute | solution.py:280
  33.0 0.1 shard_map.34
  33.1 0.1 collective-permute-start.11
  33.2 1.5 %north.1._ = f32[32,32,128]{2,1,0:T(8,128)} custom-call(f32[8,128]{1,0:T(8,128)S(1)} %get-tuple-element.23._.step, s32[176,128]{1,0:T(8,128)S(1)} %get-tuple-element.40.pack, s32[32,32,128]{2,1,0:T(8,128)S(1)} %get-tuple-element.39.full, s32[96,128]{1,0:T(8,128)S(1)} %get-tuple-element.37.planes), custom_call_target="tpu_custom_call" | custom-call | flops 4000000 | bytes 1100000 | tf_op jit(solution)/shard_map/north/pallas_call | solution.py:335
  34.7 0.0 collective-permute-done.11.pack
  34.8 0.1 south.1
  (3 shorter events, 0.0 us)
Async XLA Ops:
  0.0 1.0 %copy-start = (s32[32,32,128]{2,1,0:T(8,128)S(1)}, s32[32,32,128]{2,1,0:T(8,128)}, u32[]{:S(2)}) copy-start(s32[32,32,128]{2,1,0:T(8,128)} %q.3) | copy-start | bytes 1572868
  1.0 5.0 %copy-start.1 = (s32[32,32,128]{2,1,0:T(8,128)S(1)}, s32[32,32,128]{2,1,0:T(8,128)}, u32[]{:S(2)}) copy-start(s32[32,32,128]{2,1,0:T(8,128)} %q.3) | copy-start | bytes 1572868
  1.2 4.1 %collective-permute-start = (s32[64,128]{1,0:T(8,128)S(1)}, s32[64,128]{1,0:T(8,128)S(1)}, u32[]{:S(2)}, u32[]{:S(2)}) collective-permute-start(s32[64,128]{1,0:T(8,128)S(1)} %shard_map.28.mine), channel_id=1, source_target_pairs={{0,16},{16,0},{32,48},{48,32},{64,80},{80,64},{96,112},{112,96},{1... | collective-permute-start | bytes 98312 | tf_op jit(solution)/shard_map/ppermute | solution.py:290
  5.4 2.8 %collective-permute-start.1 = (s32[64,128]{1,0:T(8,128)S(1)}, s32[64,128]{1,0:T(8,128)S(1)}, u32[]{:S(2)}, u32[]{:S(2)}) collective-permute-start(s32[64,128]{1,0:T(8,128)S(1)} %shard_map.29.sent), channel_id=1, source_target_pairs={{0,4},{1,5},{2,6},{3,7},{4,0},{5,1},{6,2},{7,3},{8,12},{9,13},{10,... | collective-permute-start | bytes 98312 | tf_op jit(solution)/shard_map/ppermute | solution.py:280
  8.2 3.8 %collective-permute-start.2 = (s32[64,128]{1,0:T(8,128)S(1)}, s32[64,128]{1,0:T(8,128)S(1)}, u32[]{:S(2)}, u32[]{:S(2)}) collective-permute-start(s32[64,128]{1,0:T(8,128)S(1)} %get-tuple-element.24.sent), channel_id=1, source_target_pairs={{0,4},{1,5},{2,6},{3,7},{4,0},{5,1},{6,2},{7,3},{8,12},{9,13},{10,... | collective-permute-start | bytes 98312 | tf_op jit(solution)/shard_map/ppermute | solution.py:280
  9.8 6.1 %collective-permute-start.4 = (s32[128,128]{1,0:T(8,128)S(1)}, s32[128,128]{1,0:T(8,128)S(1)}, u32[]{:S(2)}, u32[]{:S(2)}) collective-permute-start(s32[128,128]{1,0:T(8,128)S(1)} %get-tuple-element.28.mine), channel_id=1, source_target_pairs={{0,16},{16,0},{32,48},{48,32},{64,80},{80,64},{96,112},{112,96},{1... | collective-permute-start | bytes 196616 | tf_op jit(solution)/shard_map/ppermute | solution.py:290
  11.9 5.2 %collective-permute-start.3 = (s32[64,128]{1,0:T(8,128)S(1)}, s32[64,128]{1,0:T(8,128)S(1)}, u32[]{:S(2)}, u32[]{:S(2)}) collective-permute-start(s32[64,128]{1,0:T(8,128)S(1)} %get-tuple-element.26), channel_id=1, source_target_pairs={{0,4},{1,5},{2,6},{3,7},{4,0},{5,1},{6,2},{7,3},{8,12},{9,13},{10,... | collective-permute-start | bytes 98312 | tf_op jit(solution)/shard_map/ppermute | solution.py:280
  17.3 3.9 %collective-permute-start.5 = (s32[72,128]{1,0:T(8,128)S(1)}, s32[72,128]{1,0:T(8,128)S(1)}, u32[]{:S(2)}, u32[]{:S(2)}) collective-permute-start(s32[72,128]{1,0:T(8,128)S(1)} %get-tuple-element.29), channel_id=1, source_target_pairs={{0,4},{1,5},{2,6},{3,7},{4,0},{5,1},{6,2},{7,3},{8,12},{9,13},{10,... | collective-permute-start | bytes 110600 | tf_op jit(solution)/shard_map/ppermute | solution.py:280
  18.6 4.6 %collective-permute-start.6 = (s32[72,128]{1,0:T(8,128)S(1)}, s32[72,128]{1,0:T(8,128)S(1)}, u32[]{:S(2)}, u32[]{:S(2)}) collective-permute-start(s32[72,128]{1,0:T(8,128)S(1)} %get-tuple-element.30), channel_id=1, source_target_pairs={{0,4},{1,5},{2,6},{3,7},{4,0},{5,1},{6,2},{7,3},{8,12},{9,13},{10,... | collective-permute-start | bytes 110600 | tf_op jit(solution)/shard_map/ppermute | solution.py:280
  21.1 4.0 %collective-permute-start.7 = (s32[72,128]{1,0:T(8,128)S(1)}, s32[72,128]{1,0:T(8,128)S(1)}, u32[]{:S(2)}, u32[]{:S(2)}) collective-permute-start(s32[72,128]{1,0:T(8,128)S(1)} %get-tuple-element.31), channel_id=1, source_target_pairs={{0,4},{1,5},{2,6},{3,7},{4,0},{5,1},{6,2},{7,3},{8,12},{9,13},{10,... | collective-permute-start | bytes 110600 | tf_op jit(solution)/shard_map/ppermute | solution.py:280
  25.2 4.0 %collective-permute-start.8 = (s32[40,128]{1,0:T(8,128)S(1)}, s32[40,128]{1,0:T(8,128)S(1)}, u32[]{:S(2)}, u32[]{:S(2)}) collective-permute-start(s32[40,128]{1,0:T(8,128)S(1)} %get-tuple-element.33), channel_id=1, source_target_pairs={{0,4},{1,5},{2,6},{3,7},{4,0},{5,1},{6,2},{7,3},{8,12},{9,13},{10,... | collective-permute-start | bytes 61448 | tf_op jit(solution)/shard_map/ppermute | solution.py:280
  26.6 4.1 %collective-permute-start.9 = (s32[40,128]{1,0:T(8,128)S(1)}, s32[40,128]{1,0:T(8,128)S(1)}, u32[]{:S(2)}, u32[]{:S(2)}) collective-permute-start(s32[40,128]{1,0:T(8,128)S(1)} %get-tuple-element.34), channel_id=1, source_target_pairs={{0,4},{1,5},{2,6},{3,7},{4,0},{5,1},{6,2},{7,3},{8,12},{9,13},{10,... | collective-permute-start | bytes 61448 | tf_op jit(solution)/shard_map/ppermute | solution.py:280
  29.2 3.8 %collective-permute-start.10 = (s32[40,128]{1,0:T(8,128)S(1)}, s32[40,128]{1,0:T(8,128)S(1)}, u32[]{:S(2)}, u32[]{:S(2)}) collective-permute-start(s32[40,128]{1,0:T(8,128)S(1)} %get-tuple-element.35), channel_id=1, source_target_pairs={{0,4},{1,5},{2,6},{3,7},{4,0},{5,1},{6,2},{7,3},{8,12},{9,13},{10,... | collective-permute-start | bytes 61448 | tf_op jit(solution)/shard_map/ppermute | solution.py:280
  33.1 1.6 %collective-permute-start.11 = (s32[176,128]{1,0:T(8,128)S(1)}, s32[176,128]{1,0:T(8,128)S(1)}, u32[]{:S(2)}, u32[]{:S(2)}) collective-permute-start(s32[176,128]{1,0:T(8,128)S(1)} %get-tuple-element.38), channel_id=1, source_target_pairs={{0,16},{16,0},{32,48},{48,32},{64,80},{80,64},{96,112},{112,96},{1... | collective-permute-start | bytes 270344 | tf_op jit(solution)/shard_map/ppermute | solution.py:290

commit v6 on v5

--- a/solution.py
+++ b/solution.py
@@ -92,7 +92,7 @@
     state[32:64, :] = got[32:64, :]
 
 
-def quad_kernel(sent, got, before, other, send, state):
+def quad_kernel(sent, got, before, other, _, send, state):
     chip = lax.axis_index("gx") // 2
     send[0:32, :] = sent[0:32, :] + got[0:32, :]
     send[32:64, :] = other[32:64, :]
@@ -187,78 +187,114 @@
     north[144:176, :] = planes[32:64, :]
 
 
-def stencil(step, pack, full, high, result, field, left, right, out, sems, *, n, ny, nz):
-    x, y, z = lax.axis_index("gx"), lax.axis_index("gy"), lax.axis_index("gz")
-    f32 = jnp.float32
+def inner_kernel(full, _, inner, field, *, ny, nz):
+    has_y = lax.axis_index("gy") < ny - 1
+    has_z = lax.axis_index("gz") < nz - 1
     nx = full.shape[0]
-    ay, az, hz, hy = pack[0:40, :], pack[40:72, :], pack[80:112, :], pack[112:144, :]
-    ayz, hyz, c = pack[72:73, :], pack[73:74, :], pack[144:176, :]
-    has_x = (x < n - 1).astype(f32)
-    has_y = (y < ny - 1).astype(f32)
-    has_z = (z < nz - 1).astype(f32)
-    half = jnp.broadcast_to(step[0:1, :], (32, 128)) * 0.5
-    twelfth = jnp.broadcast_to(step[0:1, :], (32, 128)) * (1.0 / 12.0)
-    for i in range(-1, nx + 1):
-        k = nx if i < 0 else nx + 1 if i == nx else i
-        edge = at_lane(az, k)
-        here = c + edge + ay[k : k + 1, :]
-        if i >= 0:
-            here = here + full[min(i, nx - 1)]
-        if i == nx:
-            field[i + 1, 8:40, :] = (here + high).astype(f32) * has_x
-            continue
-        field[i + 1, 8:40, :] = here.astype(f32)
-        if i < 0:
-            continue
-        left[i] = edge.astype(f32)
-        right[i] = (here + at_lane(hz, i)).astype(f32) * has_z
-        up = ay[i : i + 1, :] + jnp.broadcast_to(ayz[:, i : i + 1], (1, 128))
-        field[i + 1, 7:8, :] = up.astype(f32)
-        down = here[31:32, :] + hy[i : i + 1, :] + jnp.broadcast_to(hyz[:, i : i + 1], (1, 128))
-        field[i + 1, 40:41, :] = down.astype(f32) * has_y
     lane = lax.broadcasted_iota(I32, (32, 128), 1)
+    for i in range(nx):
+        field[i, 8:40, :] = full[i]
+        field[i, 7:8, :] = jnp.zeros((1, 128), I32)
+        field[i, 40:41, :] = jnp.where(has_y, full[i, 31:32, :], 0)
+    for i in range(nx):
+        now = full[i]
+        total = 6 * now + (field[i, 7:39, :] + field[i, 9:41, :])
+        if i > 0:
+            total = total + full[i - 1]
+        if i < nx - 1:
+            total = total + full[i + 1]
+        total = total + jnp.where(lane == 0, 0, pltpu.roll(now, 1, 1))
+        beyond_z = jnp.where(has_z, now, 0)
+        inner[i] = total + jnp.where(lane == 127, beyond_z, pltpu.roll(now, 127, 1))
+
+
+def stencil(step, pack, inner, full, high, result, out, sems, *, n, ny, nz):
+    has_x = lax.axis_index("gx") < n - 1
+    has_y = lax.axis_index("gy") < ny - 1
+    has_z = lax.axis_index("gz") < nz - 1
+    nx = full.shape[0]
+    lane = lax.broadcasted_iota(I32, (32, 128), 1)
+    row = lax.broadcasted_iota(I32, (32, 128), 0)
+    ay, az, hz, hy = pack[0:32, :], pack[40:72, :], pack[80:112, :], pack[112:144, :]
+    hyz, low = pack[73:74, :], pack[144:176, :]
+
+    def beside(v, before, after, axis, last):
+        at = lane if axis else row
+        down = jnp.where(at == 0, before, pltpu.roll(v, 1, axis))
+        return down + jnp.where(at == last, after, pltpu.roll(v, (-1) % v.shape[axis], axis))
+
+    def held(flag, v):
+        return jnp.where(flag, v, 0)
+
+    rows = 8 * ay + beside(ay, pack[32:33, :], held(has_x, pack[33:34, :]), 0, 31)
+    rows = rows + beside(ay, 0, held(has_z, ay), 1, 127)
+    cols = 8 * az + beside(az, at_lane(az, 32), held(has_x, at_lane(az, 33)), 1, 31)
+    cols = cols + beside(az, pack[72:73, :], held(has_y, az), 0, 31)
+    both = 8 * low + beside(low, 0, held(has_y, low), 0, 31)
+    both = both + beside(low, 0, held(has_z, low), 1, 127)
+    end_y = jnp.where(has_y, hy, -ay)
+    hyz = held(has_y, hyz)
+    end_z = jnp.where(has_z, hz, -az)
+    scale = jnp.broadcast_to(step[0:1, :], (32, 128)) * (1.0 / 12.0)
     copies = []
     for i in range(nx):
-        now = field[i + 1, 8:40, :]
-        total = field[i, 8:40, :] + field[i + 2, 8:40, :]
-        total = total + (field[i + 1, 7:39, :] + field[i + 1, 9:41, :])
-        total = total + jnp.where(lane == 0, left[i], pltpu.roll(now, 1, 1))
-        total = total + jnp.where(lane == 127, right[i], pltpu.roll(now, 127, 1))
-        out[i] = now * half + total * twelfth
+        total = inner[i] + (both + rows[i : i + 1, :]) + at_lane(cols, i)
+        total = total + jnp.where(lane == 127, at_lane(end_z, i), 0)
+        edge = end_y[i : i + 1, :] + jnp.broadcast_to(hyz[:, i : i + 1], (1, 128))
+        total = total + jnp.where(row == 31, edge, 0)
+        if i == nx - 1:
+            total = total + jnp.where(has_x, full[i] + high, -low)
+        out[i] = total.astype(jnp.float32) * scale
         if i % 8 == 7:
-            rows = slice(i - 7, i + 1)
-            copies.append(pltpu.make_async_copy(out.at[rows], result.at[rows], sems.at[i // 8]))
+            part = slice(i - 7, i + 1)
+            copies.append(pltpu.make_async_copy(out.at[part], result.at[part], sems.at[i // 8]))
             copies[-1].start()
     for c in copies:
         c.wait()
 
 
-def north_kernel(step, pack, full, planes, *rest, **sizes):
+def north_kernel(step, pack, inner, full, planes, *rest, **sizes):
     @pl.when(lax.axis_index("gx") % 2 == 1)
     def _():
-        stencil(step, pack, full, planes[64:96, :], *rest, **sizes)
-
-
-def south_kernel(step, pack, full, other, _, *rest, **sizes):
+        stencil(step, pack, inner, full, planes[64:96, :], *rest, **sizes)
+
+
+def south_kernel(step, pack, inner, full, other, _, *rest, **sizes):
     @pl.when(lax.axis_index("gx") % 2 == 0)
     def _():
-        stencil(step, pack, full, other[32:64, :], *rest, **sizes)
+        stencil(step, pack, inner, full, other[32:64, :], *rest, **sizes)
 
 
 def routes(n, ny, nz):
-    def route(move):
+    def route(move, south=lambda x, y, z: (x, y ^ 1, z)):
         pairs = []
         for x in range(n):
             for y in range(ny):
                 for z in range(nz):
-                    to = move(x, y, z) if x % 2 else (x, y ^ 1, z)
+                    to = (move if x % 2 else south)(x, y, z)
                     pairs.append(((x * ny + y) * nz + z, (to[0] * ny + to[1]) * nz + to[2]))
         return pairs
 
     across = [route(lambda x, y, z, d=d: (x ^ d, y, z)) for d in (2, 4)]
     across.append(route(lambda x, y, z: (n - x, y, z)))
-    along_y = [route(lambda x, y, z, d=d: (x, y ^ d, z)) for d in (1, 2, 3)]
-    along_z = [route(lambda x, y, z, d=d: (x, y, z ^ d)) for d in (1, 2, 3)]
+    along_y = [route(lambda x, y, z, d=d: (x, y ^ d, z)) for d in (1, 2)]
+    along_z = [route(lambda x, y, z, d=d: (x, y, z ^ d)) for d in (1, 2)]
+
+    def far(x, at, size):
+        if x % 2:
+            return (x, size - 1 - at) if at < size - 1 else (x - 1, at)
+        return (x, at - 1) if at else (x + 1, at)
+
+    def far_y(x, y, z):
+        x, y = far(x, y, ny)
+        return x, y, z
+
+    def far_z(x, y, z):
+        x, z = far(x, z, nz)
+        return x, y, z
+
+    along_y.append(route(far_y, far_y))
+    along_z.append(route(far_z, far_z))
     return across, along_y, along_z
 
 
@@ -307,7 +343,15 @@
     got = send(sent, across[0])
     sent, state = call(pair_kernel, (64, 64), sent, got, scale)
     got = send(sent, across[1])
-    sent, state = call(quad_kernel, (64, 64), sent, got, state, other)
+    inner = pl.pallas_call(
+        functools.partial(inner_kernel, ny=ny, nz=nz),
+        out_shape=shape(quant_codes.shape, I32),
+        scratch_shapes=[pltpu.VMEM((32, 48, 128), I32)],
+        compiler_params=params(),
+        cost_estimate=pl.CostEstimate(flops=4_000_000, bytes_accessed=1_100_000, transcendentals=0),
+        name="inner",
+    )(full, state)
+    sent, state = call(quad_kernel, (64, 64), sent, got, state, other, inner)
     their_faces = swap(faces)
     got = send(sent, across[2])
     *sent, z_base, planes = call(
@@ -323,9 +367,6 @@
         out_specs=hbm,
         out_shape=shape(quant_codes.shape, jnp.float32),
         scratch_shapes=[
-            pltpu.VMEM((34, 48, 128), jnp.float32),
-            pltpu.VMEM(quant_codes.shape, jnp.float32),
-            pltpu.VMEM(quant_codes.shape, jnp.float32),
             pltpu.VMEM(quant_codes.shape, jnp.float32),
             pltpu.SemaphoreType.DMA((4,)),
         ],
@@ -333,15 +374,15 @@
         cost_estimate=pl.CostEstimate(flops=4_000_000, bytes_accessed=1_100_000, transcendentals=0),
     )
     result = pl.pallas_call(
-        functools.partial(north_kernel, **sizes), in_specs=[vmem] * 4, name="north", **options
-    )(scale, north, full, planes)
+        functools.partial(north_kernel, **sizes), in_specs=[vmem] * 5, name="north", **options
+    )(scale, north, inner, full, planes)
     return pl.pallas_call(
         functools.partial(south_kernel, **sizes),
-        in_specs=[vmem] * 4 + [hbm],
-        input_output_aliases={4: 0},
+        in_specs=[vmem] * 5 + [hbm],
+        input_output_aliases={5: 0},
         name="south",
         **options,
-    )(scale, pack, full, other, result)
+    )(scale, pack, inner, full, other, result)
 
 
 def solution(mesh):

time: 34.9 us -> 31.5 us (0.903)
  waiting for transfers between devices: 13.3 us -> 8.7 us
  starting transfers between devices: 17 us -> 18 us
    ppermute x9, waiting for transfers between devices: 12.4 us -> 7.83 us  [send(): return lax.ppermute(block, ('gx', 'gy', 'gz'), route)]
    ppermute x3, starting transfers between devices: 3.44 us -> 4.48 us  [swap(): return lax.ppermute(block, 'gx', [(i, i ^ 1) for i in range(n)])]
    pallas_call x0 -> x1, Pallas kernels: none -> 0.4 us  [on_device(): pl.pallas_call(functools.partial(inner_kernel, ny=ny, nz=nz), out_shape=s...]
  transfers between devices with their start and end apart: 12 -> 12, of which waited for: 8 -> 6; matrix products, arithmetic and copies ran while one was open for 0% -> 0% of each run, Pallas kernels for 6% -> 7%
where the time goes in v6:
time: 31.5 us; the launch traced here: 31.3 us
  starting transfers between devices  18 us (57%)
  waiting for transfers between devices  8.7 us (28%)
  Pallas kernels  2.87 us (9%)
  local copies, waits for them, and re-layouts  1.04 us (3%)
  between operations  0.73 us (2%)
    ppermute x9, starting transfers between devices, send(): return lax.ppermute(block, ('gx', 'gy', 'gz'), route)  13.5 us
    ppermute x9, waiting for transfers between devices, send(): return lax.ppermute(block, ('gx', 'gy', 'gz'), route)  7.83 us
    ppermute x3, starting transfers between devices, swap(): return lax.ppermute(block, 'gx', [(i, i ^ 1) for i in range(n)])  4.48 us
    pallas_call x1, Pallas kernels, on_device(): pl.pallas_call(functools.partial(north_kernel, **sizes), in_specs=[vmem]...  1.19 us
    unnamed x4, local copies, waits for them, and re-layouts  1.04 us
    ppermute x3, waiting for transfers between devices, swap(): return lax.ppermute(block, 'gx', [(i, i ^ 1) for i in range(n)])  0.87 us
    pallas_call x1, Pallas kernels, on_device(): pl.pallas_call(block_kernel, in_specs=[smem, vmem], out_shape=(shape(quan...  0.68 us
  transfers between devices with their start and end apart: 12, of which 6 were waited for; matrix products, arithmetic and copies ran while one was open for 0% of the time, Pallas kernels for 7%

profile of v6, /device:TPU:1, one launch (start us, length us, event | category | flops | bytes accessed | tf_op | source)
XLA Modules:
  0.0 31.3 jit_solution(11686636779852076700)
XLA Ops:
  0.0 0.0 copy-start
  0.0 1.0 %copy-done = s32[32,32,128]{2,1,0:T(8,128)S(1)} copy-done((s32[32,32,128]{2,1,0:T(8,128)S(1)}, s32[32,32,128]{2,1,0:T(8,128)}, u32[]{:S(2)}) %copy-start) | copy-done | bytes 524312
  1.0 0.0 copy-start.1
  1.0 0.2 shard_map.28.mine
  1.2 3.3 %collective-permute-start = (s32[64,128]{1,0:T(8,128)S(1)}, s32[64,128]{1,0:T(8,128)S(1)}, u32[]{:S(2)}, u32[]{:S(2)}) collective-permute-start(s32[64,128]{1,0:T(8,128)S(1)} %shard_map.28.mine), channel_id=1, source_target_pairs={{0,16},{16,0},{32,48},{48,32},{64,80},{80,64},{96,112},{112,96},{1... | collective-permute-start | bytes 98312 | tf_op jit(solution)/shard_map/ppermute | solution.py:326
  4.5 0.9 %collective-permute-done.other = s32[64,128]{1,0:T(8,128)S(1)} collective-permute-done((s32[64,128]{1,0:T(8,128)S(1)}, s32[64,128]{1,0:T(8,128)S(1)}, u32[]{:S(2)}, u32[]{:S(2)}) %collective-permute-start) | collective-permute-done | bytes 32800 | tf_op jit(solution)/shard_map/ppermute | solution.py:326
  5.4 0.0 collective-permute-start.1
  6.0 0.0 copy-done.1
  6.0 0.7 %block.1 = (s32[32,32,128]{2,1,0:T(8,128)S(1)}, s32[128,128]{1,0:T(8,128)S(1)}, f32[8,128]{1,0:T(8,128)S(1)}) custom-call(f32[1]{0:T(128)S(6)} %copy.5.step, s32[32,32,128]{2,1,0:T(8,128)S(1)} %copy-done.1), custom_call_target="tpu_custom_call" | custom-call | flops 4000000 | bytes 1100000 | tf_op jit(solution)/shard_map/block/pallas_call | solution.py:330
  6.7 1.4 %collective-permute-done.1.got = s32[64,128]{1,0:T(8,128)S(1)} collective-permute-done((s32[64,128]{1,0:T(8,128)S(1)}, s32[64,128]{1,0:T(8,128)S(1)}, u32[]{:S(2)}, u32[]{:S(2)}) %collective-permute-start.1) | collective-permute-done | bytes 32800 | tf_op jit(solution)/shard_map/ppermute | solution.py:316
  8.2 1.6 %collective-permute-start.2 = (s32[64,128]{1,0:T(8,128)S(1)}, s32[64,128]{1,0:T(8,128)S(1)}, u32[]{:S(2)}, u32[]{:S(2)}) collective-permute-start(s32[64,128]{1,0:T(8,128)S(1)} %get-tuple-element.24.sent), channel_id=1, source_target_pairs={{0,4},{1,5},{2,6},{3,7},{4,0},{5,1},{6,2},{7,3},{8,12},{9,13},{10,... | collective-permute-start | bytes 98312 | tf_op jit(solution)/shard_map/ppermute | solution.py:316
  9.8 0.1 collective-permute-start.4
  9.8 0.4 %inner.1._ = s32[32,32,128]{2,1,0:T(8,128)S(1)} custom-call(s32[32,32,128]{2,1,0:T(8,128)S(1)} %get-tuple-element.26.full, s32[64,128]{1,0:T(8,128)S(1)} %get-tuple-element.25._.before), custom_call_target="tpu_custom_call" | custom-call | flops 4000000 | bytes 1100000 | tf_op jit(solution)/shard_map/inner/pallas_call | solution.py:346
  10.3 1.7 %collective-permute-done.2.got = s32[64,128]{1,0:T(8,128)S(1)} collective-permute-done((s32[64,128]{1,0:T(8,128)S(1)}, s32[64,128]{1,0:T(8,128)S(1)}, u32[]{:S(2)}, u32[]{:S(2)}) %collective-permute-start.2) | collective-permute-done | bytes 32800 | tf_op jit(solution)/shard_map/ppermute | solution.py:316
  11.9 3.9 %collective-permute-start.3 = (s32[64,128]{1,0:T(8,128)S(1)}, s32[64,128]{1,0:T(8,128)S(1)}, u32[]{:S(2)}, u32[]{:S(2)}) collective-permute-start(s32[64,128]{1,0:T(8,128)S(1)} %get-tuple-element.27), channel_id=1, source_target_pairs={{0,4},{1,5},{2,6},{3,7},{4,0},{5,1},{6,2},{7,3},{8,12},{9,13},{10,... | collective-permute-start | bytes 98312 | tf_op jit(solution)/shard_map/ppermute | solution.py:316
  15.9 0.0 collective-permute-done.4.theirs
  15.9 1.3 %collective-permute-done.3.got = s32[64,128]{1,0:T(8,128)S(1)} collective-permute-done((s32[64,128]{1,0:T(8,128)S(1)}, s32[64,128]{1,0:T(8,128)S(1)}, u32[]{:S(2)}, u32[]{:S(2)}) %collective-permute-start.3) | collective-permute-done | bytes 32800 | tf_op jit(solution)/shard_map/ppermute | solution.py:316
  17.2 0.1 shard_map.32
  17.3 1.3 %collective-permute-start.5 = (s32[72,128]{1,0:T(8,128)S(1)}, s32[72,128]{1,0:T(8,128)S(1)}, u32[]{:S(2)}, u32[]{:S(2)}) collective-permute-start(s32[72,128]{1,0:T(8,128)S(1)} %get-tuple-element.30), channel_id=1, source_target_pairs={{0,4},{1,5},{2,6},{3,7},{4,0},{5,1},{6,2},{7,3},{8,12},{9,13},{10,... | collective-permute-start | bytes 110600 | tf_op jit(solution)/shard_map/ppermute | solution.py:316
  18.6 2.4 %collective-permute-start.6 = (s32[72,128]{1,0:T(8,128)S(1)}, s32[72,128]{1,0:T(8,128)S(1)}, u32[]{:S(2)}, u32[]{:S(2)}) collective-permute-start(s32[72,128]{1,0:T(8,128)S(1)} %get-tuple-element.31), channel_id=1, source_target_pairs={{0,4},{1,5},{2,6},{3,7},{4,0},{5,1},{6,2},{7,3},{8,12},{9,13},{10,... | collective-permute-start | bytes 110600 | tf_op jit(solution)/shard_map/ppermute | solution.py:316
  21.1 0.2 collective-permute-start.7
  21.3 0.0 collective-permute-done.5.got1
  21.3 1.9 %collective-permute-done.6.got2 = s32[72,128]{1,0:T(8,128)S(1)} collective-permute-done((s32[72,128]{1,0:T(8,128)S(1)}, s32[72,128]{1,0:T(8,128)S(1)}, u32[]{:S(2)}, u32[]{:S(2)}) %collective-permute-start.6) | collective-permute-done | bytes 36896 | tf_op jit(solution)/shard_map/ppermute | solution.py:316
  23.2 0.0 collective-permute-done.7.got3
  23.2 0.1 shard_map.33
  23.3 1.4 %collective-permute-start.8 = (s32[40,128]{1,0:T(8,128)S(1)}, s32[40,128]{1,0:T(8,128)S(1)}, u32[]{:S(2)}, u32[]{:S(2)}) collective-permute-start(s32[40,128]{1,0:T(8,128)S(1)} %get-tuple-element.34), channel_id=1, source_target_pairs={{0,4},{1,5},{2,6},{3,7},{4,0},{5,1},{6,2},{7,3},{8,12},{9,13},{10,... | collective-permute-start | bytes 61448 | tf_op jit(solution)/shard_map/ppermute | solution.py:316
  24.7 2.6 %collective-permute-start.9 = (s32[40,128]{1,0:T(8,128)S(1)}, s32[40,128]{1,0:T(8,128)S(1)}, u32[]{:S(2)}, u32[]{:S(2)}) collective-permute-start(s32[40,128]{1,0:T(8,128)S(1)} %get-tuple-element.35), channel_id=1, source_target_pairs={{0,4},{1,5},{2,6},{3,7},{4,0},{5,1},{6,2},{7,3},{8,12},{9,13},{10,... | collective-permute-start | bytes 61448 | tf_op jit(solution)/shard_map/ppermute | solution.py:316
  27.3 0.0 collective-permute-start.10
  27.3 0.0 collective-permute-done.8.got1
  27.3 1.5 %collective-permute-done.9.got2 = s32[40,128]{1,0:T(8,128)S(1)} collective-permute-done((s32[40,128]{1,0:T(8,128)S(1)}, s32[40,128]{1,0:T(8,128)S(1)}, u32[]{:S(2)}, u32[]{:S(2)}) %collective-permute-start.9) | collective-permute-done | bytes 20512 | tf_op jit(solution)/shard_map/ppermute | solution.py:316
  28.8 0.0 collective-permute-done.10.got3
  28.8 0.1 shard_map.34
  28.9 1.1 %collective-permute-start.11 = (s32[176,128]{1,0:T(8,128)S(1)}, s32[176,128]{1,0:T(8,128)S(1)}, u32[]{:S(2)}, u32[]{:S(2)}) collective-permute-start(s32[176,128]{1,0:T(8,128)S(1)} %get-tuple-element.39), channel_id=1, source_target_pairs={{0,16},{16,0},{32,48},{48,32},{64,80},{80,64},{96,112},{112,96},{1... | collective-permute-start | bytes 270344 | tf_op jit(solution)/shard_map/ppermute | solution.py:326
  30.1 1.2 %north.1._ = f32[32,32,128]{2,1,0:T(8,128)} custom-call(f32[8,128]{1,0:T(8,128)S(1)} %get-tuple-element.23._.step, s32[176,128]{1,0:T(8,128)S(1)} %get-tuple-element.40.pack, s32[32,32,128]{2,1,0:T(8,128)S(1)} %inner.1._, s32[32,32,128]{2,1,0:T(8,128)S(1)} %get-tuple-element.26.full, s32[96,128]{1,0:T(8,128)S(1)} %get-tuple-element.38.planes), custom_call_target="tpu_custom_call" | custom-call | flops 4000000 | bytes 1100000 | tf_op jit(solution)/shard_map/north/pallas_call | solution.py:376
  31.3 0.0 collective-permute-done.11.pack
  31.3 0.1 south.1
  (3 shorter events, 0.0 us)
Async XLA Ops:
  0.0 1.0 %copy-start = (s32[32,32,128]{2,1,0:T(8,128)S(1)}, s32[32,32,128]{2,1,0:T(8,128)}, u32[]{:S(2)}) copy-start(s32[32,32,128]{2,1,0:T(8,128)} %q.3) | copy-start | bytes 1572868
  1.0 5.0 %copy-start.1 = (s32[32,32,128]{2,1,0:T(8,128)S(1)}, s32[32,32,128]{2,1,0:T(8,128)}, u32[]{:S(2)}) copy-start(s32[32,32,128]{2,1,0:T(8,128)} %q.3) | copy-start | bytes 1572868
  1.2 4.1 %collective-permute-start = (s32[64,128]{1,0:T(8,128)S(1)}, s32[64,128]{1,0:T(8,128)S(1)}, u32[]{:S(2)}, u32[]{:S(2)}) collective-permute-start(s32[64,128]{1,0:T(8,128)S(1)} %shard_map.28.mine), channel_id=1, source_target_pairs={{0,16},{16,0},{32,48},{48,32},{64,80},{80,64},{96,112},{112,96},{1... | collective-permute-start | bytes 98312 | tf_op jit(solution)/shard_map/ppermute | solution.py:326
  5.4 2.8 %collective-permute-start.1 = (s32[64,128]{1,0:T(8,128)S(1)}, s32[64,128]{1,0:T(8,128)S(1)}, u32[]{:S(2)}, u32[]{:S(2)}) collective-permute-start(s32[64,128]{1,0:T(8,128)S(1)} %shard_map.29.sent), channel_id=1, source_target_pairs={{0,4},{1,5},{2,6},{3,7},{4,0},{5,1},{6,2},{7,3},{8,12},{9,13},{10,... | collective-permute-start | bytes 98312 | tf_op jit(solution)/shard_map/ppermute | solution.py:316
  8.2 3.8 %collective-permute-start.2 = (s32[64,128]{1,0:T(8,128)S(1)}, s32[64,128]{1,0:T(8,128)S(1)}, u32[]{:S(2)}, u32[]{:S(2)}) collective-permute-start(s32[64,128]{1,0:T(8,128)S(1)} %get-tuple-element.24.sent), channel_id=1, source_target_pairs={{0,4},{1,5},{2,6},{3,7},{4,0},{5,1},{6,2},{7,3},{8,12},{9,13},{10,... | collective-permute-start | bytes 98312 | tf_op jit(solution)/shard_map/ppermute | solution.py:316
  9.8 6.1 %collective-permute-start.4 = (s32[128,128]{1,0:T(8,128)S(1)}, s32[128,128]{1,0:T(8,128)S(1)}, u32[]{:S(2)}, u32[]{:S(2)}) collective-permute-start(s32[128,128]{1,0:T(8,128)S(1)} %get-tuple-element.29.mine), channel_id=1, source_target_pairs={{0,16},{16,0},{32,48},{48,32},{64,80},{80,64},{96,112},{112,96},{1... | collective-permute-start | bytes 196616 | tf_op jit(solution)/shard_map/ppermute | solution.py:326
  11.9 5.2 %collective-permute-start.3 = (s32[64,128]{1,0:T(8,128)S(1)}, s32[64,128]{1,0:T(8,128)S(1)}, u32[]{:S(2)}, u32[]{:S(2)}) collective-permute-start(s32[64,128]{1,0:T(8,128)S(1)} %get-tuple-element.27), channel_id=1, source_target_pairs={{0,4},{1,5},{2,6},{3,7},{4,0},{5,1},{6,2},{7,3},{8,12},{9,13},{10,... | collective-permute-start | bytes 98312 | tf_op jit(solution)/shard_map/ppermute | solution.py:316
  17.3 3.9 %collective-permute-start.5 = (s32[72,128]{1,0:T(8,128)S(1)}, s32[72,128]{1,0:T(8,128)S(1)}, u32[]{:S(2)}, u32[]{:S(2)}) collective-permute-start(s32[72,128]{1,0:T(8,128)S(1)} %get-tuple-element.30), channel_id=1, source_target_pairs={{0,4},{1,5},{2,6},{3,7},{4,0},{5,1},{6,2},{7,3},{8,12},{9,13},{10,... | collective-permute-start | bytes 110600 | tf_op jit(solution)/shard_map/ppermute | solution.py:316
  18.6 4.6 %collective-permute-start.6 = (s32[72,128]{1,0:T(8,128)S(1)}, s32[72,128]{1,0:T(8,128)S(1)}, u32[]{:S(2)}, u32[]{:S(2)}) collective-permute-start(s32[72,128]{1,0:T(8,128)S(1)} %get-tuple-element.31), channel_id=1, source_target_pairs={{0,4},{1,5},{2,6},{3,7},{4,0},{5,1},{6,2},{7,3},{8,12},{9,13},{10,... | collective-permute-start | bytes 110600 | tf_op jit(solution)/shard_map/ppermute | solution.py:316
  21.1 2.1 %collective-permute-start.7 = (s32[72,128]{1,0:T(8,128)S(1)}, s32[72,128]{1,0:T(8,128)S(1)}, u32[]{:S(2)}, u32[]{:S(2)}) collective-permute-start(s32[72,128]{1,0:T(8,128)S(1)} %get-tuple-element.32), channel_id=1, source_target_pairs={{0,16},{1,17},{2,18},{3,19},{4,0},{5,1},{6,2},{7,3},{8,4},{9,5},{1... | collective-permute-start | bytes 110600 | tf_op jit(solution)/shard_map/ppermute | solution.py:316
  23.3 4.0 %collective-permute-start.8 = (s32[40,128]{1,0:T(8,128)S(1)}, s32[40,128]{1,0:T(8,128)S(1)}, u32[]{:S(2)}, u32[]{:S(2)}) collective-permute-start(s32[40,128]{1,0:T(8,128)S(1)} %get-tuple-element.34), channel_id=1, source_target_pairs={{0,4},{1,5},{2,6},{3,7},{4,0},{5,1},{6,2},{7,3},{8,12},{9,13},{10,... | collective-permute-start | bytes 61448 | tf_op jit(solution)/shard_map/ppermute | solution.py:316
  24.7 4.1 %collective-permute-start.9 = (s32[40,128]{1,0:T(8,128)S(1)}, s32[40,128]{1,0:T(8,128)S(1)}, u32[]{:S(2)}, u32[]{:S(2)}) collective-permute-start(s32[40,128]{1,0:T(8,128)S(1)} %get-tuple-element.35), channel_id=1, source_target_pairs={{0,4},{1,5},{2,6},{3,7},{4,0},{5,1},{6,2},{7,3},{8,12},{9,13},{10,... | collective-permute-start | bytes 61448 | tf_op jit(solution)/shard_map/ppermute | solution.py:316
  27.3 1.5 %collective-permute-start.10 = (s32[40,128]{1,0:T(8,128)S(1)}, s32[40,128]{1,0:T(8,128)S(1)}, u32[]{:S(2)}, u32[]{:S(2)}) collective-permute-start(s32[40,128]{1,0:T(8,128)S(1)} %get-tuple-element.36), channel_id=1, source_target_pairs={{0,16},{1,0},{2,1},{3,2},{4,20},{5,4},{6,5},{7,6},{8,24},{9,8},{10... | collective-permute-start | bytes 61448 | tf_op jit(solution)/shard_map/ppermute | solution.py:316
  28.9 2.3 %collective-permute-start.11 = (s32[176,128]{1,0:T(8,128)S(1)}, s32[176,128]{1,0:T(8,128)S(1)}, u32[]{:S(2)}, u32[]{:S(2)}) collective-permute-start(s32[176,128]{1,0:T(8,128)S(1)} %get-tuple-element.39), channel_id=1, source_target_pairs={{0,16},{16,0},{32,48},{48,32},{64,80},{80,64},{96,112},{112,96},{1... | collective-permute-start | bytes 270344 | tf_op jit(solution)/shard_map/ppermute | solution.py:326

commit v7 on v6

--- a/solution.py
+++ b/solution.py
@@ -94,8 +94,7 @@
 
 def quad_kernel(sent, got, before, other, _, send, state):
     chip = lax.axis_index("gx") // 2
-    send[0:32, :] = sent[0:32, :] + got[0:32, :]
-    send[32:64, :] = other[32:64, :]
+    send[...] = jnp.where(chip == 4, other[32:64, :], sent[0:32, :] + got[0:32, :])
     state[0:32, :] = before[0:32, :] + jnp.where(chip % 4 >= 2, got[0:32, :], 0)
     state[32:64, :] = jnp.where(chip % 4 == 1, got[32:64, :], before[32:64, :])
 
@@ -104,8 +103,8 @@
     chip, y = lax.axis_index("gx") // 2, lax.axis_index("gy")
     lane = lax.broadcasted_iota(I32, (32, 128), 1)
     row = lax.broadcasted_iota(I32, (8, 128), 0)
-    c = before[0:32, :] + jnp.where(chip >= 4, got[0:32, :], 0)
-    nxt = jnp.where(chip == 3, got[32:64, :], before[32:64, :])
+    c = before[0:32, :] + jnp.where(chip >= 4, got[...], 0)
+    nxt = jnp.where(chip == 3, got[...], before[32:64, :])
     d = c + other[0:32, :]
     planes[0:32, :] = c
     planes[32:64, :] = d
@@ -277,24 +276,36 @@
 
     across = [route(lambda x, y, z, d=d: (x ^ d, y, z)) for d in (2, 4)]
     across.append(route(lambda x, y, z: (n - x, y, z)))
-    along_y = [route(lambda x, y, z, d=d: (x, y ^ d, z)) for d in (1, 2)]
-    along_z = [route(lambda x, y, z, d=d: (x, y, z ^ d)) for d in (1, 2)]
+
+    def middle(x, at, size):
+        half = size // 2
+        if x % 2:
+            return (x, at + half) if at < half else (x - 1, at)
+        return (x + 1, at) if at < half else (x, size - 1 - at)
 
     def far(x, at, size):
         if x % 2:
             return (x, size - 1 - at) if at < size - 1 else (x - 1, at)
         return (x, at - 1) if at else (x + 1, at)
 
-    def far_y(x, y, z):
-        x, y = far(x, y, ny)
-        return x, y, z
-
-    def far_z(x, y, z):
-        x, z = far(x, z, nz)
-        return x, y, z
-
-    along_y.append(route(far_y, far_y))
-    along_z.append(route(far_z, far_z))
+    def in_y(step):
+        def move(x, y, z):
+            x, y = step(x, y, ny)
+            return x, y, z
+
+        return route(move, move)
+
+    def in_z(step):
+        def move(x, y, z):
+            x, z = step(x, z, nz)
+            return x, y, z
+
+        return route(move, move)
+
+    near_y = route(lambda x, y, z: (x, y ^ 1, z))
+    near_z = route(lambda x, y, z: (x, y, z ^ 1))
+    along_y = [near_y, in_y(middle), in_y(far)]
+    along_z = [near_z, in_z(middle), in_z(far)]
     return across, along_y, along_z
 
 
@@ -351,7 +362,7 @@
         cost_estimate=pl.CostEstimate(flops=4_000_000, bytes_accessed=1_100_000, transcendentals=0),
         name="inner",
     )(full, state)
-    sent, state = call(quad_kernel, (64, 64), sent, got, state, other, inner)
+    sent, state = call(quad_kernel, (32, 64), sent, got, state, other, inner)
     their_faces = swap(faces)
     got = send(sent, across[2])
     *sent, z_base, planes = call(

time: 31.5 us -> 30.9 us (0.981)
  waiting for transfers between devices: 8.7 us -> 6.53 us
  starting transfers between devices: 18 us -> 19.6 us
    ppermute x9, waiting for transfers between devices: 7.83 us -> 5.66 us  [send(): return lax.ppermute(block, ('gx', 'gy', 'gz'), route)]
    ppermute x3, starting transfers between devices: 4.48 us -> 5.29 us  [swap(): return lax.ppermute(block, 'gx', [(i, i ^ 1) for i in range(n)])]
    ppermute x9, starting transfers between devices: 13.5 us -> 14.3 us  [send(): return lax.ppermute(block, ('gx', 'gy', 'gz'), route)]
  transfers between devices with their start and end apart: 12 -> 12, of which waited for: 6 -> 8; matrix products, arithmetic and copies ran while one was open for 0% -> 0% of each run, Pallas kernels for 7% -> 7%
where the time goes in v7:
time: 30.9 us; the launch traced here: 30.8 us
  starting transfers between devices  19.6 us (63%)
  waiting for transfers between devices  6.53 us (21%)
  Pallas kernels  2.87 us (9%)
  local copies, waits for them, and re-layouts  1.04 us (3%)
  between operations  0.74 us (2%)
    ppermute x9, starting transfers between devices, send(): return lax.ppermute(block, ('gx', 'gy', 'gz'), route)  14.3 us
    ppermute x9, waiting for transfers between devices, send(): return lax.ppermute(block, ('gx', 'gy', 'gz'), route)  5.66 us
    ppermute x3, starting transfers between devices, swap(): return lax.ppermute(block, 'gx', [(i, i ^ 1) for i in range(n)])  5.29 us
    pallas_call x1, Pallas kernels, on_device(): pl.pallas_call(functools.partial(north_kernel, **sizes), in_specs=[vmem]...  1.19 us
    unnamed x4, local copies, waits for them, and re-layouts  1.04 us
    ppermute x3, waiting for transfers between devices, swap(): return lax.ppermute(block, 'gx', [(i, i ^ 1) for i in range(n)])  0.87 us
    pallas_call x1, Pallas kernels, on_device(): pl.pallas_call(block_kernel, in_specs=[smem, vmem], out_shape=(shape(quan...  0.68 us
  transfers between devices with their start and end apart: 12, of which 8 were waited for; matrix products, arithmetic and copies ran while one was open for 0% of the time, Pallas kernels for 7%

profile of v7, /device:TPU:1, one launch (start us, length us, event | category | flops | bytes accessed | tf_op | source)
XLA Modules:
  0.0 30.8 jit_solution(5734553884053110904)
XLA Ops:
  0.0 0.0 copy-start
  0.0 1.0 %copy-done = s32[32,32,128]{2,1,0:T(8,128)S(1)} copy-done((s32[32,32,128]{2,1,0:T(8,128)S(1)}, s32[32,32,128]{2,1,0:T(8,128)}, u32[]{:S(2)}) %copy-start) | copy-done | bytes 524312
  1.0 0.0 copy-start.1
  1.0 0.2 shard_map.28.mine
  1.2 3.3 %collective-permute-start = (s32[64,128]{1,0:T(8,128)S(1)}, s32[64,128]{1,0:T(8,128)S(1)}, u32[]{:S(2)}, u32[]{:S(2)}) collective-permute-start(s32[64,128]{1,0:T(8,128)S(1)} %shard_map.28.mine), channel_id=1, source_target_pairs={{0,16},{16,0},{32,48},{48,32},{64,80},{80,64},{96,112},{112,96},{1... | collective-permute-start | bytes 98312 | tf_op jit(solution)/shard_map/ppermute | solution.py:337
  4.5 0.9 %collective-permute-done.other = s32[64,128]{1,0:T(8,128)S(1)} collective-permute-done((s32[64,128]{1,0:T(8,128)S(1)}, s32[64,128]{1,0:T(8,128)S(1)}, u32[]{:S(2)}, u32[]{:S(2)}) %collective-permute-start) | collective-permute-done | bytes 32800 | tf_op jit(solution)/shard_map/ppermute | solution.py:337
  5.4 0.0 collective-permute-start.1
  6.0 0.0 copy-done.1
  6.0 0.7 %block.1 = (s32[32,32,128]{2,1,0:T(8,128)S(1)}, s32[128,128]{1,0:T(8,128)S(1)}, f32[8,128]{1,0:T(8,128)S(1)}) custom-call(f32[1]{0:T(128)S(6)} %copy.5.step, s32[32,32,128]{2,1,0:T(8,128)S(1)} %copy-done.1), custom_call_target="tpu_custom_call" | custom-call | flops 4000000 | bytes 1100000 | tf_op jit(solution)/shard_map/block/pallas_call | solution.py:341
  6.7 0.4 %collective-permute-start.4 = (s32[128,128]{1,0:T(8,128)S(1)}, s32[128,128]{1,0:T(8,128)S(1)}, u32[]{:S(2)}, u32[]{:S(2)}) collective-permute-start(s32[128,128]{1,0:T(8,128)S(1)} %get-tuple-element.29.mine), channel_id=1, source_target_pairs={{0,16},{16,0},{32,48},{48,32},{64,80},{80,64},{96,112},{112,96},{1... | collective-permute-start | bytes 196616 | tf_op jit(solution)/shard_map/ppermute | solution.py:337
  7.2 1.0 %collective-permute-done.1.got = s32[64,128]{1,0:T(8,128)S(1)} collective-permute-done((s32[64,128]{1,0:T(8,128)S(1)}, s32[64,128]{1,0:T(8,128)S(1)}, u32[]{:S(2)}, u32[]{:S(2)}) %collective-permute-start.1) | collective-permute-done | bytes 32800 | tf_op jit(solution)/shard_map/ppermute | solution.py:327
  8.2 1.9 %collective-permute-start.2 = (s32[64,128]{1,0:T(8,128)S(1)}, s32[64,128]{1,0:T(8,128)S(1)}, u32[]{:S(2)}, u32[]{:S(2)}) collective-permute-start(s32[64,128]{1,0:T(8,128)S(1)} %get-tuple-element.24.sent), channel_id=1, source_target_pairs={{0,4},{1,5},{2,6},{3,7},{4,0},{5,1},{6,2},{7,3},{8,12},{9,13},{10,... | collective-permute-start | bytes 98312 | tf_op jit(solution)/shard_map/ppermute | solution.py:327
  10.1 0.4 %inner.1._ = s32[32,32,128]{2,1,0:T(8,128)S(1)} custom-call(s32[32,32,128]{2,1,0:T(8,128)S(1)} %get-tuple-element.26.full, s32[64,128]{1,0:T(8,128)S(1)} %get-tuple-element.25._.before), custom_call_target="tpu_custom_call" | custom-call | flops 4000000 | bytes 1100000 | tf_op jit(solution)/shard_map/inner/pallas_call | solution.py:357
  10.5 1.4 %collective-permute-done.2.got = s32[64,128]{1,0:T(8,128)S(1)} collective-permute-done((s32[64,128]{1,0:T(8,128)S(1)}, s32[64,128]{1,0:T(8,128)S(1)}, u32[]{:S(2)}, u32[]{:S(2)}) %collective-permute-start.2) | collective-permute-done | bytes 32800 | tf_op jit(solution)/shard_map/ppermute | solution.py:327
  11.9 4.5 %collective-permute-start.3 = (s32[32,128]{1,0:T(8,128)S(1)}, s32[32,128]{1,0:T(8,128)S(1)}, u32[]{:S(2)}, u32[]{:S(2)}) collective-permute-start(s32[32,128]{1,0:T(8,128)S(1)} %get-tuple-element.27), channel_id=1, source_target_pairs={{0,4},{1,5},{2,6},{3,7},{4,0},{5,1},{6,2},{7,3},{8,12},{9,13},{10,... | collective-permute-start | bytes 49160 | tf_op jit(solution)/shard_map/ppermute | solution.py:327
  16.4 0.0 collective-permute-done.4.theirs
  16.4 1.1 %collective-permute-done.3.got = s32[32,128]{1,0:T(8,128)S(1)} collective-permute-done((s32[32,128]{1,0:T(8,128)S(1)}, s32[32,128]{1,0:T(8,128)S(1)}, u32[]{:S(2)}, u32[]{:S(2)}) %collective-permute-start.3) | collective-permute-done | bytes 16416 | tf_op jit(solution)/shard_map/ppermute | solution.py:327
  17.5 0.1 shard_map.32
  17.7 0.8 %collective-permute-start.5 = (s32[72,128]{1,0:T(8,128)S(1)}, s32[72,128]{1,0:T(8,128)S(1)}, u32[]{:S(2)}, u32[]{:S(2)}) collective-permute-start(s32[72,128]{1,0:T(8,128)S(1)} %get-tuple-element.30), channel_id=1, source_target_pairs={{0,4},{1,5},{2,6},{3,7},{4,0},{5,1},{6,2},{7,3},{8,12},{9,13},{10,... | collective-permute-start | bytes 110600 | tf_op jit(solution)/shard_map/ppermute | solution.py:327
  18.4 2.4 %collective-permute-start.6 = (s32[72,128]{1,0:T(8,128)S(1)}, s32[72,128]{1,0:T(8,128)S(1)}, u32[]{:S(2)}, u32[]{:S(2)}) collective-permute-start(s32[72,128]{1,0:T(8,128)S(1)} %get-tuple-element.31), channel_id=1, source_target_pairs={{0,16},{1,17},{2,18},{3,19},{4,20},{5,21},{6,22},{7,23},{8,4},{9,5... | collective-permute-start | bytes 110600 | tf_op jit(solution)/shard_map/ppermute | solution.py:327
  20.9 0.0 collective-permute-start.7
  20.9 0.0 collective-permute-done.5.got1
  20.9 1.1 %collective-permute-done.6.got2 = s32[72,128]{1,0:T(8,128)S(1)} collective-permute-done((s32[72,128]{1,0:T(8,128)S(1)}, s32[72,128]{1,0:T(8,128)S(1)}, u32[]{:S(2)}, u32[]{:S(2)}) %collective-permute-start.6) | collective-permute-done | bytes 36896 | tf_op jit(solution)/shard_map/ppermute | solution.py:327
  21.9 0.2 collective-permute-done.7.got3
  22.1 0.1 shard_map.33
  22.2 1.4 %collective-permute-start.8 = (s32[40,128]{1,0:T(8,128)S(1)}, s32[40,128]{1,0:T(8,128)S(1)}, u32[]{:S(2)}, u32[]{:S(2)}) collective-permute-start(s32[40,128]{1,0:T(8,128)S(1)} %get-tuple-element.34), channel_id=1, source_target_pairs={{0,4},{1,5},{2,6},{3,7},{4,0},{5,1},{6,2},{7,3},{8,12},{9,13},{10,... | collective-permute-start | bytes 61448 | tf_op jit(solution)/shard_map/ppermute | solution.py:327
  23.6 2.6 %collective-permute-start.9 = (s32[40,128]{1,0:T(8,128)S(1)}, s32[40,128]{1,0:T(8,128)S(1)}, u32[]{:S(2)}, u32[]{:S(2)}) collective-permute-start(s32[40,128]{1,0:T(8,128)S(1)} %get-tuple-element.35), channel_id=1, source_target_pairs={{0,16},{1,17},{2,1},{3,0},{4,20},{5,21},{6,5},{7,4},{8,24},{9,25},... | collective-permute-start | bytes 61448 | tf_op jit(solution)/shard_map/ppermute | solution.py:327
  26.2 0.7 %collective-permute-start.10 = (s32[40,128]{1,0:T(8,128)S(1)}, s32[40,128]{1,0:T(8,128)S(1)}, u32[]{:S(2)}, u32[]{:S(2)}) collective-permute-start(s32[40,128]{1,0:T(8,128)S(1)} %get-tuple-element.36), channel_id=1, source_target_pairs={{0,16},{1,0},{2,1},{3,2},{4,20},{5,4},{6,5},{7,6},{8,24},{9,8},{10... | collective-permute-start | bytes 61448 | tf_op jit(solution)/shard_map/ppermute | solution.py:327
  26.9 0.0 collective-permute-done.8.got1
  26.9 0.2 collective-permute-done.9.got2
  27.1 0.7 %collective-permute-done.10.got3 = s32[40,128]{1,0:T(8,128)S(1)} collective-permute-done((s32[40,128]{1,0:T(8,128)S(1)}, s32[40,128]{1,0:T(8,128)S(1)}, u32[]{:S(2)}, u32[]{:S(2)}) %collective-permute-start.10) | collective-permute-done | bytes 20512 | tf_op jit(solution)/shard_map/ppermute | solution.py:327
  27.8 0.1 shard_map.34
  27.9 1.6 %collective-permute-start.11 = (s32[176,128]{1,0:T(8,128)S(1)}, s32[176,128]{1,0:T(8,128)S(1)}, u32[]{:S(2)}, u32[]{:S(2)}) collective-permute-start(s32[176,128]{1,0:T(8,128)S(1)} %get-tuple-element.39), channel_id=1, source_target_pairs={{0,16},{16,0},{32,48},{48,32},{64,80},{80,64},{96,112},{112,96},{1... | collective-permute-start | bytes 270344 | tf_op jit(solution)/shard_map/ppermute | solution.py:337
  29.5 1.2 %north.1._ = f32[32,32,128]{2,1,0:T(8,128)} custom-call(f32[8,128]{1,0:T(8,128)S(1)} %get-tuple-element.23._.step, s32[176,128]{1,0:T(8,128)S(1)} %get-tuple-element.40.pack, s32[32,32,128]{2,1,0:T(8,128)S(1)} %inner.1._, s32[32,32,128]{2,1,0:T(8,128)S(1)} %get-tuple-element.26.full, s32[96,128]{1,0:T(8,128)S(1)} %get-tuple-element.38.planes), custom_call_target="tpu_custom_call" | custom-call | flops 4000000 | bytes 1100000 | tf_op jit(solution)/shard_map/north/pallas_call | solution.py:387
  30.7 0.0 collective-permute-done.11.pack
  30.7 0.1 south.1
  (3 shorter events, 0.0 us)
Async XLA Ops:
  0.0 1.0 %copy-start = (s32[32,32,128]{2,1,0:T(8,128)S(1)}, s32[32,32,128]{2,1,0:T(8,128)}, u32[]{:S(2)}) copy-start(s32[32,32,128]{2,1,0:T(8,128)} %q.3) | copy-start | bytes 1572868
  1.0 5.0 %copy-start.1 = (s32[32,32,128]{2,1,0:T(8,128)S(1)}, s32[32,32,128]{2,1,0:T(8,128)}, u32[]{:S(2)}) copy-start(s32[32,32,128]{2,1,0:T(8,128)} %q.3) | copy-start | bytes 1572868
  1.2 4.1 %collective-permute-start = (s32[64,128]{1,0:T(8,128)S(1)}, s32[64,128]{1,0:T(8,128)S(1)}, u32[]{:S(2)}, u32[]{:S(2)}) collective-permute-start(s32[64,128]{1,0:T(8,128)S(1)} %shard_map.28.mine), channel_id=1, source_target_pairs={{0,16},{16,0},{32,48},{48,32},{64,80},{80,64},{96,112},{112,96},{1... | collective-permute-start | bytes 98312 | tf_op jit(solution)/shard_map/ppermute | solution.py:337
  5.4 2.8 %collective-permute-start.1 = (s32[64,128]{1,0:T(8,128)S(1)}, s32[64,128]{1,0:T(8,128)S(1)}, u32[]{:S(2)}, u32[]{:S(2)}) collective-permute-start(s32[64,128]{1,0:T(8,128)S(1)} %shard_map.29.sent), channel_id=1, source_target_pairs={{0,4},{1,5},{2,6},{3,7},{4,0},{5,1},{6,2},{7,3},{8,12},{9,13},{10,... | collective-permute-start | bytes 98312 | tf_op jit(solution)/shard_map/ppermute | solution.py:327
  6.7 9.7 %collective-permute-start.4 = (s32[128,128]{1,0:T(8,128)S(1)}, s32[128,128]{1,0:T(8,128)S(1)}, u32[]{:S(2)}, u32[]{:S(2)}) collective-permute-start(s32[128,128]{1,0:T(8,128)S(1)} %get-tuple-element.29.mine), channel_id=1, source_target_pairs={{0,16},{16,0},{32,48},{48,32},{64,80},{80,64},{96,112},{112,96},{1... | collective-permute-start | bytes 196616 | tf_op jit(solution)/shard_map/ppermute | solution.py:337
  8.2 3.8 %collective-permute-start.2 = (s32[64,128]{1,0:T(8,128)S(1)}, s32[64,128]{1,0:T(8,128)S(1)}, u32[]{:S(2)}, u32[]{:S(2)}) collective-permute-start(s32[64,128]{1,0:T(8,128)S(1)} %get-tuple-element.24.sent), channel_id=1, source_target_pairs={{0,4},{1,5},{2,6},{3,7},{4,0},{5,1},{6,2},{7,3},{8,12},{9,13},{10,... | collective-permute-start | bytes 98312 | tf_op jit(solution)/shard_map/ppermute | solution.py:327
  11.9 5.6 %collective-permute-start.3 = (s32[32,128]{1,0:T(8,128)S(1)}, s32[32,128]{1,0:T(8,128)S(1)}, u32[]{:S(2)}, u32[]{:S(2)}) collective-permute-start(s32[32,128]{1,0:T(8,128)S(1)} %get-tuple-element.27), channel_id=1, source_target_pairs={{0,4},{1,5},{2,6},{3,7},{4,0},{5,1},{6,2},{7,3},{8,12},{9,13},{10,... | collective-permute-start | bytes 49160 | tf_op jit(solution)/shard_map/ppermute | solution.py:327
  17.7 3.2 %collective-permute-start.5 = (s32[72,128]{1,0:T(8,128)S(1)}, s32[72,128]{1,0:T(8,128)S(1)}, u32[]{:S(2)}, u32[]{:S(2)}) collective-permute-start(s32[72,128]{1,0:T(8,128)S(1)} %get-tuple-element.30), channel_id=1, source_target_pairs={{0,4},{1,5},{2,6},{3,7},{4,0},{5,1},{6,2},{7,3},{8,12},{9,13},{10,... | collective-permute-start | bytes 110600 | tf_op jit(solution)/shard_map/ppermute | solution.py:327
  18.4 3.5 %collective-permute-start.6 = (s32[72,128]{1,0:T(8,128)S(1)}, s32[72,128]{1,0:T(8,128)S(1)}, u32[]{:S(2)}, u32[]{:S(2)}) collective-permute-start(s32[72,128]{1,0:T(8,128)S(1)} %get-tuple-element.31), channel_id=1, source_target_pairs={{0,16},{1,17},{2,18},{3,19},{4,20},{5,21},{6,22},{7,23},{8,4},{9,5... | collective-permute-start | bytes 110600 | tf_op jit(solution)/shard_map/ppermute | solution.py:327
  20.9 1.2 %collective-permute-start.7 = (s32[72,128]{1,0:T(8,128)S(1)}, s32[72,128]{1,0:T(8,128)S(1)}, u32[]{:S(2)}, u32[]{:S(2)}) collective-permute-start(s32[72,128]{1,0:T(8,128)S(1)} %get-tuple-element.32), channel_id=1, source_target_pairs={{0,16},{1,17},{2,18},{3,19},{4,0},{5,1},{6,2},{7,3},{8,4},{9,5},{1... | collective-permute-start | bytes 110600 | tf_op jit(solution)/shard_map/ppermute | solution.py:327
  22.2 4.7 %collective-permute-start.8 = (s32[40,128]{1,0:T(8,128)S(1)}, s32[40,128]{1,0:T(8,128)S(1)}, u32[]{:S(2)}, u32[]{:S(2)}) collective-permute-start(s32[40,128]{1,0:T(8,128)S(1)} %get-tuple-element.34), channel_id=1, source_target_pairs={{0,4},{1,5},{2,6},{3,7},{4,0},{5,1},{6,2},{7,3},{8,12},{9,13},{10,... | collective-permute-start | bytes 61448 | tf_op jit(solution)/shard_map/ppermute | solution.py:327
  23.6 3.5 %collective-permute-start.9 = (s32[40,128]{1,0:T(8,128)S(1)}, s32[40,128]{1,0:T(8,128)S(1)}, u32[]{:S(2)}, u32[]{:S(2)}) collective-permute-start(s32[40,128]{1,0:T(8,128)S(1)} %get-tuple-element.35), channel_id=1, source_target_pairs={{0,16},{1,17},{2,1},{3,0},{4,20},{5,21},{6,5},{7,4},{8,24},{9,25},... | collective-permute-start | bytes 61448 | tf_op jit(solution)/shard_map/ppermute | solution.py:327
  26.2 1.6 %collective-permute-start.10 = (s32[40,128]{1,0:T(8,128)S(1)}, s32[40,128]{1,0:T(8,128)S(1)}, u32[]{:S(2)}, u32[]{:S(2)}) collective-permute-start(s32[40,128]{1,0:T(8,128)S(1)} %get-tuple-element.36), channel_id=1, source_target_pairs={{0,16},{1,0},{2,1},{3,2},{4,20},{5,4},{6,5},{7,6},{8,24},{9,8},{10... | collective-permute-start | bytes 61448 | tf_op jit(solution)/shard_map/ppermute | solution.py:327
  27.9 2.8 %collective-permute-start.11 = (s32[176,128]{1,0:T(8,128)S(1)}, s32[176,128]{1,0:T(8,128)S(1)}, u32[]{:S(2)}, u32[]{:S(2)}) collective-permute-start(s32[176,128]{1,0:T(8,128)S(1)} %get-tuple-element.39), channel_id=1, source_target_pairs={{0,16},{16,0},{32,48},{48,32},{64,80},{80,64},{96,112},{112,96},{1... | collective-permute-start | bytes 270344 | tf_op jit(solution)/shard_map/ppermute | solution.py:337

commit v8 on v7

--- a/solution.py
+++ b/solution.py
@@ -235,18 +235,19 @@
     hyz = held(has_y, hyz)
     end_z = jnp.where(has_z, hz, -az)
     scale = jnp.broadcast_to(step[0:1, :], (32, 128)) * (1.0 / 12.0)
+    ends = jnp.where(lane < 64, cols, pltpu.roll(cols + end_z, 64, 1))
     copies = []
     for i in range(nx):
-        total = inner[i] + (both + rows[i : i + 1, :]) + at_lane(cols, i)
-        total = total + jnp.where(lane == 127, at_lane(end_z, i), 0)
+        picked = jnp.take_along_axis(ends, jnp.where(lane == 127, 64 + i, i), axis=1)
+        total = inner[i] + (both + rows[i : i + 1, :]) + picked
         edge = end_y[i : i + 1, :] + jnp.broadcast_to(hyz[:, i : i + 1], (1, 128))
         total = total + jnp.where(row == 31, edge, 0)
         if i == nx - 1:
             total = total + jnp.where(has_x, full[i] + high, -low)
         out[i] = total.astype(jnp.float32) * scale
-        if i % 8 == 7:
-            part = slice(i - 7, i + 1)
-            copies.append(pltpu.make_async_copy(out.at[part], result.at[part], sems.at[i // 8]))
+        if i % 4 == 3:
+            part = slice(i - 3, i + 1)
+            copies.append(pltpu.make_async_copy(out.at[part], result.at[part], sems.at[i // 4]))
             copies[-1].start()
     for c in copies:
         c.wait()
@@ -379,7 +380,7 @@
         out_shape=shape(quant_codes.shape, jnp.float32),
         scratch_shapes=[
             pltpu.VMEM(quant_codes.shape, jnp.float32),
-            pltpu.SemaphoreType.DMA((4,)),
+            pltpu.SemaphoreType.DMA((8,)),
         ],
         compiler_params=params(),
         cost_estimate=pl.CostEstimate(flops=4_000_000, bytes_accessed=1_100_000, transcendentals=0),

time: 30.9 us -> 30.9 us (level)
  no operation moved by 1% of the time
where the time goes in v8:
time: 30.9 us; the launch traced here: 30.8 us
  starting transfers between devices  19.6 us (63%)
  waiting for transfers between devices  6.53 us (21%)
  Pallas kernels  2.9 us (9%)
  local copies, waits for them, and re-layouts  1.04 us (3%)
  between operations  0.74 us (2%)
    ppermute x9, starting transfers between devices, send(): return lax.ppermute(block, ('gx', 'gy', 'gz'), route)  14.3 us
    ppermute x9, waiting for transfers between devices, send(): return lax.ppermute(block, ('gx', 'gy', 'gz'), route)  5.66 us
    ppermute x3, starting transfers between devices, swap(): return lax.ppermute(block, 'gx', [(i, i ^ 1) for i in range(n)])  5.29 us
    pallas_call x1, Pallas kernels, on_device(): pl.pallas_call(functools.partial(north_kernel, **sizes), in_specs=[vmem]...  1.19 us
    unnamed x4, local copies, waits for them, and re-layouts  1.04 us
    ppermute x3, waiting for transfers between devices, swap(): return lax.ppermute(block, 'gx', [(i, i ^ 1) for i in range(n)])  0.87 us
    pallas_call x1, Pallas kernels, on_device(): pl.pallas_call(block_kernel, in_specs=[smem, vmem], out_shape=(shape(quan...  0.68 us
  transfers between devices with their start and end apart: 12, of which 8 were waited for; matrix products, arithmetic and copies ran while one was open for 0% of the time, Pallas kernels for 7%

profile of v8, /device:TPU:1, one launch (start us, length us, event | category | flops | bytes accessed | tf_op | source)
XLA Modules:
  0.0 30.8 jit_solution(2985060205312365474)
XLA Ops:
  0.0 0.0 copy-start
  0.0 1.0 %copy-done = s32[32,32,128]{2,1,0:T(8,128)S(1)} copy-done((s32[32,32,128]{2,1,0:T(8,128)S(1)}, s32[32,32,128]{2,1,0:T(8,128)}, u32[]{:S(2)}) %copy-start) | copy-done | bytes 524312
  1.0 0.0 copy-start.1
  1.0 0.2 shard_map.28.mine
  1.2 3.3 %collective-permute-start = (s32[64,128]{1,0:T(8,128)S(1)}, s32[64,128]{1,0:T(8,128)S(1)}, u32[]{:S(2)}, u32[]{:S(2)}) collective-permute-start(s32[64,128]{1,0:T(8,128)S(1)} %shard_map.28.mine), channel_id=1, source_target_pairs={{0,16},{16,0},{32,48},{48,32},{64,80},{80,64},{96,112},{112,96},{1... | collective-permute-start | bytes 98312 | tf_op jit(solution)/shard_map/ppermute | solution.py:338
  4.5 0.9 %collective-permute-done.other = s32[64,128]{1,0:T(8,128)S(1)} collective-permute-done((s32[64,128]{1,0:T(8,128)S(1)}, s32[64,128]{1,0:T(8,128)S(1)}, u32[]{:S(2)}, u32[]{:S(2)}) %collective-permute-start) | collective-permute-done | bytes 32800 | tf_op jit(solution)/shard_map/ppermute | solution.py:338
  5.4 0.0 collective-permute-start.1
  6.0 0.0 copy-done.1
  6.0 0.7 %block.1 = (s32[32,32,128]{2,1,0:T(8,128)S(1)}, s32[128,128]{1,0:T(8,128)S(1)}, f32[8,128]{1,0:T(8,128)S(1)}) custom-call(f32[1]{0:T(128)S(6)} %copy.5.step, s32[32,32,128]{2,1,0:T(8,128)S(1)} %copy-done.1), custom_call_target="tpu_custom_call" | custom-call | flops 4000000 | bytes 1100000 | tf_op jit(solution)/shard_map/block/pallas_call | solution.py:342
  6.7 0.4 %collective-permute-start.4 = (s32[128,128]{1,0:T(8,128)S(1)}, s32[128,128]{1,0:T(8,128)S(1)}, u32[]{:S(2)}, u32[]{:S(2)}) collective-permute-start(s32[128,128]{1,0:T(8,128)S(1)} %get-tuple-element.29.mine), channel_id=1, source_target_pairs={{0,16},{16,0},{32,48},{48,32},{64,80},{80,64},{96,112},{112,96},{1... | collective-permute-start | bytes 196616 | tf_op jit(solution)/shard_map/ppermute | solution.py:338
  7.2 1.0 %collective-permute-done.1.got = s32[64,128]{1,0:T(8,128)S(1)} collective-permute-done((s32[64,128]{1,0:T(8,128)S(1)}, s32[64,128]{1,0:T(8,128)S(1)}, u32[]{:S(2)}, u32[]{:S(2)}) %collective-permute-start.1) | collective-permute-done | bytes 32800 | tf_op jit(solution)/shard_map/ppermute | solution.py:328
  8.2 1.9 %collective-permute-start.2 = (s32[64,128]{1,0:T(8,128)S(1)}, s32[64,128]{1,0:T(8,128)S(1)}, u32[]{:S(2)}, u32[]{:S(2)}) collective-permute-start(s32[64,128]{1,0:T(8,128)S(1)} %get-tuple-element.24.sent), channel_id=1, source_target_pairs={{0,4},{1,5},{2,6},{3,7},{4,0},{5,1},{6,2},{7,3},{8,12},{9,13},{10,... | collective-permute-start | bytes 98312 | tf_op jit(solution)/shard_map/ppermute | solution.py:328
  10.1 0.4 %inner.1._ = s32[32,32,128]{2,1,0:T(8,128)S(1)} custom-call(s32[32,32,128]{2,1,0:T(8,128)S(1)} %get-tuple-element.26.full, s32[64,128]{1,0:T(8,128)S(1)} %get-tuple-element.25._.before), custom_call_target="tpu_custom_call" | custom-call | flops 4000000 | bytes 1100000 | tf_op jit(solution)/shard_map/inner/pallas_call | solution.py:358
  10.5 1.4 %collective-permute-done.2.got = s32[64,128]{1,0:T(8,128)S(1)} collective-permute-done((s32[64,128]{1,0:T(8,128)S(1)}, s32[64,128]{1,0:T(8,128)S(1)}, u32[]{:S(2)}, u32[]{:S(2)}) %collective-permute-start.2) | collective-permute-done | bytes 32800 | tf_op jit(solution)/shard_map/ppermute | solution.py:328
  11.9 4.5 %collective-permute-start.3 = (s32[32,128]{1,0:T(8,128)S(1)}, s32[32,128]{1,0:T(8,128)S(1)}, u32[]{:S(2)}, u32[]{:S(2)}) collective-permute-start(s32[32,128]{1,0:T(8,128)S(1)} %get-tuple-element.27), channel_id=1, source_target_pairs={{0,4},{1,5},{2,6},{3,7},{4,0},{5,1},{6,2},{7,3},{8,12},{9,13},{10,... | collective-permute-start | bytes 49160 | tf_op jit(solution)/shard_map/ppermute | solution.py:328
  16.4 0.0 collective-permute-done.4.theirs
  16.4 1.1 %collective-permute-done.3.got = s32[32,128]{1,0:T(8,128)S(1)} collective-permute-done((s32[32,128]{1,0:T(8,128)S(1)}, s32[32,128]{1,0:T(8,128)S(1)}, u32[]{:S(2)}, u32[]{:S(2)}) %collective-permute-start.3) | collective-permute-done | bytes 16416 | tf_op jit(solution)/shard_map/ppermute | solution.py:328
  17.5 0.1 shard_map.32
  17.7 0.8 %collective-permute-start.5 = (s32[72,128]{1,0:T(8,128)S(1)}, s32[72,128]{1,0:T(8,128)S(1)}, u32[]{:S(2)}, u32[]{:S(2)}) collective-permute-start(s32[72,128]{1,0:T(8,128)S(1)} %get-tuple-element.30), channel_id=1, source_target_pairs={{0,4},{1,5},{2,6},{3,7},{4,0},{5,1},{6,2},{7,3},{8,12},{9,13},{10,... | collective-permute-start | bytes 110600 | tf_op jit(solution)/shard_map/ppermute | solution.py:328
  18.4 2.4 %collective-permute-start.6 = (s32[72,128]{1,0:T(8,128)S(1)}, s32[72,128]{1,0:T(8,128)S(1)}, u32[]{:S(2)}, u32[]{:S(2)}) collective-permute-start(s32[72,128]{1,0:T(8,128)S(1)} %get-tuple-element.31), channel_id=1, source_target_pairs={{0,16},{1,17},{2,18},{3,19},{4,20},{5,21},{6,22},{7,23},{8,4},{9,5... | collective-permute-start | bytes 110600 | tf_op jit(solution)/shard_map/ppermute | solution.py:328
  20.9 0.0 collective-permute-start.7
  20.9 0.0 collective-permute-done.5.got1
  20.9 1.1 %collective-permute-done.6.got2 = s32[72,128]{1,0:T(8,128)S(1)} collective-permute-done((s32[72,128]{1,0:T(8,128)S(1)}, s32[72,128]{1,0:T(8,128)S(1)}, u32[]{:S(2)}, u32[]{:S(2)}) %collective-permute-start.6) | collective-permute-done | bytes 36896 | tf_op jit(solution)/shard_map/ppermute | solution.py:328
  21.9 0.2 collective-permute-done.7.got3
  22.1 0.1 shard_map.33
  22.2 1.4 %collective-permute-start.8 = (s32[40,128]{1,0:T(8,128)S(1)}, s32[40,128]{1,0:T(8,128)S(1)}, u32[]{:S(2)}, u32[]{:S(2)}) collective-permute-start(s32[40,128]{1,0:T(8,128)S(1)} %get-tuple-element.34), channel_id=1, source_target_pairs={{0,4},{1,5},{2,6},{3,7},{4,0},{5,1},{6,2},{7,3},{8,12},{9,13},{10,... | collective-permute-start | bytes 61448 | tf_op jit(solution)/shard_map/ppermute | solution.py:328
  23.6 2.6 %collective-permute-start.9 = (s32[40,128]{1,0:T(8,128)S(1)}, s32[40,128]{1,0:T(8,128)S(1)}, u32[]{:S(2)}, u32[]{:S(2)}) collective-permute-start(s32[40,128]{1,0:T(8,128)S(1)} %get-tuple-element.35), channel_id=1, source_target_pairs={{0,16},{1,17},{2,1},{3,0},{4,20},{5,21},{6,5},{7,4},{8,24},{9,25},... | collective-permute-start | bytes 61448 | tf_op jit(solution)/shard_map/ppermute | solution.py:328
  26.2 0.7 %collective-permute-start.10 = (s32[40,128]{1,0:T(8,128)S(1)}, s32[40,128]{1,0:T(8,128)S(1)}, u32[]{:S(2)}, u32[]{:S(2)}) collective-permute-start(s32[40,128]{1,0:T(8,128)S(1)} %get-tuple-element.36), channel_id=1, source_target_pairs={{0,16},{1,0},{2,1},{3,2},{4,20},{5,4},{6,5},{7,6},{8,24},{9,8},{10... | collective-permute-start | bytes 61448 | tf_op jit(solution)/shard_map/ppermute | solution.py:328
  26.9 0.0 collective-permute-done.8.got1
  26.9 0.2 collective-permute-done.9.got2
  27.1 0.7 %collective-permute-done.10.got3 = s32[40,128]{1,0:T(8,128)S(1)} collective-permute-done((s32[40,128]{1,0:T(8,128)S(1)}, s32[40,128]{1,0:T(8,128)S(1)}, u32[]{:S(2)}, u32[]{:S(2)}) %collective-permute-start.10) | collective-permute-done | bytes 20512 | tf_op jit(solution)/shard_map/ppermute | solution.py:328
  27.8 0.1 shard_map.34
  27.9 1.6 %collective-permute-start.11 = (s32[176,128]{1,0:T(8,128)S(1)}, s32[176,128]{1,0:T(8,128)S(1)}, u32[]{:S(2)}, u32[]{:S(2)}) collective-permute-start(s32[176,128]{1,0:T(8,128)S(1)} %get-tuple-element.39), channel_id=1, source_target_pairs={{0,16},{16,0},{32,48},{48,32},{64,80},{80,64},{96,112},{112,96},{1... | collective-permute-start | bytes 270344 | tf_op jit(solution)/shard_map/ppermute | solution.py:338
  29.5 1.2 %north.1._ = f32[32,32,128]{2,1,0:T(8,128)} custom-call(f32[8,128]{1,0:T(8,128)S(1)} %get-tuple-element.23._.step, s32[176,128]{1,0:T(8,128)S(1)} %get-tuple-element.40.pack, s32[32,32,128]{2,1,0:T(8,128)S(1)} %inner.1._, s32[32,32,128]{2,1,0:T(8,128)S(1)} %get-tuple-element.26.full, s32[96,128]{1,0:T(8,128)S(1)} %get-tuple-element.38.planes), custom_call_target="tpu_custom_call" | custom-call | flops 4000000 | bytes 1100000 | tf_op jit(solution)/shard_map/north/pallas_call | solution.py:388
  30.7 0.0 collective-permute-done.11.pack
  30.7 0.1 south.1
  (3 shorter events, 0.0 us)
Async XLA Ops:
  0.0 1.0 %copy-start = (s32[32,32,128]{2,1,0:T(8,128)S(1)}, s32[32,32,128]{2,1,0:T(8,128)}, u32[]{:S(2)}) copy-start(s32[32,32,128]{2,1,0:T(8,128)} %q.3) | copy-start | bytes 1572868
  1.0 5.0 %copy-start.1 = (s32[32,32,128]{2,1,0:T(8,128)S(1)}, s32[32,32,128]{2,1,0:T(8,128)}, u32[]{:S(2)}) copy-start(s32[32,32,128]{2,1,0:T(8,128)} %q.3) | copy-start | bytes 1572868
  1.2 4.1 %collective-permute-start = (s32[64,128]{1,0:T(8,128)S(1)}, s32[64,128]{1,0:T(8,128)S(1)}, u32[]{:S(2)}, u32[]{:S(2)}) collective-permute-start(s32[64,128]{1,0:T(8,128)S(1)} %shard_map.28.mine), channel_id=1, source_target_pairs={{0,16},{16,0},{32,48},{48,32},{64,80},{80,64},{96,112},{112,96},{1... | collective-permute-start | bytes 98312 | tf_op jit(solution)/shard_map/ppermute | solution.py:338
  5.4 2.8 %collective-permute-start.1 = (s32[64,128]{1,0:T(8,128)S(1)}, s32[64,128]{1,0:T(8,128)S(1)}, u32[]{:S(2)}, u32[]{:S(2)}) collective-permute-start(s32[64,128]{1,0:T(8,128)S(1)} %shard_map.29.sent), channel_id=1, source_target_pairs={{0,4},{1,5},{2,6},{3,7},{4,0},{5,1},{6,2},{7,3},{8,12},{9,13},{10,... | collective-permute-start | bytes 98312 | tf_op jit(solution)/shard_map/ppermute | solution.py:328
  6.7 9.7 %collective-permute-start.4 = (s32[128,128]{1,0:T(8,128)S(1)}, s32[128,128]{1,0:T(8,128)S(1)}, u32[]{:S(2)}, u32[]{:S(2)}) collective-permute-start(s32[128,128]{1,0:T(8,128)S(1)} %get-tuple-element.29.mine), channel_id=1, source_target_pairs={{0,16},{16,0},{32,48},{48,32},{64,80},{80,64},{96,112},{112,96},{1... | collective-permute-start | bytes 196616 | tf_op jit(solution)/shard_map/ppermute | solution.py:338
  8.2 3.8 %collective-permute-start.2 = (s32[64,128]{1,0:T(8,128)S(1)}, s32[64,128]{1,0:T(8,128)S(1)}, u32[]{:S(2)}, u32[]{:S(2)}) collective-permute-start(s32[64,128]{1,0:T(8,128)S(1)} %get-tuple-element.24.sent), channel_id=1, source_target_pairs={{0,4},{1,5},{2,6},{3,7},{4,0},{5,1},{6,2},{7,3},{8,12},{9,13},{10,... | collective-permute-start | bytes 98312 | tf_op jit(solution)/shard_map/ppermute | solution.py:328
  11.9 5.6 %collective-permute-start.3 = (s32[32,128]{1,0:T(8,128)S(1)}, s32[32,128]{1,0:T(8,128)S(1)}, u32[]{:S(2)}, u32[]{:S(2)}) collective-permute-start(s32[32,128]{1,0:T(8,128)S(1)} %get-tuple-element.27), channel_id=1, source_target_pairs={{0,4},{1,5},{2,6},{3,7},{4,0},{5,1},{6,2},{7,3},{8,12},{9,13},{10,... | collective-permute-start | bytes 49160 | tf_op jit(solution)/shard_map/ppermute | solution.py:328
  17.7 3.2 %collective-permute-start.5 = (s32[72,128]{1,0:T(8,128)S(1)}, s32[72,128]{1,0:T(8,128)S(1)}, u32[]{:S(2)}, u32[]{:S(2)}) collective-permute-start(s32[72,128]{1,0:T(8,128)S(1)} %get-tuple-element.30), channel_id=1, source_target_pairs={{0,4},{1,5},{2,6},{3,7},{4,0},{5,1},{6,2},{7,3},{8,12},{9,13},{10,... | collective-permute-start | bytes 110600 | tf_op jit(solution)/shard_map/ppermute | solution.py:328
  18.4 3.5 %collective-permute-start.6 = (s32[72,128]{1,0:T(8,128)S(1)}, s32[72,128]{1,0:T(8,128)S(1)}, u32[]{:S(2)}, u32[]{:S(2)}) collective-permute-start(s32[72,128]{1,0:T(8,128)S(1)} %get-tuple-element.31), channel_id=1, source_target_pairs={{0,16},{1,17},{2,18},{3,19},{4,20},{5,21},{6,22},{7,23},{8,4},{9,5... | collective-permute-start | bytes 110600 | tf_op jit(solution)/shard_map/ppermute | solution.py:328
  20.9 1.2 %collective-permute-start.7 = (s32[72,128]{1,0:T(8,128)S(1)}, s32[72,128]{1,0:T(8,128)S(1)}, u32[]{:S(2)}, u32[]{:S(2)}) collective-permute-start(s32[72,128]{1,0:T(8,128)S(1)} %get-tuple-element.32), channel_id=1, source_target_pairs={{0,16},{1,17},{2,18},{3,19},{4,0},{5,1},{6,2},{7,3},{8,4},{9,5},{1... | collective-permute-start | bytes 110600 | tf_op jit(solution)/shard_map/ppermute | solution.py:328
  22.2 4.7 %collective-permute-start.8 = (s32[40,128]{1,0:T(8,128)S(1)}, s32[40,128]{1,0:T(8,128)S(1)}, u32[]{:S(2)}, u32[]{:S(2)}) collective-permute-start(s32[40,128]{1,0:T(8,128)S(1)} %get-tuple-element.34), channel_id=1, source_target_pairs={{0,4},{1,5},{2,6},{3,7},{4,0},{5,1},{6,2},{7,3},{8,12},{9,13},{10,... | collective-permute-start | bytes 61448 | tf_op jit(solution)/shard_map/ppermute | solution.py:328
  23.6 3.5 %collective-permute-start.9 = (s32[40,128]{1,0:T(8,128)S(1)}, s32[40,128]{1,0:T(8,128)S(1)}, u32[]{:S(2)}, u32[]{:S(2)}) collective-permute-start(s32[40,128]{1,0:T(8,128)S(1)} %get-tuple-element.35), channel_id=1, source_target_pairs={{0,16},{1,17},{2,1},{3,0},{4,20},{5,21},{6,5},{7,4},{8,24},{9,25},... | collective-permute-start | bytes 61448 | tf_op jit(solution)/shard_map/ppermute | solution.py:328
  26.2 1.6 %collective-permute-start.10 = (s32[40,128]{1,0:T(8,128)S(1)}, s32[40,128]{1,0:T(8,128)S(1)}, u32[]{:S(2)}, u32[]{:S(2)}) collective-permute-start(s32[40,128]{1,0:T(8,128)S(1)} %get-tuple-element.36), channel_id=1, source_target_pairs={{0,16},{1,0},{2,1},{3,2},{4,20},{5,4},{6,5},{7,6},{8,24},{9,8},{10... | collective-permute-start | bytes 61448 | tf_op jit(solution)/shard_map/ppermute | solution.py:328
  27.9 2.8 %collective-permute-start.11 = (s32[176,128]{1,0:T(8,128)S(1)}, s32[176,128]{1,0:T(8,128)S(1)}, u32[]{:S(2)}, u32[]{:S(2)}) collective-permute-start(s32[176,128]{1,0:T(8,128)S(1)} %get-tuple-element.39), channel_id=1, source_target_pairs={{0,16},{16,0},{32,48},{48,32},{64,80},{80,64},{96,112},{112,96},{1... | collective-permute-start | bytes 270344 | tf_op jit(solution)/shard_map/ppermute | solution.py:338

commit v9 on v8

--- a/solution.py
+++ b/solution.py
@@ -164,7 +164,7 @@
 def split_kernel(got1, got2, got3, rows, planes, south, north):
     z = lax.axis_index("gz")
     az = lower(z, got1, got2, got3)
-    hz = beyond(z, got1, got3)[0:32, :]
+    hz = pltpu.roll(beyond(z, got1, got3), 64, 1)
     lane = lax.broadcasted_iota(I32, (40, 128), 1)
     row = lax.broadcasted_iota(I32, (8, 128), 0)
 
@@ -174,16 +174,15 @@
     south[0:32, :] = rows[0:32, :]
     south[32:40, :] = tail(64, 32)
     edges = jnp.where(lane == 32, at_lane(az, 64), jnp.where(lane == 33, at_lane(az, 32), az))
-    south[40:80, :] = edges
-    south[80:112, :] = hz
-    south[112:144, :] = rows[72:104, :]
-    south[144:176, :] = planes[0:32, :]
+    south[40:80, :] = jnp.where(lane < 64, edges, hz)
+    south[80:112, :] = rows[72:104, :]
+    south[112:144, :] = planes[0:32, :]
     north[0:32, :] = rows[32:64, :]
     north[32:40, :] = tail(31, 65)
-    north[40:80, :] = jnp.where(lane == 32, at_lane(az, 31), pltpu.roll(az, 96, 1))
-    north[80:112, :] = pltpu.roll(hz, 96, 1)
-    north[112:144, :] = rows[104:136, :]
-    north[144:176, :] = planes[32:64, :]
+    edges = jnp.where(lane == 32, at_lane(az, 31), pltpu.roll(az, 96, 1))
+    north[40:80, :] = jnp.where(lane < 64, edges, pltpu.roll(hz, 96, 1))
+    north[80:112, :] = rows[104:136, :]
+    north[112:144, :] = planes[32:64, :]
 
 
 def inner_kernel(full, _, inner, field, *, ny, nz):
@@ -214,8 +213,9 @@
     nx = full.shape[0]
     lane = lax.broadcasted_iota(I32, (32, 128), 1)
     row = lax.broadcasted_iota(I32, (32, 128), 0)
-    ay, az, hz, hy = pack[0:32, :], pack[40:72, :], pack[80:112, :], pack[112:144, :]
-    hyz, low = pack[73:74, :], pack[144:176, :]
+    ay, az, hy = pack[0:32, :], pack[40:72, :], pack[80:112, :]
+    hz = pltpu.roll(az, 64, 1)
+    hyz, low = pack[73:74, :], pack[112:144, :]
 
     def beside(v, before, after, axis, last):
         at = lane if axis else row
@@ -372,7 +372,7 @@
     got = exchange(sent, along_y)
     rows, *sent = call(columns_kernel, (144, 40, 40, 40), *got, z_base)
     got = exchange(sent, along_z)
-    south, north = call(split_kernel, (176, 176), *got, rows, planes)
+    south, north = call(split_kernel, (144, 144), *got, rows, planes)
     pack = swap(south)
     sizes = dict(n=n, ny=ny, nz=nz)
     options = dict(

time: 30.9 us -> 30.9 us (level)
  no operation moved by 1% of the time
where the time goes in v9:
time: 30.9 us; the launch traced here: 30.8 us
  starting transfers between devices  19.6 us (63%)
  waiting for transfers between devices  6.53 us (21%)
  Pallas kernels  2.95 us (10%)
  local copies, waits for them, and re-layouts  1.04 us (3%)
  between operations  0.73 us (2%)
    ppermute x9, starting transfers between devices, send(): return lax.ppermute(block, ('gx', 'gy', 'gz'), route)  14.3 us
    ppermute x9, waiting for transfers between devices, send(): return lax.ppermute(block, ('gx', 'gy', 'gz'), route)  5.66 us
    ppermute x3, starting transfers between devices, swap(): return lax.ppermute(block, 'gx', [(i, i ^ 1) for i in range(n)])  5.25 us
    pallas_call x1, Pallas kernels, on_device(): pl.pallas_call(functools.partial(north_kernel, **sizes), in_specs=[vmem]...  1.2 us
    unnamed x4, local copies, waits for them, and re-layouts  1.04 us
    ppermute x3, waiting for transfers between devices, swap(): return lax.ppermute(block, 'gx', [(i, i ^ 1) for i in range(n)])  0.87 us
    pallas_call x1, Pallas kernels, on_device(): pl.pallas_call(block_kernel, in_specs=[smem, vmem], out_shape=(shape(quan...  0.68 us
  transfers between devices with their start and end apart: 12, of which 8 were waited for; matrix products, arithmetic and copies ran while one was open for 0% of the time, Pallas kernels for 7%

profile of v9, /device:TPU:1, one launch (start us, length us, event | category | flops | bytes accessed | tf_op | source)
XLA Modules:
  0.0 30.8 jit_solution(1990162205750429794)
XLA Ops:
  0.0 0.0 copy-start
  0.0 1.0 %copy-done = s32[32,32,128]{2,1,0:T(8,128)S(1)} copy-done((s32[32,32,128]{2,1,0:T(8,128)S(1)}, s32[32,32,128]{2,1,0:T(8,128)}, u32[]{:S(2)}) %copy-start) | copy-done | bytes 524312
  1.0 0.0 copy-start.1
  1.0 0.2 shard_map.28.mine
  1.2 3.3 %collective-permute-start = (s32[64,128]{1,0:T(8,128)S(1)}, s32[64,128]{1,0:T(8,128)S(1)}, u32[]{:S(2)}, u32[]{:S(2)}) collective-permute-start(s32[64,128]{1,0:T(8,128)S(1)} %shard_map.28.mine), channel_id=1, source_target_pairs={{0,16},{16,0},{32,48},{48,32},{64,80},{80,64},{96,112},{112,96},{1... | collective-permute-start | bytes 98312 | tf_op jit(solution)/shard_map/ppermute | solution.py:338
  4.5 0.9 %collective-permute-done.other = s32[64,128]{1,0:T(8,128)S(1)} collective-permute-done((s32[64,128]{1,0:T(8,128)S(1)}, s32[64,128]{1,0:T(8,128)S(1)}, u32[]{:S(2)}, u32[]{:S(2)}) %collective-permute-start) | collective-permute-done | bytes 32800 | tf_op jit(solution)/shard_map/ppermute | solution.py:338
  5.4 0.0 collective-permute-start.1
  6.0 0.0 copy-done.1
  6.0 0.7 %block.1 = (s32[32,32,128]{2,1,0:T(8,128)S(1)}, s32[128,128]{1,0:T(8,128)S(1)}, f32[8,128]{1,0:T(8,128)S(1)}) custom-call(f32[1]{0:T(128)S(6)} %copy.5.step, s32[32,32,128]{2,1,0:T(8,128)S(1)} %copy-done.1), custom_call_target="tpu_custom_call" | custom-call | flops 4000000 | bytes 1100000 | tf_op jit(solution)/shard_map/block/pallas_call | solution.py:342
  6.7 0.4 %collective-permute-start.4 = (s32[128,128]{1,0:T(8,128)S(1)}, s32[128,128]{1,0:T(8,128)S(1)}, u32[]{:S(2)}, u32[]{:S(2)}) collective-permute-start(s32[128,128]{1,0:T(8,128)S(1)} %get-tuple-element.29.mine), channel_id=1, source_target_pairs={{0,16},{16,0},{32,48},{48,32},{64,80},{80,64},{96,112},{112,96},{1... | collective-permute-start | bytes 196616 | tf_op jit(solution)/shard_map/ppermute | solution.py:338
  7.2 1.0 %collective-permute-done.1.got = s32[64,128]{1,0:T(8,128)S(1)} collective-permute-done((s32[64,128]{1,0:T(8,128)S(1)}, s32[64,128]{1,0:T(8,128)S(1)}, u32[]{:S(2)}, u32[]{:S(2)}) %collective-permute-start.1) | collective-permute-done | bytes 32800 | tf_op jit(solution)/shard_map/ppermute | solution.py:328
  8.2 1.9 %collective-permute-start.2 = (s32[64,128]{1,0:T(8,128)S(1)}, s32[64,128]{1,0:T(8,128)S(1)}, u32[]{:S(2)}, u32[]{:S(2)}) collective-permute-start(s32[64,128]{1,0:T(8,128)S(1)} %get-tuple-element.24.sent), channel_id=1, source_target_pairs={{0,4},{1,5},{2,6},{3,7},{4,0},{5,1},{6,2},{7,3},{8,12},{9,13},{10,... | collective-permute-start | bytes 98312 | tf_op jit(solution)/shard_map/ppermute | solution.py:328
  10.1 0.4 %inner.1._ = s32[32,32,128]{2,1,0:T(8,128)S(1)} custom-call(s32[32,32,128]{2,1,0:T(8,128)S(1)} %get-tuple-element.26.full, s32[64,128]{1,0:T(8,128)S(1)} %get-tuple-element.25._.before), custom_call_target="tpu_custom_call" | custom-call | flops 4000000 | bytes 1100000 | tf_op jit(solution)/shard_map/inner/pallas_call | solution.py:358
  10.5 1.4 %collective-permute-done.2.got = s32[64,128]{1,0:T(8,128)S(1)} collective-permute-done((s32[64,128]{1,0:T(8,128)S(1)}, s32[64,128]{1,0:T(8,128)S(1)}, u32[]{:S(2)}, u32[]{:S(2)}) %collective-permute-start.2) | collective-permute-done | bytes 32800 | tf_op jit(solution)/shard_map/ppermute | solution.py:328
  11.9 4.5 %collective-permute-start.3 = (s32[32,128]{1,0:T(8,128)S(1)}, s32[32,128]{1,0:T(8,128)S(1)}, u32[]{:S(2)}, u32[]{:S(2)}) collective-permute-start(s32[32,128]{1,0:T(8,128)S(1)} %get-tuple-element.27), channel_id=1, source_target_pairs={{0,4},{1,5},{2,6},{3,7},{4,0},{5,1},{6,2},{7,3},{8,12},{9,13},{10,... | collective-permute-start | bytes 49160 | tf_op jit(solution)/shard_map/ppermute | solution.py:328
  16.4 0.0 collective-permute-done.4.theirs
  16.4 1.1 %collective-permute-done.3.got = s32[32,128]{1,0:T(8,128)S(1)} collective-permute-done((s32[32,128]{1,0:T(8,128)S(1)}, s32[32,128]{1,0:T(8,128)S(1)}, u32[]{:S(2)}, u32[]{:S(2)}) %collective-permute-start.3) | collective-permute-done | bytes 16416 | tf_op jit(solution)/shard_map/ppermute | solution.py:328
  17.5 0.1 shard_map.32
  17.7 0.8 %collective-permute-start.5 = (s32[72,128]{1,0:T(8,128)S(1)}, s32[72,128]{1,0:T(8,128)S(1)}, u32[]{:S(2)}, u32[]{:S(2)}) collective-permute-start(s32[72,128]{1,0:T(8,128)S(1)} %get-tuple-element.30), channel_id=1, source_target_pairs={{0,4},{1,5},{2,6},{3,7},{4,0},{5,1},{6,2},{7,3},{8,12},{9,13},{10,... | collective-permute-start | bytes 110600 | tf_op jit(solution)/shard_map/ppermute | solution.py:328
  18.4 2.4 %collective-permute-start.6 = (s32[72,128]{1,0:T(8,128)S(1)}, s32[72,128]{1,0:T(8,128)S(1)}, u32[]{:S(2)}, u32[]{:S(2)}) collective-permute-start(s32[72,128]{1,0:T(8,128)S(1)} %get-tuple-element.31), channel_id=1, source_target_pairs={{0,16},{1,17},{2,18},{3,19},{4,20},{5,21},{6,22},{7,23},{8,4},{9,5... | collective-permute-start | bytes 110600 | tf_op jit(solution)/shard_map/ppermute | solution.py:328
  20.9 0.0 collective-permute-start.7
  20.9 0.0 collective-permute-done.5.got1
  20.9 1.1 %collective-permute-done.6.got2 = s32[72,128]{1,0:T(8,128)S(1)} collective-permute-done((s32[72,128]{1,0:T(8,128)S(1)}, s32[72,128]{1,0:T(8,128)S(1)}, u32[]{:S(2)}, u32[]{:S(2)}) %collective-permute-start.6) | collective-permute-done | bytes 36896 | tf_op jit(solution)/shard_map/ppermute | solution.py:328
  21.9 0.2 collective-permute-done.7.got3
  22.1 0.1 shard_map.33
  22.2 1.4 %collective-permute-start.8 = (s32[40,128]{1,0:T(8,128)S(1)}, s32[40,128]{1,0:T(8,128)S(1)}, u32[]{:S(2)}, u32[]{:S(2)}) collective-permute-start(s32[40,128]{1,0:T(8,128)S(1)} %get-tuple-element.34), channel_id=1, source_target_pairs={{0,4},{1,5},{2,6},{3,7},{4,0},{5,1},{6,2},{7,3},{8,12},{9,13},{10,... | collective-permute-start | bytes 61448 | tf_op jit(solution)/shard_map/ppermute | solution.py:328
  23.6 2.6 %collective-permute-start.9 = (s32[40,128]{1,0:T(8,128)S(1)}, s32[40,128]{1,0:T(8,128)S(1)}, u32[]{:S(2)}, u32[]{:S(2)}) collective-permute-start(s32[40,128]{1,0:T(8,128)S(1)} %get-tuple-element.35), channel_id=1, source_target_pairs={{0,16},{1,17},{2,1},{3,0},{4,20},{5,21},{6,5},{7,4},{8,24},{9,25},... | collective-permute-start | bytes 61448 | tf_op jit(solution)/shard_map/ppermute | solution.py:328
  26.2 0.7 %collective-permute-start.10 = (s32[40,128]{1,0:T(8,128)S(1)}, s32[40,128]{1,0:T(8,128)S(1)}, u32[]{:S(2)}, u32[]{:S(2)}) collective-permute-start(s32[40,128]{1,0:T(8,128)S(1)} %get-tuple-element.36), channel_id=1, source_target_pairs={{0,16},{1,0},{2,1},{3,2},{4,20},{5,4},{6,5},{7,6},{8,24},{9,8},{10... | collective-permute-start | bytes 61448 | tf_op jit(solution)/shard_map/ppermute | solution.py:328
  26.9 0.0 collective-permute-done.8.got1
  26.9 0.2 collective-permute-done.9.got2
  27.1 0.7 %collective-permute-done.10.got3 = s32[40,128]{1,0:T(8,128)S(1)} collective-permute-done((s32[40,128]{1,0:T(8,128)S(1)}, s32[40,128]{1,0:T(8,128)S(1)}, u32[]{:S(2)}, u32[]{:S(2)}) %collective-permute-start.10) | collective-permute-done | bytes 20512 | tf_op jit(solution)/shard_map/ppermute | solution.py:328
  27.8 0.1 shard_map.34
  28.0 1.5 %collective-permute-start.11 = (s32[144,128]{1,0:T(8,128)S(1)}, s32[144,128]{1,0:T(8,128)S(1)}, u32[]{:S(2)}, u32[]{:S(2)}) collective-permute-start(s32[144,128]{1,0:T(8,128)S(1)} %get-tuple-element.39), channel_id=1, source_target_pairs={{0,16},{16,0},{32,48},{48,32},{64,80},{80,64},{96,112},{112,96},{1... | collective-permute-start | bytes 221192 | tf_op jit(solution)/shard_map/ppermute | solution.py:338
  29.5 1.2 %north.1._ = f32[32,32,128]{2,1,0:T(8,128)} custom-call(f32[8,128]{1,0:T(8,128)S(1)} %get-tuple-element.23._.step, s32[144,128]{1,0:T(8,128)S(1)} %get-tuple-element.40.pack, s32[32,32,128]{2,1,0:T(8,128)S(1)} %inner.1._, s32[32,32,128]{2,1,0:T(8,128)S(1)} %get-tuple-element.26.full, s32[96,128]{1,0:T(8,128)S(1)} %get-tuple-element.38.planes), custom_call_target="tpu_custom_call" | custom-call | flops 4000000 | bytes 1100000 | tf_op jit(solution)/shard_map/north/pallas_call | solution.py:388
  30.7 0.0 collective-permute-done.11.pack
  30.7 0.1 south.1
  (3 shorter events, 0.0 us)
Async XLA Ops:
  0.0 1.0 %copy-start = (s32[32,32,128]{2,1,0:T(8,128)S(1)}, s32[32,32,128]{2,1,0:T(8,128)}, u32[]{:S(2)}) copy-start(s32[32,32,128]{2,1,0:T(8,128)} %q.3) | copy-start | bytes 1572868
  1.0 5.0 %copy-start.1 = (s32[32,32,128]{2,1,0:T(8,128)S(1)}, s32[32,32,128]{2,1,0:T(8,128)}, u32[]{:S(2)}) copy-start(s32[32,32,128]{2,1,0:T(8,128)} %q.3) | copy-start | bytes 1572868
  1.2 4.1 %collective-permute-start = (s32[64,128]{1,0:T(8,128)S(1)}, s32[64,128]{1,0:T(8,128)S(1)}, u32[]{:S(2)}, u32[]{:S(2)}) collective-permute-start(s32[64,128]{1,0:T(8,128)S(1)} %shard_map.28.mine), channel_id=1, source_target_pairs={{0,16},{16,0},{32,48},{48,32},{64,80},{80,64},{96,112},{112,96},{1... | collective-permute-start | bytes 98312 | tf_op jit(solution)/shard_map/ppermute | solution.py:338
  5.4 2.8 %collective-permute-start.1 = (s32[64,128]{1,0:T(8,128)S(1)}, s32[64,128]{1,0:T(8,128)S(1)}, u32[]{:S(2)}, u32[]{:S(2)}) collective-permute-start(s32[64,128]{1,0:T(8,128)S(1)} %shard_map.29.sent), channel_id=1, source_target_pairs={{0,4},{1,5},{2,6},{3,7},{4,0},{5,1},{6,2},{7,3},{8,12},{9,13},{10,... | collective-permute-start | bytes 98312 | tf_op jit(solution)/shard_map/ppermute | solution.py:328
  6.7 9.7 %collective-permute-start.4 = (s32[128,128]{1,0:T(8,128)S(1)}, s32[128,128]{1,0:T(8,128)S(1)}, u32[]{:S(2)}, u32[]{:S(2)}) collective-permute-start(s32[128,128]{1,0:T(8,128)S(1)} %get-tuple-element.29.mine), channel_id=1, source_target_pairs={{0,16},{16,0},{32,48},{48,32},{64,80},{80,64},{96,112},{112,96},{1... | collective-permute-start | bytes 196616 | tf_op jit(solution)/shard_map/ppermute | solution.py:338
  8.2 3.8 %collective-permute-start.2 = (s32[64,128]{1,0:T(8,128)S(1)}, s32[64,128]{1,0:T(8,128)S(1)}, u32[]{:S(2)}, u32[]{:S(2)}) collective-permute-start(s32[64,128]{1,0:T(8,128)S(1)} %get-tuple-element.24.sent), channel_id=1, source_target_pairs={{0,4},{1,5},{2,6},{3,7},{4,0},{5,1},{6,2},{7,3},{8,12},{9,13},{10,... | collective-permute-start | bytes 98312 | tf_op jit(solution)/shard_map/ppermute | solution.py:328
  11.9 5.6 %collective-permute-start.3 = (s32[32,128]{1,0:T(8,128)S(1)}, s32[32,128]{1,0:T(8,128)S(1)}, u32[]{:S(2)}, u32[]{:S(2)}) collective-permute-start(s32[32,128]{1,0:T(8,128)S(1)} %get-tuple-element.27), channel_id=1, source_target_pairs={{0,4},{1,5},{2,6},{3,7},{4,0},{5,1},{6,2},{7,3},{8,12},{9,13},{10,... | collective-permute-start | bytes 49160 | tf_op jit(solution)/shard_map/ppermute | solution.py:328
  17.7 3.2 %collective-permute-start.5 = (s32[72,128]{1,0:T(8,128)S(1)}, s32[72,128]{1,0:T(8,128)S(1)}, u32[]{:S(2)}, u32[]{:S(2)}) collective-permute-start(s32[72,128]{1,0:T(8,128)S(1)} %get-tuple-element.30), channel_id=1, source_target_pairs={{0,4},{1,5},{2,6},{3,7},{4,0},{5,1},{6,2},{7,3},{8,12},{9,13},{10,... | collective-permute-start | bytes 110600 | tf_op jit(solution)/shard_map/ppermute | solution.py:328
  18.4 3.5 %collective-permute-start.6 = (s32[72,128]{1,0:T(8,128)S(1)}, s32[72,128]{1,0:T(8,128)S(1)}, u32[]{:S(2)}, u32[]{:S(2)}) collective-permute-start(s32[72,128]{1,0:T(8,128)S(1)} %get-tuple-element.31), channel_id=1, source_target_pairs={{0,16},{1,17},{2,18},{3,19},{4,20},{5,21},{6,22},{7,23},{8,4},{9,5... | collective-permute-start | bytes 110600 | tf_op jit(solution)/shard_map/ppermute | solution.py:328
  20.9 1.2 %collective-permute-start.7 = (s32[72,128]{1,0:T(8,128)S(1)}, s32[72,128]{1,0:T(8,128)S(1)}, u32[]{:S(2)}, u32[]{:S(2)}) collective-permute-start(s32[72,128]{1,0:T(8,128)S(1)} %get-tuple-element.32), channel_id=1, source_target_pairs={{0,16},{1,17},{2,18},{3,19},{4,0},{5,1},{6,2},{7,3},{8,4},{9,5},{1... | collective-permute-start | bytes 110600 | tf_op jit(solution)/shard_map/ppermute | solution.py:328
  22.2 4.7 %collective-permute-start.8 = (s32[40,128]{1,0:T(8,128)S(1)}, s32[40,128]{1,0:T(8,128)S(1)}, u32[]{:S(2)}, u32[]{:S(2)}) collective-permute-start(s32[40,128]{1,0:T(8,128)S(1)} %get-tuple-element.34), channel_id=1, source_target_pairs={{0,4},{1,5},{2,6},{3,7},{4,0},{5,1},{6,2},{7,3},{8,12},{9,13},{10,... | collective-permute-start | bytes 61448 | tf_op jit(solution)/shard_map/ppermute | solution.py:328
  23.6 3.5 %collective-permute-start.9 = (s32[40,128]{1,0:T(8,128)S(1)}, s32[40,128]{1,0:T(8,128)S(1)}, u32[]{:S(2)}, u32[]{:S(2)}) collective-permute-start(s32[40,128]{1,0:T(8,128)S(1)} %get-tuple-element.35), channel_id=1, source_target_pairs={{0,16},{1,17},{2,1},{3,0},{4,20},{5,21},{6,5},{7,4},{8,24},{9,25},... | collective-permute-start | bytes 61448 | tf_op jit(solution)/shard_map/ppermute | solution.py:328
  26.2 1.6 %collective-permute-start.10 = (s32[40,128]{1,0:T(8,128)S(1)}, s32[40,128]{1,0:T(8,128)S(1)}, u32[]{:S(2)}, u32[]{:S(2)}) collective-permute-start(s32[40,128]{1,0:T(8,128)S(1)} %get-tuple-element.36), channel_id=1, source_target_pairs={{0,16},{1,0},{2,1},{3,2},{4,20},{5,4},{6,5},{7,6},{8,24},{9,8},{10... | collective-permute-start | bytes 61448 | tf_op jit(solution)/shard_map/ppermute | solution.py:328
  28.0 2.7 %collective-permute-start.11 = (s32[144,128]{1,0:T(8,128)S(1)}, s32[144,128]{1,0:T(8,128)S(1)}, u32[]{:S(2)}, u32[]{:S(2)}) collective-permute-start(s32[144,128]{1,0:T(8,128)S(1)} %get-tuple-element.39), channel_id=1, source_target_pairs={{0,16},{16,0},{32,48},{48,32},{64,80},{80,64},{96,112},{112,96},{1... | collective-permute-start | bytes 221192 | tf_op jit(solution)/shard_map/ppermute | solution.py:338
